TPU v7x, 32 devices: a whole 2x2x4 slice. The times are simulated.
32 devices in a mesh: elem: 8 (over z, y), comp: 2 (over x), rep: 2 (over core).
Axes of the slice: x: 2, y: 2, z: 4, core: 2. Of those that a mesh axis runs over, the one named last changes fastest.
Arguments:
- velocity: float32 [3, 10, 10, 10, 2, 6144], P(None, 'comp', None, None, None, ('elem', 'rep')), may hold values from -6 to 6
- geometry: float32 [3, 3, 10, 10, 10, 2, 6144], P(None, None, 'comp', None, None, None, ('elem', 'rep')), may hold values from -40 to 40
- element_place: int32 [2, 6144], P('comp', ('elem', 'rep')), may hold values from 0 to 383, as said below
Outputs:
- pressure: float32 [10, 10, 10, 2, 6144], P(None, None, None, 'comp', ('elem', 'rep'))
Inputs may be any that keep to these rules, and one draw needn't show every extreme that they name: `element_place`: in each row and each aligned run of 384 entries of it, every value 0 to 383 appears once.
All inputs are finite; a program needn't handle non-finite values.
Results may differ from a plain program's by a relative error of at most 0.000071.
Values sent between devices are 32-bit elements; how exact they have to be, the bound alone decides.
No kernel may reach another device: no remote copies, remote signals or barrier semaphores. Data moves between devices by JAX's collectives and lax.ppermute only.
A program may use at most 192 MiB of HBM per device.

v0:
```python
import jax
import jax.numpy as jnp
import numpy as np
from jax import lax
from jax.sharding import PartitionSpec as P

BLOCK_X = 6
BLOCK_Y = 8
BLOCK_Z = 8
GRID_Y = 4


exact_mode = lax.Precision.HIGHEST


def passed_along(x, axis, by):
    count = lax.axis_size(axis)
    pairs = [(i, i + by) for i in range(count) if 0 <= i + by < count]
    return lax.ppermute(x, axis, pairs)


def legendre_columns(points, degree):
    columns = [points * 0.0 + 1.0, points]
    for order in range(2, degree + 1):
        columns.append(
            ((2 * order - 1) * points * columns[order - 1] - (order - 1) * columns[order - 2])
            / order
        )
    return columns


def derivative_table(node_count):
    degree = node_count - 1
    points = np.cos(np.pi * np.arange(node_count) / degree)
    for sweep in range(100):
        columns = legendre_columns(points, degree)
        points = points - (points * columns[degree] - columns[degree - 1]) / (
            node_count * columns[degree]
        )
    points = np.sort(points)
    values = legendre_columns(points, degree)[degree]
    identity = np.eye(node_count)
    spacing = points[:, None] - points[None, :] + identity
    matrix = values[:, None] / (values[None, :] * spacing)
    matrix = np.where(identity > 0.5, 0.0, matrix)
    matrix[0, 0] = -degree * (degree + 1) / 4.0
    matrix[degree, degree] = degree * (degree + 1) / 4.0
    return matrix


def apply_transpose(deriv_table, flux_r, flux_s, flux_t):
    along_r = jnp.einsum("ia,i...->a...", deriv_table, flux_r, precision=exact_mode)
    along_s = jnp.einsum("ib,ai...->ab...", deriv_table, flux_s, precision=exact_mode)
    along_t = jnp.einsum("ic,abi...->abc...", deriv_table, flux_t, precision=exact_mode)
    return along_r + along_s + along_t


def local_pass(field, direction, block_grid):
    last_node = field.shape[0] - 1
    element_axis = 3 + direction
    extent = block_grid[direction]
    lower = lax.slice_in_dim(field, 0, 1, axis=direction)
    upper = lax.slice_in_dim(field, last_node, last_node + 1, axis=direction)
    zero_lower = jnp.zeros_like(lax.slice_in_dim(lower, 0, 1, axis=element_axis))
    add_upper = jnp.concatenate(
        [lax.slice_in_dim(lower, 1, extent, axis=element_axis), zero_lower], axis=element_axis
    )
    add_lower = jnp.concatenate(
        [zero_lower, lax.slice_in_dim(upper, 0, extent - 1, axis=element_axis)], axis=element_axis
    )
    node_iota = lax.broadcasted_iota(jnp.int32, field.shape, direction)
    field = field + jnp.where(node_iota == 0, add_lower, 0.0)
    return field + jnp.where(node_iota == last_node, add_upper, 0.0)


def node_keep(sign_code, last_node):
    if sign_code > 0:
        return slice(last_node, last_node + 1)
    if sign_code < 0:
        return slice(0, 1)
    return slice(None)


def element_keep(sign_code, extent):
    if sign_code > 0:
        return slice(extent - 1, extent)
    if sign_code < 0:
        return slice(0, 1)
    return slice(None)


def take_region(field, offset, block_grid):
    last_node = field.shape[0] - 1
    nodes_key = tuple((node_keep(component, last_node) for component in offset))
    elems_key = tuple(
        (element_keep(offset[dim_index], block_grid[dim_index]) for dim_index in range(3))
    )
    return field[nodes_key + elems_key]


def region_mask(shape, offset, block_grid):
    last_node = shape[0] - 1
    verdict = jnp.ones(shape, dtype=jnp.bool_)
    for dim_index in range(3):
        if offset[dim_index] != 0:
            node_target = last_node if offset[dim_index] > 0 else 0
            elem_target = block_grid[dim_index] - 1 if offset[dim_index] > 0 else 0
            verdict = jnp.logical_and(
                verdict, lax.broadcasted_iota(jnp.int32, shape, dim_index) == node_target
            )
            verdict = jnp.logical_and(
                verdict, lax.broadcasted_iota(jnp.int32, shape, 3 + dim_index) == elem_target
            )
    return verdict


def add_region(field, offset, values, block_grid):
    return field + jnp.where(region_mask(field.shape, offset, block_grid), values, 0.0)


def neighbor_offsets():
    listing = []
    for step_x in (-1, 0, 1):
        for step_y in (-1, 0, 1):
            for step_z in (-1, 0, 1):
                if step_x != 0 or step_y != 0 or step_z != 0:
                    listing.append((step_x, step_y, step_z))
    return listing


def inside(position, offset, extents):
    verdict = jnp.asarray(True)
    for dim_index in range(3):
        target = position[dim_index] + offset[dim_index]
        verdict = jnp.logical_and(
            verdict, jnp.logical_and(target >= 0, target < extents[dim_index])
        )
    return verdict


def body(velocity, geometry, element_place):
    comp_count = lax.axis_size("comp")
    half_nodes = velocity.shape[1]
    node_count = half_nodes * comp_count
    deriv_table = jnp.asarray(derivative_table(node_count), jnp.float32)
    fluxes = []
    for direction in range(3):
        fluxes.append(
            geometry[0, direction] * velocity[0]
            + geometry[1, direction] * velocity[1]
            + geometry[2, direction] * velocity[2]
        )
    flux_r, flux_s, flux_t = (
        lax.all_to_all(fluxes[0], "comp", split_axis=3, concat_axis=0, tiled=True),
        lax.all_to_all(fluxes[1], "comp", split_axis=3, concat_axis=0, tiled=True),
        lax.all_to_all(fluxes[2], "comp", split_axis=3, concat_axis=0, tiled=True),
    )
    owned_nodes = apply_transpose(deriv_table, flux_r, flux_s, flux_t)
    owned_nodes = owned_nodes[:, :, :, 0, :]
    places = element_place[0]
    sub_count = places.shape[0]
    place_matrix = (places[:, None] == jnp.arange(sub_count, dtype=jnp.int32)[None, :]).astype(
        jnp.float32
    )
    canonical = jnp.einsum("abci,ij->abcj", owned_nodes, place_matrix, precision=exact_mode)
    block_grid = (BLOCK_X, BLOCK_Y, BLOCK_Z)
    canonical = canonical.reshape((node_count, node_count, node_count) + block_grid)
    layers = comp_count * lax.axis_size("rep")
    stride_x = GRID_Y * layers
    strides = (stride_x, layers, 1)
    extents = (lax.axis_size(("elem", "comp", "rep")) // stride_x, GRID_Y, layers)
    device = lax.axis_index(("elem", "comp", "rep"))
    position = (device // stride_x, device // layers % GRID_Y, device % layers)
    local_only = canonical
    for direction in range(3):
        local_only = local_pass(local_only, direction, block_grid)
    assembled = local_only
    for offset in neighbor_offsets():
        opposite = tuple((-component for component in offset))
        outgoing = take_region(local_only, opposite, block_grid)
        shift_by = -sum((component * stride for component, stride in zip(offset, strides)))
        incoming = passed_along(outgoing.reshape(-1), ("elem", "comp", "rep"), shift_by)
        within = inside(position, offset, extents)
        payload = jnp.where(within, incoming, 0.0).reshape(outgoing.shape)
        assembled = add_region(assembled, offset, payload, block_grid)
    assembled = assembled.reshape(node_count, node_count, node_count, sub_count)
    result = jnp.einsum("abcj,ij->abci", assembled, place_matrix, precision=exact_mode)
    return result[:, :, :, None, :]


def solution(mesh):
    placed = (
        P(None, "comp", None, None, None, ("elem", "rep")),
        P(None, None, "comp", None, None, None, ("elem", "rep")),
        P("comp", ("elem", "rep")),
    )
    return jax.shard_map(
        body,
        mesh=mesh,
        in_specs=placed,
        out_specs=P(None, None, None, "comp", ("elem", "rep")),
        check_vma=False,
    )
```

profile of v0, /device:TPU:7, one launch (start us, length us, event | category | flops | bytes accessed | tf_op | source)
XLA Modules:
  0.0 409.7 jit_solution(2351560866955214997)
XLA Ops:
  3.9 7.8 %fusion.121 = (f32[1,1,5,10,10,2,384]{6,5,4,3,2,1,0:T(2,128)S(1)}, f32[1,1,5,10,10,2,384]{6,5,4,3,2,1,0:T(2,128)S(1)}, f32[1,1,5,10,10,2,384]{6,5,4,3,2,1,0:T(2,...) fusion(f32[3,3,5,10,10,2,384]{6,5,4,3,2,1,0:T(2,128)} %param.5), kind=kLoop, calls=%fused_computation.193 | loop fusion | bytes 27648000 | tf_op jit(solution)/shard_map/slice | solution.py:149
  16.2 30.7 %all_to_all.45 = f32[5,10,10,2,384]{4,2,1,0,3:T(8,128)} all-to-all(f32[5,10,10,2,384]{4,2,1,0,3:T(8,128)S(1)} %get-tuple-element.45), channel_id=1, replica_groups=mesh['elem'=8,'comp'=2,'rep'=2] {'comp'}, dimensions={3} | all-to-all | bytes 3072000 | tf_op jit(solution)/shard_map/all_to_all | solution.py:155
  46.9 5.1 %all-to-all-start.2 = ((f32[5,10,10,2,384]{4,2,1,0,3:T(8,128)}), f32[5,10,10,2,384]{4,2,1,0,3:T(8,128)S(1)}, u32[]{:S(2)}, u32[]{:S(2)}) async-start(f32[5,10,10,2,384]{4,2,1,0,3:T(8,128)} %get-tuple-element.46), calls=%async_computation.2 | async-start | bytes 4915200 | tf_op jit(solution)/shard_map/all_to_all | solution.py:156
  56.3 21.8 %all-to-all-done.2 = f32[5,10,10,2,384]{4,2,1,0,3:T(8,128)S(1)} async-done(((f32[5,10,10,2,384]{4,2,1,0,3:T(8,128)}), f32[5,10,10,2,384]{4,2,1,0,3:T(8,128)S(1)}, u32[]{:S(2)}, u32[]{:S(2)}) %all-to-all-start.2) | async-done | bytes 1536032 | tf_op jit(solution)/shard_map/all_to_all | solution.py:156
  78.1 6.3 %all-to-all-start = ((f32[5,10,10,2,384]{4,2,1,0,3:T(8,128)}), f32[5,10,10,2,384]{4,2,1,0,3:T(8,128)}, u32[]{:S(2)}, u32[]{:S(2)}) async-start(f32[5,10,10,2,384]{4,2,1,0,3:T(8,128)} %get-tuple-element.44), calls=%async_computation | async-start | bytes 4915200 | tf_op jit(solution)/shard_map/all_to_all | solution.py:154
  94.0 15.7 %all-to-all-done = f32[5,10,10,2,384]{4,2,1,0,3:T(8,128)} async-done(((f32[5,10,10,2,384]{4,2,1,0,3:T(8,128)}), f32[5,10,10,2,384]{4,2,1,0,3:T(8,128)}, u32[]{:S(2)}, u32[]{:S(2)}) %all-to-all-start) | async-done | bytes 1536032 | tf_op jit(solution)/shard_map/all_to_all | solution.py:154
  109.7 7.6 %fusion.37 = f32[10,10,10,384]{3,0,2,1:T(8,128)S(1)} fusion(f32[10,10,384,10]{2,3,1,0:T(8,128)} %fusion.131, f32[10,10,384,10]{2,3,1,0:T(8,128)} %fusion.130, f32[10,10,1,1]{0,1,3,2:T(8,128)S(1)} %copy-done.11, f32[10,10,10,384]{3,2,1,0:T(8,128)} %bitcast.10), kind=kOutput, calls=%fused_computation.71 | convolution fusion | flops 46848000 | bytes 6144400 | tf_op jit(solution)/shard_map/ia,i...->a.../dot_general | solution.py:52
  120.4 15.3 %reshape.219 = f32[10,10,10,6,8,8]{5,4,3,2,1,0:T(8,128)} reshape(f32[10,10,10,384]{3,2,1,0:T(8,128)S(1)} %fusion.38) | data formatting | bytes 3072000 | tf_op jit(solution)/shard_map/reshape | solution.py:167
  147.0 20.9 %select_add_fusion.2 = f32[10,10,10,6,8,8]{5,4,3,2,1,0:T(8,128)} fusion(f32[10,10,10,6,8,8]{5,4,3,2,1,0:T(8,128)} %reshape.219, f32[10,10,6,8,8]{4,3,2,1,0:T(8,128)S(1)} %get-tuple-element.63, f32[10,10,6,8,8]{4,3,2,1,0:T(8,128)S(1)} %get-tuple-element.61, pred[10]{0:T(512)(128)(4,1)S(1)} %iota_compare_fusion.5, pred[10]{0:T(512)(128)(4,1)S(1)} %iota_compare_fusion.6), kind=kLoop, calls=%fused_computation.2 | loop fusion | flops 1536000 | bytes 3379220 | tf_op jit(solution)/shard_map/add | solution.py:73
  167.9 5.9 %fusion.120 = (f32[10,1,10,6,7,8]{5,4,3,2,1,0:T(8,128)}, f32[10,1,10,6,7,8]{5,4,3,2,1,0:T(8,128)}) fusion(f32[10,10,10,6,8,8]{5,4,3,2,1,0:T(8,128)} %select_add_fusion.2), kind=kLoop, calls=%fused_computation.192 | loop fusion | bytes 537600 | tf_op jit(solution)/shard_map/slice | solution.py:69
  173.8 6.9 %fusion.123 = (f32[10,1,10,6,8,8]{5,4,3,2,1,0:T(8,128)}, f32[10,10,6,8,8]{4,3,2,1,0:T(8,128)}, f32[10,10,6,8,8]{4,3,2,1,0:T(8,128)}, f32[10,1,10,6,8,8]{5,4,3,2,1,0:T(8,128)}) fusion(f32[10,1,10,6,7,8]{5,4,3,2,1,0:T(8,128)} %get-tuple-element.33, f32[10,1,10,6,7,8]{5,4,3,2,1,0:T(8,128)} %get-tuple-element.34), kind=kLoop, calls=%fused_computation.195 | loop fusion | bytes 883200 | tf_op jit(solution)/shard_map/concatenate | solution.py:68
  180.8 14.5 %select_add_fusion.1 = f32[10,10,10,6,8,8]{5,4,3,2,1,0:T(8,128)} fusion(f32[10,10,6,8,8]{4,3,2,1,0:T(8,128)} %get-tuple-element.64, f32[10,10,6,8,8]{4,3,2,1,0:T(8,128)} %get-tuple-element.51, pred[10]{0:T(512)(128)(4,1)S(1)} %iota_compare_fusion.5, pred[10]{0:T(512)(128)(4,1)S(1)} %iota_compare_fusion.6, f32[10,10,6,8,8]{4,3,2,1,0:T(8,128)S(1)} %get-tuple-element.63, ...), kind=kLoop, calls=%fused_computation.1 | loop fusion | flops 3072000 | bytes 3686420 | tf_op jit(solution)/shard_map/add | solution.py:73
  204.3 17.5 %select_add_fusion = f32[10,10,10,6,8,8]{5,4,3,2,1,0:T(8,128)} fusion(f32[10,10,6,8,8]{4,3,2,1,0:T(8,128)} %get-tuple-element.57, f32[10,10,6,8,8]{4,3,2,1,0:T(8,128)} %get-tuple-element.55, pred[10]{0:T(512)(128)(4,1)S(1)} %iota_compare_fusion.5, pred[10]{0:T(512)(128)(4,1)S(1)} %iota_compare_fusion.6, f32[10,10,6,8,8]{4,3,2,1,0:T(8,128)} %get-tuple-element.64, ...), kind=kLoop, calls=%fused_computation | loop fusion | flops 4608000 | bytes 3993620 | tf_op jit(solution)/shard_map/add | solution.py:73
  228.2 4.5 %slice_reduce_fusion.1 = (f32[10,10,6,8]{3,2,1,0:T(8,128)S(1)}, f32[10,10,6,8]{3,2,1,0:T(8,128)S(1)}) fusion(f32[10,10,10,6,8,8]{5,4,3,2,1,0:T(8,128)} %select_add_fusion), kind=kLoop, calls=%fused_computation.42 | loop fusion | bytes 76800 | tf_op jit(solution)/shard_map/slice | solution.py:98
  234.9 5.0 %slice_reduce_fusion.3 = (f32[10,10,6,8]{3,2,1,0:T(8,128)}, f32[10,10,6,8]{3,2,1,0:T(8,128)}) fusion(f32[10,10,10,6,8,8]{5,4,3,2,1,0:T(8,128)} %select_add_fusion), kind=kLoop, calls=%fused_computation.143 | loop fusion | bytes 76800 | tf_op jit(solution)/shard_map/slice | solution.py:98
  255.8 9.8 %collective-permute-start = (f32[1]{0:T(128)}, f32[1]{0:T(128)}, u32[]{:S(2)}, u32[]{:S(2)}) collective-permute-start(f32[1]{0:T(128)} %bitcast.39), channel_id=1, source_target_pairs={{0,21},{1,22},{2,23},{3,24},{4,25},{5,26},{6,27},{7,28},{8,29},{9,... | collective-permute-start | bytes 20 | tf_op jit(solution)/shard_map/ppermute | solution.py:19
  269.5 6.9 %collective-permute-start.8 = (f32[1]{0:T(128)}, f32[1]{0:T(128)}, u32[]{:S(2)}, u32[]{:S(2)}) collective-permute-start(f32[1]{0:T(128)} %bitcast.48), channel_id=1, source_target_pairs={{0,11},{1,12},{2,13},{3,14},{4,15},{5,16},{6,17},{7,18},{8,19},{9,... | collective-permute-start | bytes 20 | tf_op jit(solution)/shard_map/ppermute | solution.py:19
  290.1 6.5 %collective-permute-start.6 = (f32[1]{0:T(128)}, f32[1]{0:T(128)}, u32[]{:S(2)}, u32[]{:S(2)}) collective-permute-start(f32[1]{0:T(128)} %bitcast.45), channel_id=1, source_target_pairs={{0,13},{1,14},{2,15},{3,16},{4,17},{5,18},{6,19},{7,20},{8,21},{9,... | collective-permute-start | bytes 20 | tf_op jit(solution)/shard_map/ppermute | solution.py:19
  310.2 4.5 %collective-permute-start.9 = (f32[60]{0:T(128)S(1)}, f32[60]{0:T(128)S(1)}, u32[]{:S(2)}, u32[]{:S(2)}) collective-permute-start(f32[60]{0:T(128)S(1)} %reshape.229), channel_id=1, source_target_pairs={{0,5},{1,6},{2,7},{3,8},{4,9},{5,10},{6,11},{7,12},{8,13},{9,14},{... | collective-permute-start | bytes 728 | tf_op jit(solution)/shard_map/ppermute | solution.py:19
  320.5 7.9 %collective-permute-start.3 = (f32[80]{0:T(128)S(1)}, f32[80]{0:T(128)S(1)}, u32[]{:S(2)}, u32[]{:S(2)}) collective-permute-start(f32[80]{0:T(128)S(1)} %reshape.223), channel_id=1, source_target_pairs={{0,17},{1,18},{2,19},{3,20},{4,21},{5,22},{6,23},{7,24},{8,25},{9,... | collective-permute-start | bytes 968 | tf_op jit(solution)/shard_map/ppermute | solution.py:19
  336.2 6.7 %collective-permute-start.1 = (f32[80]{0:T(128)S(1)}, f32[80]{0:T(128)S(1)}, u32[]{:S(2)}, u32[]{:S(2)}) collective-permute-start(f32[80]{0:T(128)S(1)} %reshape.221), channel_id=1, source_target_pairs={{0,20},{1,21},{2,22},{3,23},{4,24},{5,25},{6,26},{7,27},{8,28},{9,... | collective-permute-start | bytes 968 | tf_op jit(solution)/shard_map/ppermute | solution.py:19
  344.9 5.4 %collective-permute-start.12 = (f32[4800]{0:T(1024)S(1)}, f32[4800]{0:T(1024)S(1)}, u32[]{:S(2)}, u32[]{:S(2)}) collective-permute-start(f32[4800]{0:T(1024)S(1)} %reshape.232), channel_id=1, source_target_pairs={{0,1},{1,2},{2,3},{3,4},{4,5},{5,6},{6,7},{7,8},{8,9},{9,10},{10,1... | collective-permute-start | bytes 57608 | tf_op jit(solution)/shard_map/ppermute | solution.py:19
  365.0 5.7 %collective-permute-start.4 = (f32[6400]{0:T(1024)}, f32[6400]{0:T(1024)}, u32[]{:S(2)}, u32[]{:S(2)}) collective-permute-start(f32[6400]{0:T(1024)} %reshape.224), channel_id=1, source_target_pairs={{0,16},{1,17},{2,18},{3,19},{4,20},{5,21},{6,22},{7,23},{8,24},{9,... | collective-permute-start | bytes 76808 | tf_op jit(solution)/shard_map/ppermute | solution.py:19
  393.0 13.5 %fusion.61 = f32[10,10,10,1,384]{4,2,1,0,3:T(8,128)S(1)} fusion(f32[10,10,10,384]{3,2,1,0:T(8,128)S(1)} %copy-done.3, f32[]{:T(128)} %bitcast.61, f32[10,384]{1,0:T(8,128)S(1)} %copy-done.17, f32[]{:T(128)} %bitcast.58, f32[10,384]{1,0:T(8,128)S(1)} %copy-done.21, f32[10,10,384]{2,1,0:T(8,128)} %broadcast_in_dim.546, f32[10,384]{1,0:T(8,128)S(1)} %copy-done.22, ...), kind=kOutput, calls=%fused_computation.94 | convolution fusion | flops 1811859456 | bytes 5103412 | tf_op jit(solution)/shard_map/abcj,ij->abci/dot_general | solution.py:187
  (270 shorter events, 150.4 us)
Async XLA Ops:
  46.9 31.2 %all-to-all-start.2 = ((f32[5,10,10,2,384]{4,2,1,0,3:T(8,128)}), f32[5,10,10,2,384]{4,2,1,0,3:T(8,128)S(1)}, u32[]{:S(2)}, u32[]{:S(2)}) async-start(f32[5,10,10,2,384]{4,2,1,0,3:T(8,128)} %get-tuple-element.46), calls=%async_computation.2 | async-start | bytes 4915200 | tf_op jit(solution)/shard_map/all_to_all | solution.py:156
  78.1 31.6 %all-to-all-start = ((f32[5,10,10,2,384]{4,2,1,0,3:T(8,128)}), f32[5,10,10,2,384]{4,2,1,0,3:T(8,128)}, u32[]{:S(2)}, u32[]{:S(2)}) async-start(f32[5,10,10,2,384]{4,2,1,0,3:T(8,128)} %get-tuple-element.44), calls=%async_computation | async-start | bytes 4915200 | tf_op jit(solution)/shard_map/all_to_all | solution.py:154
  255.8 32.5 %collective-permute-start = (f32[1]{0:T(128)}, f32[1]{0:T(128)}, u32[]{:S(2)}, u32[]{:S(2)}) collective-permute-start(f32[1]{0:T(128)} %bitcast.39), channel_id=1, source_target_pairs={{0,21},{1,22},{2,23},{3,24},{4,25},{5,26},{6,27},{7,28},{8,29},{9,... | collective-permute-start | bytes 20 | tf_op jit(solution)/shard_map/ppermute | solution.py:19
  265.6 24.5 %collective-permute-start.25 = (f32[1]{0:T(128)}, f32[1]{0:T(128)}, u32[]{:S(2)}, u32[]{:S(2)}) collective-permute-start(f32[1]{0:T(128)} %bitcast.60), channel_id=1, source_target_pairs={{21,0},{22,1},{23,2},{24,3},{25,4},{26,5},{27,6},{28,7},{29,8},{30... | collective-permute-start | bytes 20 | tf_op jit(solution)/shard_map/ppermute | solution.py:19
  266.9 30.4 %collective-permute-start.19 = (f32[1]{0:T(128)}, f32[1]{0:T(128)}, u32[]{:S(2)}, u32[]{:S(2)}) collective-permute-start(f32[1]{0:T(128)} %bitcast.54), channel_id=1, source_target_pairs={{13,0},{14,1},{15,2},{16,3},{17,4},{18,5},{19,6},{20,7},{21,8},{22... | collective-permute-start | bytes 20 | tf_op jit(solution)/shard_map/ppermute | solution.py:19
  268.2 32.6 %collective-permute-start.17 = (f32[1]{0:T(128)}, f32[1]{0:T(128)}, u32[]{:S(2)}, u32[]{:S(2)}) collective-permute-start(f32[1]{0:T(128)} %bitcast.51), channel_id=1, source_target_pairs={{11,0},{12,1},{13,2},{14,3},{15,4},{16,5},{17,6},{18,7},{19,8},{20... | collective-permute-start | bytes 20 | tf_op jit(solution)/shard_map/ppermute | solution.py:19
  269.5 33.9 %collective-permute-start.8 = (f32[1]{0:T(128)}, f32[1]{0:T(128)}, u32[]{:S(2)}, u32[]{:S(2)}) collective-permute-start(f32[1]{0:T(128)} %bitcast.48), channel_id=1, source_target_pairs={{0,11},{1,12},{2,13},{3,14},{4,15},{5,16},{6,17},{7,18},{8,19},{9,... | collective-permute-start | bytes 20 | tf_op jit(solution)/shard_map/ppermute | solution.py:19
  288.3 19.4 %collective-permute-start.23 = (f32[1]{0:T(128)}, f32[1]{0:T(128)}, u32[]{:S(2)}, u32[]{:S(2)}) collective-permute-start(f32[1]{0:T(128)} %bitcast.57), channel_id=1, source_target_pairs={{19,0},{20,1},{21,2},{22,3},{23,4},{24,5},{25,6},{26,7},{27,8},{28... | collective-permute-start | bytes 20 | tf_op jit(solution)/shard_map/ppermute | solution.py:19
  290.1 20.1 %collective-permute-start.6 = (f32[1]{0:T(128)}, f32[1]{0:T(128)}, u32[]{:S(2)}, u32[]{:S(2)}) collective-permute-start(f32[1]{0:T(128)} %bitcast.45), channel_id=1, source_target_pairs={{0,13},{1,14},{2,15},{3,16},{4,17},{5,18},{6,19},{7,20},{8,21},{9,... | collective-permute-start | bytes 20 | tf_op jit(solution)/shard_map/ppermute | solution.py:19
  297.3 18.1 %collective-permute-start.2 = (f32[1]{0:T(128)}, f32[1]{0:T(128)}, u32[]{:S(2)}, u32[]{:S(2)}) collective-permute-start(f32[1]{0:T(128)} %bitcast.42), channel_id=1, source_target_pairs={{0,19},{1,20},{2,21},{3,22},{4,23},{5,24},{6,25},{7,26},{8,27},{9,... | collective-permute-start | bytes 20 | tf_op jit(solution)/shard_map/ppermute | solution.py:19
  300.8 17.0 %collective-permute-start.11 = (f32[60]{0:T(128)S(1)}, f32[60]{0:T(128)S(1)}, u32[]{:S(2)}, u32[]{:S(2)}) collective-permute-start(f32[60]{0:T(128)S(1)} %reshape.231), channel_id=1, source_target_pairs={{0,3},{1,4},{2,5},{3,6},{4,7},{5,8},{6,9},{7,10},{8,11},{9,12},{10... | collective-permute-start | bytes 728 | tf_op jit(solution)/shard_map/ppermute | solution.py:19
  310.2 18.4 %collective-permute-start.9 = (f32[60]{0:T(128)S(1)}, f32[60]{0:T(128)S(1)}, u32[]{:S(2)}, u32[]{:S(2)}) collective-permute-start(f32[60]{0:T(128)S(1)} %reshape.229), channel_id=1, source_target_pairs={{0,5},{1,6},{2,7},{3,8},{4,9},{5,10},{6,11},{7,12},{8,13},{9,14},{... | collective-permute-start | bytes 728 | tf_op jit(solution)/shard_map/ppermute | solution.py:19
  315.4 18.1 %collective-permute-start.5 = (f32[80]{0:T(128)S(1)}, f32[80]{0:T(128)S(1)}, u32[]{:S(2)}, u32[]{:S(2)}) collective-permute-start(f32[80]{0:T(128)S(1)} %reshape.225), channel_id=1, source_target_pairs={{0,15},{1,16},{2,17},{3,18},{4,19},{5,20},{6,21},{7,22},{8,23},{9,... | collective-permute-start | bytes 968 | tf_op jit(solution)/shard_map/ppermute | solution.py:19
  317.9 17.0 %collective-permute-start.20 = (f32[80]{0:T(128)S(1)}, f32[80]{0:T(128)S(1)}, u32[]{:S(2)}, u32[]{:S(2)}) collective-permute-start(f32[80]{0:T(128)S(1)} %reshape.240), channel_id=1, source_target_pairs={{15,0},{16,1},{17,2},{18,3},{19,4},{20,5},{21,6},{22,7},{23,8},{24... | collective-permute-start | bytes 968 | tf_op jit(solution)/shard_map/ppermute | solution.py:19
  319.2 17.0 %collective-permute-start.22 = (f32[80]{0:T(128)S(1)}, f32[80]{0:T(128)S(1)}, u32[]{:S(2)}, u32[]{:S(2)}) collective-permute-start(f32[80]{0:T(128)S(1)} %reshape.242), channel_id=1, source_target_pairs={{17,0},{18,1},{19,2},{20,3},{21,4},{22,5},{23,6},{24,7},{25,8},{26... | collective-permute-start | bytes 968 | tf_op jit(solution)/shard_map/ppermute | solution.py:19
  320.5 22.4 %collective-permute-start.3 = (f32[80]{0:T(128)S(1)}, f32[80]{0:T(128)S(1)}, u32[]{:S(2)}, u32[]{:S(2)}) collective-permute-start(f32[80]{0:T(128)S(1)} %reshape.223), channel_id=1, source_target_pairs={{0,17},{1,18},{2,19},{3,20},{4,21},{5,22},{6,23},{7,24},{8,25},{9,... | collective-permute-start | bytes 968 | tf_op jit(solution)/shard_map/ppermute | solution.py:19
  334.9 17.4 %collective-permute-start.24 = (f32[80]{0:T(128)S(1)}, f32[80]{0:T(128)S(1)}, u32[]{:S(2)}, u32[]{:S(2)}) collective-permute-start(f32[80]{0:T(128)S(1)} %reshape.244), channel_id=1, source_target_pairs={{20,0},{21,1},{22,2},{23,3},{24,4},{25,5},{26,6},{27,7},{28,8},{29... | collective-permute-start | bytes 968 | tf_op jit(solution)/shard_map/ppermute | solution.py:19
  336.2 20.4 %collective-permute-start.1 = (f32[80]{0:T(128)S(1)}, f32[80]{0:T(128)S(1)}, u32[]{:S(2)}, u32[]{:S(2)}) collective-permute-start(f32[80]{0:T(128)S(1)} %reshape.221), channel_id=1, source_target_pairs={{0,20},{1,21},{2,22},{3,23},{4,24},{5,25},{6,26},{7,27},{8,28},{9,... | collective-permute-start | bytes 968 | tf_op jit(solution)/shard_map/ppermute | solution.py:19
  342.9 22.1 %collective-permute-start.13 = (f32[4800]{0:T(1024)S(1)}, f32[4800]{0:T(1024)S(1)}, u32[]{:S(2)}, u32[]{:S(2)}) collective-permute-start(f32[4800]{0:T(1024)S(1)} %reshape.233), channel_id=1, source_target_pairs={{1,0},{2,1},{3,2},{4,3},{5,4},{6,5},{7,6},{8,7},{9,8},{10,9},{11,1... | collective-permute-start | bytes 57608 | tf_op jit(solution)/shard_map/ppermute | solution.py:19
  344.9 25.8 %collective-permute-start.12 = (f32[4800]{0:T(1024)S(1)}, f32[4800]{0:T(1024)S(1)}, u32[]{:S(2)}, u32[]{:S(2)}) collective-permute-start(f32[4800]{0:T(1024)S(1)} %reshape.232), channel_id=1, source_target_pairs={{0,1},{1,2},{2,3},{3,4},{4,5},{5,6},{6,7},{7,8},{8,9},{9,10},{10,1... | collective-permute-start | bytes 57608 | tf_op jit(solution)/shard_map/ppermute | solution.py:19
  350.3 20.4 %collective-permute-start.15 = (f32[4800]{0:T(1024)S(1)}, f32[4800]{0:T(1024)S(1)}, u32[]{:S(2)}, u32[]{:S(2)}) collective-permute-start(f32[4800]{0:T(1024)S(1)} %reshape.235), channel_id=1, source_target_pairs={{4,0},{5,1},{6,2},{7,3},{8,4},{9,5},{10,6},{11,7},{12,8},{13,9},{1... | collective-permute-start | bytes 57608 | tf_op jit(solution)/shard_map/ppermute | solution.py:19
  352.3 18.5 %collective-permute-start.10 = (f32[4800]{0:T(1024)S(1)}, f32[4800]{0:T(1024)S(1)}, u32[]{:S(2)}, u32[]{:S(2)}) collective-permute-start(f32[4800]{0:T(1024)S(1)} %reshape.230), channel_id=1, source_target_pairs={{0,4},{1,5},{2,6},{3,7},{4,8},{5,9},{6,10},{7,11},{8,12},{9,13},{1... | collective-permute-start | bytes 57608 | tf_op jit(solution)/shard_map/ppermute | solution.py:19
  356.6 28.2 %collective-permute-start.21 = (f32[6400]{0:T(1024)}, f32[6400]{0:T(1024)S(1)}, u32[]{:S(2)}, u32[]{:S(2)}) collective-permute-start(f32[6400]{0:T(1024)} %reshape.241), channel_id=1, source_target_pairs={{16,0},{17,1},{18,2},{19,3},{20,4},{21,5},{22,6},{23,7},{24,8},{25... | collective-permute-start | bytes 76808 | tf_op jit(solution)/shard_map/ppermute | solution.py:19
  365.0 19.5 %collective-permute-start.4 = (f32[6400]{0:T(1024)}, f32[6400]{0:T(1024)}, u32[]{:S(2)}, u32[]{:S(2)}) collective-permute-start(f32[6400]{0:T(1024)} %reshape.224), channel_id=1, source_target_pairs={{0,16},{1,17},{2,18},{3,19},{4,20},{5,21},{6,22},{7,23},{8,24},{9,... | collective-permute-start | bytes 76808 | tf_op jit(solution)/shard_map/ppermute | solution.py:19
  (49 other events, 773.9 us)
where the time goes:
time: 417 us; the launch traced here: 410 us
  local copies, waits for them, and re-layouts  148 us (35%)
  starting transfers between devices  97.9 us (23%)
  other arithmetic  57.6 us (14%)
  waiting for transfers between devices  37.5 us (9%)
  matrix products  31.4 us (8%)
  blocking collectives  30.7 us (7%)
  between operations  6.74 us (2%)
    ppermute x26, starting transfers between devices, passed_along(): return lax.ppermute(x, axis, pairs)  86.5 us
    add x3, other arithmetic, local_pass(): return field + jnp.where(node_iota == last_node, add_upper, 0.0)  52.9 us
    broadcast_in_dim x54, local copies, waits for them, and re-layouts, add_region(): jnp.where(region_mask(field.shape, offset, block_grid), values, 0.0)  32.5 us
    all_to_all x1, blocking collectives, body(): lax.all_to_all(fluxes[1], 'comp', split_axis=3, concat_axis=0, tiled=True)  30.7 us
    all_to_all x1, waiting for transfers between devices, body(): lax.all_to_all(fluxes[2], 'comp', split_axis=3, concat_axis=0, tiled=True)  21.8 us
    slice x7, local copies, waits for them, and re-layouts, take_region(): return field[nodes_key + elems_key]  18.2 us
    all_to_all x1, waiting for transfers between devices, body(): lax.all_to_all(fluxes[0], 'comp', split_axis=3, concat_axis=0, tiled=True)  15.7 us
    reshape x1, local copies, waits for them, and re-layouts, body(): canonical.reshape((node_count, node_count, node_count) + block_grid)  15.3 us
  transfers between devices with their start and end apart: 28, of which 2 were waited for; matrix products, arithmetic and copies ran while one was open for 12% of the time, Pallas kernels for 0%

commit v1 on v0

v1 whole, which is shorter than its diff:
```python
import jax
import jax.numpy as jnp
import numpy as np
from jax import lax
from jax.experimental import pallas as pl
from jax.experimental.pallas import tpu as pltpu
from jax.sharding import PartitionSpec as P

BLOCK_X = 6
BLOCK_Y = 8
BLOCK_Z = 8
GRID_Y = 4
LANES = 128

SLAB_AXES = ((1, 2), (0, 2), (0, 1))


def legendre_columns(points, degree):
    columns = [points * 0.0 + 1.0, points]
    for order in range(2, degree + 1):
        columns.append(
            ((2 * order - 1) * points * columns[order - 1] - (order - 1) * columns[order - 2])
            / order
        )
    return columns


def derivative_table(node_count):
    degree = node_count - 1
    points = np.cos(np.pi * np.arange(node_count) / degree)
    for sweep in range(100):
        columns = legendre_columns(points, degree)
        points = points - (points * columns[degree] - columns[degree - 1]) / (
            node_count * columns[degree]
        )
    points = np.sort(points)
    values = legendre_columns(points, degree)[degree]
    identity = np.eye(node_count)
    spacing = points[:, None] - points[None, :] + identity
    matrix = values[:, None] / (values[None, :] * spacing)
    matrix = np.where(identity > 0.5, 0.0, matrix)
    matrix[0, 0] = -degree * (degree + 1) / 4.0
    matrix[degree, degree] = degree * (degree + 1) / 4.0
    return matrix


def weighted(terms):
    total = None
    for value, factor in terms:
        total = value * factor if total is None else total + value * factor
    return total


def transpose_line(line, table):
    count = len(line)
    half = count // 2
    even = [line[i] + line[count - 1 - i] for i in range(half)]
    odd = [line[i] - line[count - 1 - i] for i in range(half)]
    out = [None] * count
    for m in range(half):
        w = count - 1 - m
        both = weighted([(odd[i], float(0.5 * (table[i, m] + table[i, w]))) for i in range(half)])
        diff = weighted([(even[i], float(0.5 * (table[i, m] - table[i, w]))) for i in range(half)])
        out[m] = both + diff
        out[w] = both - diff
    return out


def rows_padded(node_count):
    return (node_count * node_count + 7) // 8 * 8


def flux_kernel(velocity, geometry, *, node_count):
    n = node_count
    planes = velocity.shape[1]
    groups = velocity.shape[5] // LANES
    halves = velocity.shape[4]
    table = derivative_table(n)
    pad = rows_padded(n)
    inner = n - 2

    def body(v_hbm, g_hbm, keep, send, faces, v, g, f0, f1, st, part, sem):
        step = pl.program_id(0)
        comp = lax.axis_index("comp")

        def copies(plane, slot):
            out = []
            for k in range(groups):
                lanes = pl.ds(k * LANES, LANES)
                subs = pl.ds(k * halves, halves)
                out.append(
                    pltpu.make_async_copy(
                        v_hbm.at[:, plane, :, :, :, lanes], v.at[slot, :, :, :, subs, :], sem.at[2 * k, slot]
                    )
                )
                out.append(
                    pltpu.make_async_copy(
                        g_hbm.at[:, :, plane, :, :, :, lanes],
                        g.at[slot, :, :, :, :, subs, :],
                        sem.at[2 * k + 1, slot],
                    )
                )
            return out

        slot = step % 2

        @pl.when(step == 0)
        def _():
            for c in copies(0, 0):
                c.start()

        @pl.when(step + 1 < planes)
        def _():
            for c in copies(step + 1, 1 - slot):
                c.start()

        for c in copies(step, slot):
            c.wait()

        def along_last(b, carry):
            line = []
            for c in range(n):
                vel = [v[slot, i, b, c] for i in range(3)]
                flux = [weighted([(g[slot, i, j, b, c], vel[i]) for i in range(3)]) for j in range(3)]
                f0[step, b, c] = flux[0]
                f1[b, c] = flux[1]
                line.append(flux[2])
            out = transpose_line(line, table)
            for c in range(n):
                st[step, b, c] = out[c]
            return carry

        lax.fori_loop(0, n, along_last, 0)

        def along_mid(c, carry):
            out = transpose_line([f1[b, c] for b in range(n)], table)
            for b in range(n):
                st[step, b, c] = st[step, b, c] + out[b]
            return carry

        lax.fori_loop(0, n, along_mid, 0)

        @pl.when(step == planes - 1)
        def _():
            first = comp == 0
            low = jnp.where(first, 1.0, 0.0)
            own = (low, 1.0 - low)
            coef = [
                [jnp.where(first, float(table[i, m]), float(table[planes + i, m])) for m in range(n)]
                for i in range(planes)
            ]

            def along_first(b, carry):
                for c in range(n):
                    line = [f0[i, b, c] for i in range(planes)]
                    for m in range(n):
                        total = weighted([(line[i], coef[i][m]) for i in range(planes)])
                        row = m * n * n + b * n + c
                        part[pl.ds(pl.multiple_of(row * 8, 8), 8), :] = total + st[m % planes, b, c] * own[m // planes]
                return carry

            lax.fori_loop(0, n, along_first, 0)
            for a in range(inner):
                for b in range(inner):
                    for k in range(groups):
                        base = ((a + 1) * n * n + (b + 1) * n + 1) * 8 + k * halves
                        zero = part[pl.ds(base, inner, stride=8), :]
                        one = part[pl.ds(base + 1, inner, stride=8), :]
                        dst = pl.ds(((a * inner + b) * groups + k) * inner, inner)
                        keep[dst, :] = jnp.where(first, zero, one)
                        send[dst, :] = jnp.where(first, one, zero)
            for h in range(halves):
                for k in range(groups):
                    sub = k * halves + h
                    for side in range(2):
                        at = side * (n - 1)
                        faces[h, side, k, 0 : n * n, :] = part[pl.ds(at * n * n * 8 + sub, n * n, stride=8), :]
                        for a in range(n):
                            faces[h, 2 + side, k, a * n : a * n + n, :] = part[
                                pl.ds((a * n * n + at * n) * 8 + sub, n, stride=8), :
                            ]
                        faces[h, 4 + side, k, 0 : n * n, :] = part[pl.ds(at * 8 + sub, n * n, stride=8 * n), :]

    tile = (8, LANES)
    count = inner * inner * inner * groups
    return pl.pallas_call(
        body,
        grid=(planes,),
        in_specs=[pl.BlockSpec(memory_space=pltpu.HBM), pl.BlockSpec(memory_space=pltpu.HBM)],
        out_specs=[
            pl.BlockSpec((count, LANES), lambda i: (0, 0)),
            pl.BlockSpec((count, LANES), lambda i: (0, 0)),
            pl.BlockSpec((halves, 6, groups, pad, LANES), lambda i: (0, 0, 0, 0, 0)),
        ],
        out_shape=[
            jax.ShapeDtypeStruct((count, LANES), jnp.float32),
            jax.ShapeDtypeStruct((count, LANES), jnp.float32),
            jax.ShapeDtypeStruct((halves, 6, groups, pad, LANES), jnp.float32),
        ],
        scratch_shapes=[
            pltpu.VMEM((2, 3, n, n) + tile, jnp.float32),
            pltpu.VMEM((2, 3, 3, n, n) + tile, jnp.float32),
            pltpu.VMEM((planes, n, n) + tile, jnp.float32),
            pltpu.VMEM((n, n) + tile, jnp.float32),
            pltpu.VMEM((planes, n, n) + tile, jnp.float32),
            pltpu.VMEM((n * n * n * 8, LANES), jnp.float32),
            pltpu.SemaphoreType.DMA((2 * groups, 2)),
        ],
        compiler_params=pltpu.CompilerParams(vmem_limit_bytes=48 * 2**20),
        name="flux",
    )(velocity, geometry)


def lane_iota(rows):
    return lax.broadcasted_iota(jnp.int32, (rows, LANES), 1)


def lane_part(rows, direction):
    lane = lane_iota(rows)
    if direction == 0:
        return lane // (BLOCK_Y * BLOCK_Z)
    if direction == 1:
        return lane // BLOCK_Z % BLOCK_Y
    return lane % BLOCK_Z


STRIDE = (BLOCK_Y * BLOCK_Z, BLOCK_Z, 1)


def turn(x, by):
    by = by % LANES
    return x if by == 0 else pltpu.roll(x, by, 1)


def split_dot(x, matrix, dims):
    high = x.astype(jnp.bfloat16)
    low = (x - high.astype(jnp.float32)).astype(jnp.bfloat16)
    one = lax.dot_general(high, matrix, (dims, ((), ())), preferred_element_type=jnp.float32)
    return one + lax.dot_general(low, matrix, (dims, ((), ())), preferred_element_type=jnp.float32)


def one_hot(place):
    size = place.shape[1]
    target = lax.broadcasted_iota(jnp.int32, (size, size), 0)
    return jnp.where(target == place, 1.0, 0.0).astype(jnp.bfloat16)


def shell(direction, faces, h, k, high):
    return faces[h, 2 * direction + (1 if high else 0), k]


def slots(direction, groups):
    return LANES // STRIDE[direction] if direction == 0 else (BLOCK_Y, BLOCK_Z)[direction - 1]


def payload_x(faces, groups, pad):
    lane = lane_iota(pad)
    low = lane < STRIDE[0]
    high_out = jnp.where(low, turn(faces[0, 1, groups - 1], STRIDE[0]), faces[1, 1, groups - 1])
    low_out = jnp.where(low, faces[0, 0, 0], turn(faces[1, 0, 0], STRIDE[0]))
    return high_out, low_out


def gather_slots(pad, direction, pieces):
    part = lane_part(pad, direction)
    out = jnp.zeros((pad, LANES), jnp.float32)
    for slot, source, value in pieces:
        out = jnp.where(part == slot, turn(value, (slot - source) * STRIDE[direction]), out)
    return out


def payload_y(faces, groups, pad, halves):
    high_out = gather_slots(
        pad, 1, [(h * groups + k, BLOCK_Y - 1, faces[h, 3, k]) for h in range(halves) for k in range(groups)]
    )
    low_out = gather_slots(
        pad, 1, [(h * groups + k, 0, faces[h, 2, k]) for h in range(halves) for k in range(groups)]
    )
    return high_out, low_out


def row_pick(slab_axes, axis, at, n):
    if slab_axes[0] == axis:
        return pl.ds(at * n, n)
    return pl.ds(at, n, stride=n)


def add_direction(faces, h, direction, remote, up, down, n, groups, pad):
    part = lane_part(pad, direction)
    low = [faces[h, 2 * direction, k] for k in range(groups)]
    high = [faces[h, 2 * direction + 1, k] for k in range(groups)]
    for k in range(groups):
        if direction == 0:
            first = lane_iota(pad) < STRIDE[0]
            here = turn(low[k], STRIDE[0])
            after = turn(low[k + 1], STRIDE[0]) if k + 1 < groups else remote(k, True)
            to_high = jnp.where(first, here, after)
            before = turn(high[k - 1], STRIDE[0]) if k > 0 else remote(k, False)
            to_low = jnp.where(first, before, turn(high[k], STRIDE[0]))
        else:
            last = (BLOCK_Y, BLOCK_Z)[direction - 1] - 1
            to_high = jnp.where(part == last, remote(k, True), turn(low[k], -STRIDE[direction]))
            to_low = jnp.where(part == 0, remote(k, False), turn(high[k], STRIDE[direction]))
        faces[h, 2 * direction, k] = low[k] + to_low
        faces[h, 2 * direction + 1, k] = high[k] + to_high
        up[k] = to_high
        down[k] = to_low
    mine = SLAB_AXES[direction]
    for other in range(3):
        if other == direction:
            continue
        for side in range(2):
            source = row_pick(mine, other, side * (n - 1), n)
            for k in range(groups):
                view = faces.at[h, 2 * other + side, k]
                for at, delta in ((0, down), (n - 1, up)):
                    target = row_pick(SLAB_AXES[other], direction, at, n)
                    view[target, :] = view[target, :] + delta.at[k][source, :]


def parity_split(even, high_out, low_out):
    return jnp.where(even, high_out, low_out), jnp.where(even, low_out, high_out)


def whole(*shapes):
    return [jax.ShapeDtypeStruct(s, jnp.float32) for s in shapes]


def vmem_params():
    return pltpu.CompilerParams(vmem_limit_bytes=40 * 2**20)


def place_kernel(raw, own, other, *, n):
    halves, _, groups, pad, _ = raw.shape

    def body(raw_ref, own_ref, other_ref, faces, out_even, out_odd):
        comp = lax.axis_index("comp")
        line = lax.axis_index("elem") // GRID_Y
        for h in range(halves):
            place = jnp.where(comp == h, own_ref[...], other_ref[...])
            matrix = one_hot(place)
            for s in range(6):
                x = jnp.concatenate([raw_ref[h, s, k] for k in range(groups)], axis=1)
                y = split_dot(x, matrix, ((1,), (1,)))
                for k in range(groups):
                    faces[h, s, k] = y[:, k * LANES : (k + 1) * LANES]
        high_out, low_out = payload_x(faces, groups, pad)
        even, odd = parity_split(line % 2 == 0, high_out, low_out)
        out_even[...] = even
        out_odd[...] = odd

    return pl.pallas_call(
        body,
        out_shape=whole(raw.shape, (pad, LANES), (pad, LANES)),
        compiler_params=vmem_params(),
        name="place",
    )(raw, own, other)


def parity_remote(even, got_even, got_odd):
    return jnp.where(even, got_even, got_odd), jnp.where(even, got_odd, got_even)


def x_kernel(faces_in, got_even, got_odd, *, n):
    halves, _, groups, pad, _ = faces_in.shape

    def body(faces_ref, even_ref, odd_ref, faces, out_even, out_odd, up, down):
        elem = lax.axis_index("elem")
        faces[...] = faces_ref[...]
        for_high, for_low = parity_remote(elem // GRID_Y % 2 == 0, even_ref[...], odd_ref[...])
        for h in range(halves):

            def remote(k, high):
                value = for_high if high else for_low
                return turn(value, STRIDE[0]) if (h == 0) == high else value

            add_direction(faces, h, 0, remote, up, down, n, groups, pad)
        high_out, low_out = payload_y(faces, groups, pad, halves)
        even, odd = parity_split(elem % GRID_Y % 2 == 0, high_out, low_out)
        out_even[...] = even
        out_odd[...] = odd

    return pl.pallas_call(
        body,
        out_shape=whole(faces_in.shape, (pad, LANES), (pad, LANES)),
        scratch_shapes=[pltpu.VMEM((groups, pad, LANES), jnp.float32)] * 2,
        compiler_params=vmem_params(),
        name="add_x",
    )(faces_in, got_even, got_odd)


def y_kernel(faces_in, got_even, got_odd, *, n):
    halves, _, groups, pad, _ = faces_in.shape
    last = BLOCK_Z - 1

    def body(faces_ref, even_ref, odd_ref, faces, out, up, down):
        elem = lax.axis_index("elem")
        rep = lax.axis_index("rep")
        faces[...] = faces_ref[...]
        for_high, for_low = parity_remote(elem % GRID_Y % 2 == 0, even_ref[...], odd_ref[...])
        for h in range(halves):

            def remote(k, high):
                slot = h * groups + k
                if high:
                    return turn(for_high, (BLOCK_Y - 1 - slot) * STRIDE[1])
                return turn(for_low, -slot * STRIDE[1])

            add_direction(faces, h, 1, remote, up, down, n, groups, pad)
        lower = rep == 0
        choices = (((0, 1), (0, 0)), ((1, 0), (0, 1)), ((1, 1), (1, 0)))
        outs = []
        for mine, theirs in choices:
            pair = []
            for h, side in (mine, theirs):
                pair.append((h, side))
            outs.append(pair)
        part = lane_part(pad, 2)
        for page in range(2):
            value = jnp.zeros((pad, LANES), jnp.float32)
            for index, (a, b) in enumerate(outs):
                if index // 2 != page:
                    continue
                for k in range(groups):
                    slot = index % 2 * groups + k
                    one = turn(faces[a[0], 4 + a[1], k], slot - a[1] * last)
                    two = turn(faces[b[0], 4 + b[1], k], slot - b[1] * last)
                    value = jnp.where(part == slot, jnp.where(lower, one, two), value)
            out[page] = value

    return pl.pallas_call(
        body,
        out_shape=whole(faces_in.shape, (2, pad, LANES)),
        scratch_shapes=[pltpu.VMEM((groups, pad, LANES), jnp.float32)] * 2,
        compiler_params=vmem_params(),
        name="add_y",
    )(faces_in, got_even, got_odd)


def pack_layout(n, groups):
    pad = rows_padded(n)
    mid = (n - 2) * n
    tall = (pad // 2 + 7) // 8 * 8
    sizes = [pad * groups, mid * groups, mid * groups, tall, mid // 2, mid // 2]
    starts = [sum(sizes[:i]) for i in range(6)]
    return pad, mid, tall, starts, sum(sizes)


def z_kernel(faces_in, got, *, n):
    halves, _, groups, pad, _ = faces_in.shape
    last = BLOCK_Z - 1
    _, mid, tall, starts, total = pack_layout(n, groups)

    def body(faces_ref, got_ref, keep, send, faces, up, down):
        rep = lax.axis_index("rep")
        comp = lax.axis_index("comp")
        faces[...] = faces_ref[...]
        lower = rep == 0
        arrived = {
            (0, True): (0, 1),
            (0, False): (None, 0),
            (1, True): (2, None),
            (1, False): (1, 2),
        }
        for h in range(halves):

            def remote(k, high):
                values = []
                for index in arrived[(h, high)]:
                    if index is None:
                        values.append(jnp.zeros((pad, LANES), jnp.float32))
                    else:
                        slot = index % 2 * groups + k
                        values.append(turn(got_ref[index // 2], (last if high else 0) - slot))
                return jnp.where(lower, values[0], values[1])

            add_direction(faces, h, 2, remote, up, down, n, groups, pad)
        for dst, h in ((keep, comp), (send, 1 - comp)):
            for k in range(groups):
                dst[pl.ds(starts[0] + k * pad, pad), :] = faces[h, 0, k]
                for s in (1, 2):
                    dst[pl.ds(starts[s] + k * mid, mid), :] = faces[h, 2 * s, k, n : n + mid, :]
            x = faces.at[h, 1, groups - 1]
            dst[pl.ds(starts[3], tall), :] = jnp.where(
                lane_iota(tall) < STRIDE[0], turn(x[0:tall, :], STRIDE[0]), x[pad - tall : pad, :]
            )
            for s in (1, 2):
                pieces = []
                for part in range(2):
                    for k in range(groups):
                        rows = faces[h, 2 * s + 1, k, n + part * (mid // 2) : n + (part + 1) * (mid // 2), :]
                        pieces.append((part * groups + k, (BLOCK_Y, BLOCK_Z)[s - 1] - 1, rows))
                dst[pl.ds(starts[3 + s], mid // 2), :] = gather_slots(mid // 2, s, pieces)

    return pl.pallas_call(
        body,
        out_shape=whole((total, LANES), (total, LANES)),
        scratch_shapes=[pltpu.VMEM(faces_in.shape, jnp.float32)]
        + [pltpu.VMEM((groups, pad, LANES), jnp.float32)] * 2,
        compiler_params=vmem_params(),
        name="add_z",
    )(faces_in, got)


def final_kernel(own_face, got_face, own_in, got_in, place, *, n):
    groups = place.shape[1] // LANES
    pad, mid, tall, starts, total = pack_layout(n, groups)
    inner = n - 2

    def body(of, gf, oi, gi, place_ref, out, out_s, faces, sem):
        matrix = one_hot(place_ref[...])
        faces[...] = of[...] + gf[...]

        def put(x, store):
            y = split_dot(jnp.concatenate(x, axis=1), matrix, ((1,), (0,)))
            for k in range(groups):
                store(k, y[:, k * LANES : (k + 1) * LANES])

        first = lane_iota(pad) < STRIDE[0]
        low = [faces[pl.ds(starts[0] + k * pad, pad), :] for k in range(groups)]
        edge = faces[pl.ds(starts[3], tall), :]
        edge_full = jnp.concatenate([turn(edge, STRIDE[0])[: pad - tall], edge], axis=0)
        high = []
        for k in range(groups):
            after = turn(low[k + 1], STRIDE[0]) if k + 1 < groups else edge_full
            high.append(jnp.where(first, turn(low[k], STRIDE[0]), after))
        for side, x in ((0, low), (1, high)):

            def store(k, y):
                out_s[k, side * (n - 1) * n * n : side * (n - 1) * n * n + n * n, :] = y[: n * n]

            put(x, store)
        for s in (1, 2):
            low = [faces[pl.ds(starts[s] + k * mid, mid), :] for k in range(groups)]
            edge = faces[pl.ds(starts[3 + s], mid // 2), :]
            last = (BLOCK_Y, BLOCK_Z)[s - 1] - 1
            part = lane_part(mid, s)
            high = []
            for k in range(groups):
                far = jnp.concatenate(
                    [turn(edge, (last - (p * groups + k)) * STRIDE[s]) for p in range(2)], axis=0
                )
                high.append(jnp.where(part == last, far, turn(low[k], -STRIDE[s])))
            for side, x in ((0, low), (1, high)):

                def store(k, y):
                    for a in range(inner):
                        base = (a + 1) * n * n
                        if s == 1:
                            out_s[k, base + side * (n - 1) * n : base + side * (n - 1) * n + n, :] = y[
                                a * n : a * n + n
                            ]
                        else:
                            out_s.at[k][pl.ds(base + n + side * (n - 1), inner, stride=n), :] = y[
                                a * n + 1 : a * n + 1 + inner
                            ]

                put(x, store)
        for a in range(inner):
            for b in range(inner):
                for k in range(groups):
                    src = pl.ds(((a * inner + b) * groups + k) * inner, inner)
                    base = (a + 1) * n * n + (b + 1) * n + 1
                    out_s[k, base : base + inner, :] = oi[src, :] + gi[src, :]
        done = [
            pltpu.make_async_copy(out_s.at[k], out.at[:, 0, pl.ds(k * LANES, LANES)], sem.at[k])
            for k in range(groups)
        ]
        for c in done:
            c.start()
        for c in done:
            c.wait()

    return pl.pallas_call(
        body,
        out_shape=jax.ShapeDtypeStruct((n * n * n, 1, groups * LANES), jnp.float32),
        out_specs=pl.BlockSpec(memory_space=pltpu.HBM),
        scratch_shapes=[
            pltpu.VMEM((groups, n * n * n, LANES), jnp.float32),
            pltpu.VMEM((total, LANES), jnp.float32),
            pltpu.SemaphoreType.DMA((groups,)),
        ],
        compiler_params=vmem_params(),
        name="final",
    )(own_face, got_face, own_in, got_in, place)


def swap_pairs(count, position, extent, step, odd):
    pairs = []
    for e in range(count):
        at = position(e)
        up = at % 2 == (1 if odd else 0)
        if 0 <= at + (1 if up else -1) < extent:
            pairs.append((e, e + (step if up else -step)))
    return pairs


def exchange(even, odd, count, position, extent, step):
    got_even = lax.ppermute(even, "elem", swap_pairs(count, position, extent, step, False))
    pairs = swap_pairs(count, position, extent, step, True)
    got_odd = lax.ppermute(odd, "elem", pairs) if pairs else jnp.zeros_like(odd)
    return got_even, got_odd


def body(velocity, geometry, element_place):
    n = velocity.shape[1] * lax.axis_size("comp")
    swap = [(0, 1), (1, 0)]
    count = lax.axis_size("elem")
    other_place = lax.ppermute(element_place, "comp", swap)
    own_in, send_in, raw = flux_kernel(velocity, geometry, node_count=n)
    got_in = lax.ppermute(send_in, "comp", swap)
    faces, even, odd = place_kernel(raw, element_place, other_place, n=n)
    even, odd = exchange(even, odd, count, lambda e: e // GRID_Y, count // GRID_Y, GRID_Y)
    faces, even, odd = x_kernel(faces, even, odd, n=n)
    even, odd = exchange(even, odd, count, lambda e: e % GRID_Y, GRID_Y, 1)
    faces, out = y_kernel(faces, even, odd, n=n)
    got = lax.ppermute(out, "rep", swap)
    own_face, send_face = z_kernel(faces, got, n=n)
    got_face = lax.ppermute(send_face, "comp", swap)
    result = final_kernel(own_face, got_face, own_in, got_in, element_place, n=n)
    return result.reshape(n, n, n, 1, element_place.shape[1])


def solution(mesh):
    placed = (
        P(None, "comp", None, None, None, ("elem", "rep")),
        P(None, None, "comp", None, None, None, ("elem", "rep")),
        P("comp", ("elem", "rep")),
    )

    def run(velocity, geometry, element_place):
        with jax.sharding.use_abstract_mesh(mesh.abstract_mesh):
            return jax.shard_map(
                body,
                mesh=mesh,
                in_specs=placed,
                out_specs=P(None, None, None, "comp", ("elem", "rep")),
                check_vma=False,
            )(velocity, geometry, element_place)

    return run
```

time: 417 us -> 65.3 us (0.16)
  the two profiles are of different devices: /device:TPU:7 before, /device:TPU:24 now
where the time goes in v1:
time: 65.3 us; the launch traced here: 65.2 us
  waiting for transfers between devices  40.2 us (62%)
  Pallas kernels  17.3 us (26%)
  starting transfers between devices  7.62 us (12%)
    ppermute x1, waiting for transfers between devices, body(): other_place = lax.ppermute(element_place, 'comp', swap)  17.3 us
    ppermute x1, waiting for transfers between devices, body(): got_face = lax.ppermute(send_face, 'comp', swap)  11.4 us
    pallas_call x1, Pallas kernels, flux_kernel(): pl.pallas_call(body, grid=(planes,), in_specs=[pl.BlockSpec(memory_space=...  11 us
    ppermute x2, waiting for transfers between devices, exchange(): lax.ppermute(even, 'elem', swap_pairs(count, position, extent, step, False))  5.85 us
    ppermute x1, waiting for transfers between devices, exchange(): got_odd = lax.ppermute(odd, 'elem', pairs) if pairs else jnp.zeros_like(odd)  4.3 us
    pallas_call x1, Pallas kernels, place_kernel(): pl.pallas_call(body, out_shape=whole(raw.shape, (pad, LANES), (pad, LANES...  2.35 us
    ppermute x2, starting transfers between devices, exchange(): lax.ppermute(even, 'elem', swap_pairs(count, position, extent, step, False))  1.99 us
    pallas_call x1, Pallas kernels, final_kernel(): pl.pallas_call(body, out_shape=jax.ShapeDtypeStruct((n * n * n, 1, groups...  1.98 us
  transfers between devices with their start and end apart: 7, of which 6 were waited for; matrix products, arithmetic and copies ran while one was open for 0% of the time, Pallas kernels for 7%

profile of v1, /device:TPU:24, one launch (start us, length us, event | category | flops | bytes accessed | tf_op | source)
XLA Modules:
  0.0 65.2 jit_solution(9914040172399434493)
XLA Ops:
  0.0 0.0 copy-start
  0.0 11.0 %flux.1 = (f32[1536,128]{1,0:T(8,128)S(1)}, f32[1536,128]{1,0:T(8,128)S(1)}, f32[2,6,3,104,128]{4,3,2,1,0:T(8,128)S(1)}) custom-call(f32[3,5,10,10,2,384]{5,4,3,2,1,0:T(2,128)} %v_hbm.1, f32[3,3,5,10,10,2,384]{6,5,4,3,2,1,0:T(2,128)} %g_hbm.1), custom_call_target="tpu_custom_call" | custom-call | tf_op jit(solution)/shard_map/flux/pallas_call | solution.py:186
  11.1 1.6 %collective-permute-start.6 = (f32[1536,128]{1,0:T(8,128)S(1)}, f32[1536,128]{1,0:T(8,128)S(1)}, u32[]{:S(2)}, u32[]{:S(2)}) collective-permute-start(f32[1536,128]{1,0:T(8,128)S(1)} %get-tuple-element.28), channel_id=1, source_target_pairs={{0,2},{2,0},{1,3},{3,1},{4,6},{6,4},{5,7},{7,5},{8,10},{10,8},{9,1... | collective-permute-start | bytes 2359304 | tf_op jit(solution)/shard_map/ppermute | solution.py:611
  12.6 0.0 copy-done
  12.6 0.5 collective-permute-start
  13.2 17.3 %collective-permute-done.other_ref = s32[1,384]{1,0:T(1,128)S(1)} collective-permute-done((s32[1,384]{1,0:T(1,128)S(1)}, s32[1,384]{1,0:T(1,128)S(1)}, u32[]{:S(2)}, u32[]{:S(2)}) %collective-permute-start) | collective-permute-done | bytes 1568 | tf_op jit(solution)/shard_map/ppermute | solution.py:609
  30.5 2.4 %place.1 = (f32[2,6,3,104,128]{4,3,2,1,0:T(8,128)S(1)}, f32[104,128]{1,0:T(8,128)S(1)}, f32[104,128]{1,0:T(8,128)}) custom-call(f32[2,6,3,104,128]{4,3,2,1,0:T(8,128)S(1)} %get-tuple-element.17.raw_ref, s32[1,384]{1,0:T(1,128)S(1)} %copy-done, s32[1,384]{1,0:T(1,128)S(1)} %collective-permute-done.other_ref), custom_call_target="tpu_custom_call" | custom-call | tf_op jit(solution)/shard_map/place/pallas_call | solution.py:352
  32.8 0.4 collective-permute-start.1
  33.2 5.2 %collective-permute-done.1.even_ref = f32[104,128]{1,0:T(8,128)S(1)} collective-permute-done((f32[104,128]{1,0:T(8,128)S(1)}, f32[104,128]{1,0:T(8,128)S(1)}, u32[]{:S(2)}, u32[]{:S(2)}) %collective-permute-start.1) | collective-permute-done | bytes 53280 | tf_op jit(solution)/shard_map/ppermute | solution.py:599
  38.4 0.5 add_x.1
  38.9 1.6 %collective-permute-start.2 = (f32[104,128]{1,0:T(8,128)S(1)}, f32[104,128]{1,0:T(8,128)S(1)}, u32[]{:S(2)}, u32[]{:S(2)}) collective-permute-start(f32[104,128]{1,0:T(8,128)S(1)} %get-tuple-element.21), channel_id=1, source_target_pairs={{0,4},{4,0},{8,12},{12,8},{16,20},{20,16},{24,28},{28,24},{1,5},{5... | collective-permute-start | bytes 159752 | tf_op jit(solution)/shard_map/ppermute | solution.py:599
  40.4 1.9 %collective-permute-start.3 = (f32[104,128]{1,0:T(8,128)S(1)}, f32[104,128]{1,0:T(8,128)S(1)}, u32[]{:S(2)}, u32[]{:S(2)}) collective-permute-start(f32[104,128]{1,0:T(8,128)S(1)} %get-tuple-element.22), channel_id=1, source_target_pairs={{4,8},{8,4},{20,24},{24,20},{5,9},{9,5},{21,25},{25,21},{6,10},{10... | collective-permute-start | bytes 159752 | tf_op jit(solution)/shard_map/ppermute | solution.py:601
  42.4 0.7 %collective-permute-done.2.even_ref = f32[104,128]{1,0:T(8,128)S(1)} collective-permute-done((f32[104,128]{1,0:T(8,128)S(1)}, f32[104,128]{1,0:T(8,128)S(1)}, u32[]{:S(2)}, u32[]{:S(2)}) %collective-permute-start.2) | collective-permute-done | bytes 53280 | tf_op jit(solution)/shard_map/ppermute | solution.py:599
  43.1 4.3 %collective-permute-done.3.odd_ref = f32[104,128]{1,0:T(8,128)S(1)} collective-permute-done((f32[104,128]{1,0:T(8,128)S(1)}, f32[104,128]{1,0:T(8,128)S(1)}, u32[]{:S(2)}, u32[]{:S(2)}) %collective-permute-start.3) | collective-permute-done | bytes 53280 | tf_op jit(solution)/shard_map/ppermute | solution.py:601
  47.4 0.7 %add_y.1 = (f32[2,6,3,104,128]{4,3,2,1,0:T(8,128)S(1)}, f32[2,104,128]{2,1,0:T(8,128)S(1)}) custom-call(f32[2,6,3,104,128]{4,3,2,1,0:T(8,128)S(1)} %get-tuple-element.20.faces_ref, f32[104,128]{1,0:T(8,128)S(1)} %collective-permute-done.2.even_ref, f32[104,128]{1,0:T(8,128)S(1)} %collective-permute-done.3.odd_ref), custom_call_target="tpu_custom_call" | custom-call | tf_op jit(solution)/shard_map/add_y/pallas_call | solution.py:431
  48.0 0.1 collective-permute-start.4
  48.1 1.3 %collective-permute-done.4.got_ref = f32[2,104,128]{2,1,0:T(8,128)S(1)} collective-permute-done((f32[2,104,128]{2,1,0:T(8,128)S(1)}, f32[2,104,128]{2,1,0:T(8,128)S(1)}, u32[]{:S(2)}, u32[]{:S(2)}) %collective-permute-start.4) | collective-permute-done | bytes 106528 | tf_op jit(solution)/shard_map/ppermute | solution.py:617
  49.4 0.8 %add_z.1 = (f32[928,128]{1,0:T(8,128)S(1)}, f32[928,128]{1,0:T(8,128)S(1)}) custom-call(f32[2,6,3,104,128]{4,3,2,1,0:T(8,128)S(1)} %get-tuple-element.23.faces_ref, f32[2,104,128]{2,1,0:T(8,128)S(1)} %collective-permute-done.4.got_ref), custom_call_target="tpu_custom_call" | custom-call | tf_op jit(solution)/shard_map/add_z/pallas_call | solution.py:495
  50.2 1.6 %collective-permute-start.5 = (f32[928,128]{1,0:T(8,128)S(1)}, f32[928,128]{1,0:T(8,128)S(1)}, u32[]{:S(2)}, u32[]{:S(2)}) collective-permute-start(f32[928,128]{1,0:T(8,128)S(1)} %get-tuple-element.26), channel_id=1, source_target_pairs={{0,2},{2,0},{1,3},{3,1},{4,6},{6,4},{5,7},{7,5},{8,10},{10,8},{9,1... | collective-permute-start | bytes 1425416 | tf_op jit(solution)/shard_map/ppermute | solution.py:619
  51.8 11.4 %collective-permute-done.5.gf = f32[928,128]{1,0:T(8,128)S(1)} collective-permute-done((f32[928,128]{1,0:T(8,128)S(1)}, f32[928,128]{1,0:T(8,128)S(1)}, u32[]{:S(2)}, u32[]{:S(2)}) %collective-permute-start.5) | collective-permute-done | bytes 475168 | tf_op jit(solution)/shard_map/ppermute | solution.py:619
  63.2 0.0 collective-permute-done.6.gi
  63.2 2.0 %final.1 = f32[1000,1,384]{2,1,0:T(1,128)} custom-call(f32[928,128]{1,0:T(8,128)S(1)} %get-tuple-element.25.of, f32[928,128]{1,0:T(8,128)S(1)} %collective-permute-done.5.gf, f32[1536,128]{1,0:T(8,128)S(1)} %get-tuple-element.27.oi, f32[1536,128]{1,0:T(8,128)S(1)} %collective-permute-done.6.gi, s32[1,384]{1,0:T(1,128)S(1)} %copy-done), custom_call_target="tpu_custom_call" | custom-call | tf_op jit(solution)/shard_map/final/pallas_call | solution.py:574
  (1 shorter events, 0.0 us)
Async XLA Ops:
  0.0 12.6 %copy-start = (s32[1,384]{1,0:T(1,128)S(1)}, s32[1,384]{1,0:T(1,128)}, u32[]{:S(2)}) copy-start(s32[1,384]{1,0:T(1,128)} %place_ref.1) | copy-start | bytes 4612
  11.1 52.2 %collective-permute-start.6 = (f32[1536,128]{1,0:T(8,128)S(1)}, f32[1536,128]{1,0:T(8,128)S(1)}, u32[]{:S(2)}, u32[]{:S(2)}) collective-permute-start(f32[1536,128]{1,0:T(8,128)S(1)} %get-tuple-element.28), channel_id=1, source_target_pairs={{0,2},{2,0},{1,3},{3,1},{4,6},{6,4},{5,7},{7,5},{8,10},{10,8},{9,1... | collective-permute-start | bytes 2359304 | tf_op jit(solution)/shard_map/ppermute | solution.py:611
  12.6 17.8 %collective-permute-start = (s32[1,384]{1,0:T(1,128)S(1)}, s32[1,384]{1,0:T(1,128)S(1)}, u32[]{:S(2)}, u32[]{:S(2)}) collective-permute-start(s32[1,384]{1,0:T(1,128)S(1)} %copy-done), channel_id=1, source_target_pairs={{0,2},{2,0},{1,3},{3,1},{4,6},{6,4},{5,7},{7,5},{8,10},{10,8},{9,1... | collective-permute-start | bytes 4616 | tf_op jit(solution)/shard_map/ppermute | solution.py:609
  32.8 5.6 %collective-permute-start.1 = (f32[104,128]{1,0:T(8,128)S(1)}, f32[104,128]{1,0:T(8,128)S(1)}, u32[]{:S(2)}, u32[]{:S(2)}) collective-permute-start(f32[104,128]{1,0:T(8,128)S(1)} %get-tuple-element.19), channel_id=1, source_target_pairs={{0,16},{4,20},{8,24},{12,28},{16,0},{20,4},{24,8},{28,12},{1,17},{... | collective-permute-start | bytes 159752 | tf_op jit(solution)/shard_map/ppermute | solution.py:599
  38.9 4.2 %collective-permute-start.2 = (f32[104,128]{1,0:T(8,128)S(1)}, f32[104,128]{1,0:T(8,128)S(1)}, u32[]{:S(2)}, u32[]{:S(2)}) collective-permute-start(f32[104,128]{1,0:T(8,128)S(1)} %get-tuple-element.21), channel_id=1, source_target_pairs={{0,4},{4,0},{8,12},{12,8},{16,20},{20,16},{24,28},{28,24},{1,5},{5... | collective-permute-start | bytes 159752 | tf_op jit(solution)/shard_map/ppermute | solution.py:599
  40.4 6.9 %collective-permute-start.3 = (f32[104,128]{1,0:T(8,128)S(1)}, f32[104,128]{1,0:T(8,128)S(1)}, u32[]{:S(2)}, u32[]{:S(2)}) collective-permute-start(f32[104,128]{1,0:T(8,128)S(1)} %get-tuple-element.22), channel_id=1, source_target_pairs={{4,8},{8,4},{20,24},{24,20},{5,9},{9,5},{21,25},{25,21},{6,10},{10... | collective-permute-start | bytes 159752 | tf_op jit(solution)/shard_map/ppermute | solution.py:601
  48.0 1.4 %collective-permute-start.4 = (f32[2,104,128]{2,1,0:T(8,128)S(1)}, f32[2,104,128]{2,1,0:T(8,128)S(1)}, u32[]{:S(2)}, u32[]{:S(2)}) collective-permute-start(f32[2,104,128]{2,1,0:T(8,128)S(1)} %get-tuple-element.24), channel_id=1, source_target_pairs={{0,1},{1,0},{2,3},{3,2},{4,5},{5,4},{6,7},{7,6},{8,9},{9,8},{10,11... | collective-permute-start | bytes 319496 | tf_op jit(solution)/shard_map/ppermute | solution.py:617
  50.2 13.0 %collective-permute-start.5 = (f32[928,128]{1,0:T(8,128)S(1)}, f32[928,128]{1,0:T(8,128)S(1)}, u32[]{:S(2)}, u32[]{:S(2)}) collective-permute-start(f32[928,128]{1,0:T(8,128)S(1)} %get-tuple-element.26), channel_id=1, source_target_pairs={{0,2},{2,0},{1,3},{3,1},{4,6},{6,4},{5,7},{7,5},{8,10},{10,8},{9,1... | collective-permute-start | bytes 1425416 | tf_op jit(solution)/shard_map/ppermute | solution.py:619

commit v2 on v1

--- a/solution.py
+++ b/solution.py
@@ -6,7 +6,7 @@
 from jax.experimental.pallas import tpu as pltpu
 from jax.sharding import PartitionSpec as P
 
-BLOCK_X = 6
+
 BLOCK_Y = 8
 BLOCK_Z = 8
 GRID_Y = 4
@@ -28,7 +28,7 @@
 def derivative_table(node_count):
     degree = node_count - 1
     points = np.cos(np.pi * np.arange(node_count) / degree)
-    for sweep in range(100):
+    for _ in range(100):
         columns = legendre_columns(points, degree)
         points = points - (points * columns[degree] - columns[degree - 1]) / (
             node_count * columns[degree]
@@ -76,139 +76,140 @@
     groups = velocity.shape[5] // LANES
     halves = velocity.shape[4]
     table = derivative_table(n)
-    pad = rows_padded(n)
     inner = n - 2
-
-    def body(v_hbm, g_hbm, keep, send, faces, v, g, f0, f1, st, part, sem):
-        step = pl.program_id(0)
+    early = planes // 2 + 1
+
+    def body(v_hbm, g_hbm, send, part, v, g, f0, f1, st, sem):
         comp = lax.axis_index("comp")
-
-        def copies(plane, slot):
+        first = comp == 0
+
+        def copies(plane):
             out = []
             for k in range(groups):
                 lanes = pl.ds(k * LANES, LANES)
                 subs = pl.ds(k * halves, halves)
                 out.append(
                     pltpu.make_async_copy(
-                        v_hbm.at[:, plane, :, :, :, lanes], v.at[slot, :, :, :, subs, :], sem.at[2 * k, slot]
+                        v_hbm.at[:, plane, :, :, :, lanes], v.at[plane, :, :, :, subs, :], sem.at[2 * k, plane]
                     )
                 )
                 out.append(
                     pltpu.make_async_copy(
                         g_hbm.at[:, :, plane, :, :, :, lanes],
-                        g.at[slot, :, :, :, :, subs, :],
-                        sem.at[2 * k + 1, slot],
+                        g.at[plane, :, :, :, :, subs, :],
+                        sem.at[2 * k + 1, plane],
                     )
                 )
             return out
 
-        slot = step % 2
-
-        @pl.when(step == 0)
-        def _():
-            for c in copies(0, 0):
+        for plane in range(planes):
+            for c in copies(plane):
                 c.start()
 
-        @pl.when(step + 1 < planes)
-        def _():
-            for c in copies(step + 1, 1 - slot):
-                c.start()
-
-        for c in copies(step, slot):
-            c.wait()
-
-        def along_last(b, carry):
-            line = []
+        coef = [
+            [jnp.where(first, float(table[i, m]), float(table[planes + i, m])) for m in range(n)]
+            for i in range(planes)
+        ]
+        low = jnp.where(first, 1.0, 0.0)
+        own = (low, 1.0 - low)
+
+        def row_of(m, b, c):
+            return pl.ds(pl.multiple_of((m * n * n + b * n + c) * 8, 8), 8)
+
+        for plane in range(planes):
+            for c in copies(plane):
+                c.wait()
+
+            def along_last(b, carry):
+                line = []
+                for c in range(n):
+                    vel = [v[plane, i, b, c] for i in range(3)]
+                    flux = [
+                        weighted([(g[plane, i, j, b, c], vel[i]) for i in range(3)]) for j in range(3)
+                    ]
+                    f0[plane, b, c] = flux[0]
+                    f1[b, c] = flux[1]
+                    line.append(flux[2])
+                out = transpose_line(line, table)
+                for c in range(n):
+                    st[plane, b, c] = out[c]
+                return carry
+
+            lax.fori_loop(0, n, along_last, 0)
+
+            def along_mid(c, carry):
+                out = transpose_line([f1[b, c] for b in range(n)], table)
+                for b in range(n):
+                    st[plane, b, c] = st[plane, b, c] + out[b]
+                return carry
+
+            lax.fori_loop(0, n, along_mid, 0)
+            if plane == early - 1:
+
+                def begin_first(b, carry):
+                    for c in range(n):
+                        line = [f0[i, b, c] for i in range(early)]
+                        for m in range(n):
+                            part[row_of(m, b, c), :] = weighted([(line[i], coef[i][m]) for i in range(early)])
+                    return carry
+
+                lax.fori_loop(0, n, begin_first, 0)
+
+        def end_first(b, carry):
             for c in range(n):
-                vel = [v[slot, i, b, c] for i in range(3)]
-                flux = [weighted([(g[slot, i, j, b, c], vel[i]) for i in range(3)]) for j in range(3)]
-                f0[step, b, c] = flux[0]
-                f1[b, c] = flux[1]
-                line.append(flux[2])
-            out = transpose_line(line, table)
-            for c in range(n):
-                st[step, b, c] = out[c]
+                line = [f0[i, b, c] for i in range(early, planes)]
+                for m in range(n):
+                    row = row_of(m, b, c)
+                    rest = weighted([(line[i], coef[early + i][m]) for i in range(planes - early)])
+                    part[row, :] = part[row, :] + rest + st[m % planes, b, c] * own[m // planes]
             return carry
 
-        lax.fori_loop(0, n, along_last, 0)
-
-        def along_mid(c, carry):
-            out = transpose_line([f1[b, c] for b in range(n)], table)
-            for b in range(n):
-                st[step, b, c] = st[step, b, c] + out[b]
-            return carry
-
-        lax.fori_loop(0, n, along_mid, 0)
-
-        @pl.when(step == planes - 1)
-        def _():
-            first = comp == 0
-            low = jnp.where(first, 1.0, 0.0)
-            own = (low, 1.0 - low)
-            coef = [
-                [jnp.where(first, float(table[i, m]), float(table[planes + i, m])) for m in range(n)]
-                for i in range(planes)
-            ]
-
-            def along_first(b, carry):
-                for c in range(n):
-                    line = [f0[i, b, c] for i in range(planes)]
-                    for m in range(n):
-                        total = weighted([(line[i], coef[i][m]) for i in range(planes)])
-                        row = m * n * n + b * n + c
-                        part[pl.ds(pl.multiple_of(row * 8, 8), 8), :] = total + st[m % planes, b, c] * own[m // planes]
-                return carry
-
-            lax.fori_loop(0, n, along_first, 0)
-            for a in range(inner):
-                for b in range(inner):
-                    for k in range(groups):
-                        base = ((a + 1) * n * n + (b + 1) * n + 1) * 8 + k * halves
-                        zero = part[pl.ds(base, inner, stride=8), :]
-                        one = part[pl.ds(base + 1, inner, stride=8), :]
-                        dst = pl.ds(((a * inner + b) * groups + k) * inner, inner)
-                        keep[dst, :] = jnp.where(first, zero, one)
-                        send[dst, :] = jnp.where(first, one, zero)
-            for h in range(halves):
+        lax.fori_loop(0, n, end_first, 0)
+        for a in range(inner):
+            for b in range(inner):
                 for k in range(groups):
-                    sub = k * halves + h
-                    for side in range(2):
-                        at = side * (n - 1)
-                        faces[h, side, k, 0 : n * n, :] = part[pl.ds(at * n * n * 8 + sub, n * n, stride=8), :]
-                        for a in range(n):
-                            faces[h, 2 + side, k, a * n : a * n + n, :] = part[
-                                pl.ds((a * n * n + at * n) * 8 + sub, n, stride=8), :
-                            ]
-                        faces[h, 4 + side, k, 0 : n * n, :] = part[pl.ds(at * 8 + sub, n * n, stride=8 * n), :]
+                    base = ((a + 1) * n * n + (b + 1) * n + 1) * 8 + k * halves
+                    send[pl.ds(((a * inner + b) * groups + k) * inner, inner), :] = part[
+                        pl.ds(base + 1 - comp, inner, stride=8), :
+                    ]
 
     tile = (8, LANES)
-    count = inner * inner * inner * groups
     return pl.pallas_call(
         body,
-        grid=(planes,),
         in_specs=[pl.BlockSpec(memory_space=pltpu.HBM), pl.BlockSpec(memory_space=pltpu.HBM)],
-        out_specs=[
-            pl.BlockSpec((count, LANES), lambda i: (0, 0)),
-            pl.BlockSpec((count, LANES), lambda i: (0, 0)),
-            pl.BlockSpec((halves, 6, groups, pad, LANES), lambda i: (0, 0, 0, 0, 0)),
-        ],
-        out_shape=[
-            jax.ShapeDtypeStruct((count, LANES), jnp.float32),
-            jax.ShapeDtypeStruct((count, LANES), jnp.float32),
-            jax.ShapeDtypeStruct((halves, 6, groups, pad, LANES), jnp.float32),
-        ],
+        out_shape=whole((inner * inner * inner * groups, LANES), (n * n * n * 8, LANES)),
         scratch_shapes=[
-            pltpu.VMEM((2, 3, n, n) + tile, jnp.float32),
-            pltpu.VMEM((2, 3, 3, n, n) + tile, jnp.float32),
+            pltpu.VMEM((planes, 3, n, n) + tile, jnp.float32),
+            pltpu.VMEM((planes, 3, 3, n, n) + tile, jnp.float32),
             pltpu.VMEM((planes, n, n) + tile, jnp.float32),
             pltpu.VMEM((n, n) + tile, jnp.float32),
             pltpu.VMEM((planes, n, n) + tile, jnp.float32),
-            pltpu.VMEM((n * n * n * 8, LANES), jnp.float32),
-            pltpu.SemaphoreType.DMA((2 * groups, 2)),
+            pltpu.SemaphoreType.DMA((2 * groups, planes)),
         ],
-        compiler_params=pltpu.CompilerParams(vmem_limit_bytes=48 * 2**20),
+        compiler_params=pltpu.CompilerParams(vmem_limit_bytes=42 * 2**20),
         name="flux",
     )(velocity, geometry)
+
+
+def keep_kernel(part, *, n, groups, halves):
+    inner = n - 2
+
+    def body(part, keep):
+        comp = lax.axis_index("comp")
+        for a in range(inner):
+            for b in range(inner):
+                for k in range(groups):
+                    base = ((a + 1) * n * n + (b + 1) * n + 1) * 8 + k * halves
+                    keep[pl.ds(((a * inner + b) * groups + k) * inner, inner), :] = part[
+                        pl.ds(base + comp, inner, stride=8), :
+                    ]
+
+    return pl.pallas_call(
+        body,
+        out_shape=whole((inner * inner * inner * groups, LANES))[0],
+        compiler_params=vmem_params(),
+        name="keep",
+    )(part)
 
 
 def lane_iota(rows):
@@ -235,22 +236,14 @@
 def split_dot(x, matrix, dims):
     high = x.astype(jnp.bfloat16)
     low = (x - high.astype(jnp.float32)).astype(jnp.bfloat16)
-    one = lax.dot_general(high, matrix, (dims, ((), ())), preferred_element_type=jnp.float32)
-    return one + lax.dot_general(low, matrix, (dims, ((), ())), preferred_element_type=jnp.float32)
+    both = jnp.concatenate([high, low], axis=1)
+    return lax.dot_general(both, matrix, (dims, ((), ())), preferred_element_type=jnp.float32)
 
 
 def one_hot(place):
     size = place.shape[1]
     target = lax.broadcasted_iota(jnp.int32, (size, size), 0)
     return jnp.where(target == place, 1.0, 0.0).astype(jnp.bfloat16)
-
-
-def shell(direction, faces, h, k, high):
-    return faces[h, 2 * direction + (1 if high else 0), k]
-
-
-def slots(direction, groups):
-    return LANES // STRIDE[direction] if direction == 0 else (BLOCK_Y, BLOCK_Z)[direction - 1]
 
 
 def payload_x(faces, groups, pad):
@@ -330,17 +323,33 @@
     return pltpu.CompilerParams(vmem_limit_bytes=40 * 2**20)
 
 
-def place_kernel(raw, own, other, *, n):
-    halves, _, groups, pad, _ = raw.shape
-
-    def body(raw_ref, own_ref, other_ref, faces, out_even, out_odd):
+def place_kernel(part, own, other, *, n):
+    groups = own.shape[1] // LANES
+    halves = 2
+    pad = rows_padded(n)
+    shape = (halves, 6, groups, pad, LANES)
+
+    def body(part_ref, own_ref, other_ref, faces, out_even, out_odd, line_rows):
         comp = lax.axis_index("comp")
         line = lax.axis_index("elem") // GRID_Y
         for h in range(halves):
             place = jnp.where(comp == h, own_ref[...], other_ref[...])
             matrix = one_hot(place)
+            matrix = jnp.concatenate([matrix, matrix], axis=1)
             for s in range(6):
-                x = jnp.concatenate([raw_ref[h, s, k] for k in range(groups)], axis=1)
+                at = s % 2 * (n - 1)
+                for k in range(groups):
+                    sub = k * halves + h
+                    if s // 2 == 0:
+                        line_rows[s, k, 0 : n * n, :] = part_ref[pl.ds(at * n * n * 8 + sub, n * n, stride=8), :]
+                    elif s // 2 == 2:
+                        line_rows[s, k, 0 : n * n, :] = part_ref[pl.ds(at * 8 + sub, n * n, stride=8 * n), :]
+                    else:
+                        for a in range(n):
+                            line_rows[s, k, a * n : a * n + n, :] = part_ref[
+                                pl.ds((a * n * n + at * n) * 8 + sub, n, stride=8), :
+                            ]
+                x = jnp.concatenate([line_rows[s, k] for k in range(groups)], axis=1)
                 y = split_dot(x, matrix, ((1,), (1,)))
                 for k in range(groups):
                     faces[h, s, k] = y[:, k * LANES : (k + 1) * LANES]
@@ -351,10 +360,11 @@
 
     return pl.pallas_call(
         body,
-        out_shape=whole(raw.shape, (pad, LANES), (pad, LANES)),
+        out_shape=whole(shape, (pad, LANES), (pad, LANES)),
+        scratch_shapes=[pltpu.VMEM(shape[1:], jnp.float32)],
         compiler_params=vmem_params(),
         name="place",
-    )(raw, own, other)
+    )(part, own, other)
 
 
 def parity_remote(even, got_even, got_odd):
@@ -509,6 +519,7 @@
 
     def body(of, gf, oi, gi, place_ref, out, out_s, faces, sem):
         matrix = one_hot(place_ref[...])
+        matrix = jnp.concatenate([matrix, matrix], axis=0)
         faces[...] = of[...] + gf[...]
 
         def put(x, store):
@@ -607,9 +618,12 @@
     swap = [(0, 1), (1, 0)]
     count = lax.axis_size("elem")
     other_place = lax.ppermute(element_place, "comp", swap)
-    own_in, send_in, raw = flux_kernel(velocity, geometry, node_count=n)
+    velocity = pltpu.with_memory_space_constraint(velocity, pltpu.HBM)
+    geometry = pltpu.with_memory_space_constraint(geometry, pltpu.HBM)
+    send_in, part = flux_kernel(velocity, geometry, node_count=n)
     got_in = lax.ppermute(send_in, "comp", swap)
-    faces, even, odd = place_kernel(raw, element_place, other_place, n=n)
+    faces, even, odd = place_kernel(part, element_place, other_place, n=n)
+    own_in = keep_kernel(part, n=n, groups=element_place.shape[1] // LANES, halves=velocity.shape[4])
     even, odd = exchange(even, odd, count, lambda e: e // GRID_Y, count // GRID_Y, GRID_Y)
     faces, even, odd = x_kernel(faces, even, odd, n=n)
     even, odd = exchange(even, odd, count, lambda e: e % GRID_Y, GRID_Y, 1)
@@ -628,14 +642,16 @@
         P("comp", ("elem", "rep")),
     )
 
+    step = jax.shard_map(
+        body,
+        mesh=mesh,
+        in_specs=placed,
+        out_specs=P(None, None, None, "comp", ("elem", "rep")),
+        check_vma=False,
+    )
+
     def run(velocity, geometry, element_place):
         with jax.sharding.use_abstract_mesh(mesh.abstract_mesh):
-            return jax.shard_map(
-                body,
-                mesh=mesh,
-                in_specs=placed,
-                out_specs=P(None, None, None, "comp", ("elem", "rep")),
-                check_vma=False,
-            )(velocity, geometry, element_place)
+            return step(velocity, geometry, element_place)
 
     return run

time: 65.3 us -> 62.4 us (0.956)
  Pallas kernels: 17.3 us -> 14.5 us
    pallas_call x2 -> x3, Pallas kernels: 13.4 us -> 10.7 us  [the longest x1 8.34 us: flux_kernel(): pl.pallas_call(body, in_specs=[pl.BlockSpec(memory_space=pltpu.HBM), pl.B...]
where the time goes in v2:
time: 62.4 us; the launch traced here: 62.2 us
  waiting for transfers between devices  40 us (64%)
  Pallas kernels  14.5 us (23%)
  starting transfers between devices  7.61 us (12%)
    ppermute x1, waiting for transfers between devices, body(): other_place = lax.ppermute(element_place, 'comp', swap)  17.3 us
    ppermute x1, waiting for transfers between devices, body(): got_face = lax.ppermute(send_face, 'comp', swap)  11.3 us
    pallas_call x1, Pallas kernels, flux_kernel(): pl.pallas_call(body, in_specs=[pl.BlockSpec(memory_space=pltpu.HBM), pl.B...  8.34 us
    ppermute x2, waiting for transfers between devices, exchange(): lax.ppermute(even, 'elem', swap_pairs(count, position, extent, step, False))  5.85 us
    ppermute x1, waiting for transfers between devices, exchange(): got_odd = lax.ppermute(odd, 'elem', pairs) if pairs else jnp.zeros_like(odd)  4.3 us
    pallas_call x1, Pallas kernels, place_kernel(): pl.pallas_call(body, out_shape=whole(shape, (pad, LANES), (pad, LANES)),...  2.16 us
    ppermute x2, starting transfers between devices, exchange(): lax.ppermute(even, 'elem', swap_pairs(count, position, extent, step, False))  1.98 us
    pallas_call x1, Pallas kernels, final_kernel(): pl.pallas_call(body, out_shape=jax.ShapeDtypeStruct((n * n * n, 1, groups...  1.94 us
  transfers between devices with their start and end apart: 7, of which 6 were waited for; matrix products, arithmetic and copies ran while one was open for 0% of the time, Pallas kernels for 7%

profile of v2, /device:TPU:24, one launch (start us, length us, event | category | flops | bytes accessed | tf_op | source)
XLA Modules:
  0.0 62.2 jit_solution(12312371624120714131)
XLA Ops:
  0.0 0.0 copy-start
  0.0 8.3 %flux.1 = (f32[1536,128]{1,0:T(8,128)S(1)}, f32[8000,128]{1,0:T(8,128)S(1)}) custom-call(f32[3,5,10,10,2,384]{5,4,3,2,1,0:T(2,128)} %v_hbm.1, f32[3,3,5,10,10,2,384]{6,5,4,3,2,1,0:T(2,128)} %g_hbm.1), custom_call_target="tpu_custom_call" | custom-call | tf_op jit(solution)/shard_map/flux/pallas_call | solution.py:177
  8.3 1.6 %collective-permute-start.6 = (f32[1536,128]{1,0:T(8,128)S(1)}, f32[1536,128]{1,0:T(8,128)S(1)}, u32[]{:S(2)}, u32[]{:S(2)}) collective-permute-start(f32[1536,128]{1,0:T(8,128)S(1)} %get-tuple-element.26), channel_id=1, source_target_pairs={{0,2},{2,0},{1,3},{3,1},{4,6},{6,4},{5,7},{7,5},{8,10},{10,8},{9,1... | collective-permute-start | bytes 2359304 | tf_op jit(solution)/shard_map/ppermute | solution.py:624
  9.9 0.0 copy-done
  9.9 0.5 collective-permute-start
  10.4 17.3 %collective-permute-done.other_ref = s32[1,384]{1,0:T(1,128)S(1)} collective-permute-done((s32[1,384]{1,0:T(1,128)S(1)}, s32[1,384]{1,0:T(1,128)S(1)}, u32[]{:S(2)}, u32[]{:S(2)}) %collective-permute-start) | collective-permute-done | bytes 1568 | tf_op jit(solution)/shard_map/ppermute | solution.py:620
  27.8 2.2 %place.1 = (f32[2,6,3,104,128]{4,3,2,1,0:T(8,128)S(1)}, f32[104,128]{1,0:T(8,128)S(1)}, f32[104,128]{1,0:T(8,128)}) custom-call(f32[8000,128]{1,0:T(8,128)S(1)} %get-tuple-element.16.part_ref.part, s32[1,384]{1,0:T(1,128)S(1)} %copy-done, s32[1,384]{1,0:T(1,128)S(1)} %collective-permute-done.other_ref), custom_call_target="tpu_custom_call" | custom-call | tf_op jit(solution)/shard_map/place/pallas_call | solution.py:361
  29.9 0.4 collective-permute-start.1
  30.3 5.2 %collective-permute-done.1.even_ref = f32[104,128]{1,0:T(8,128)S(1)} collective-permute-done((f32[104,128]{1,0:T(8,128)S(1)}, f32[104,128]{1,0:T(8,128)S(1)}, u32[]{:S(2)}, u32[]{:S(2)}) %collective-permute-start.1) | collective-permute-done | bytes 53280 | tf_op jit(solution)/shard_map/ppermute | solution.py:610
  35.5 0.5 add_x.1
  36.0 1.6 %collective-permute-start.2 = (f32[104,128]{1,0:T(8,128)S(1)}, f32[104,128]{1,0:T(8,128)S(1)}, u32[]{:S(2)}, u32[]{:S(2)}) collective-permute-start(f32[104,128]{1,0:T(8,128)S(1)} %get-tuple-element.20), channel_id=1, source_target_pairs={{0,4},{4,0},{8,12},{12,8},{16,20},{20,16},{24,28},{28,24},{1,5},{5... | collective-permute-start | bytes 159752 | tf_op jit(solution)/shard_map/ppermute | solution.py:610
  37.5 1.9 %collective-permute-start.3 = (f32[104,128]{1,0:T(8,128)S(1)}, f32[104,128]{1,0:T(8,128)S(1)}, u32[]{:S(2)}, u32[]{:S(2)}) collective-permute-start(f32[104,128]{1,0:T(8,128)S(1)} %get-tuple-element.21), channel_id=1, source_target_pairs={{4,8},{8,4},{20,24},{24,20},{5,9},{9,5},{21,25},{25,21},{6,10},{10... | collective-permute-start | bytes 159752 | tf_op jit(solution)/shard_map/ppermute | solution.py:612
  39.5 0.7 %collective-permute-done.2.even_ref = f32[104,128]{1,0:T(8,128)S(1)} collective-permute-done((f32[104,128]{1,0:T(8,128)S(1)}, f32[104,128]{1,0:T(8,128)S(1)}, u32[]{:S(2)}, u32[]{:S(2)}) %collective-permute-start.2) | collective-permute-done | bytes 53280 | tf_op jit(solution)/shard_map/ppermute | solution.py:610
  40.2 4.3 %collective-permute-done.3.odd_ref = f32[104,128]{1,0:T(8,128)S(1)} collective-permute-done((f32[104,128]{1,0:T(8,128)S(1)}, f32[104,128]{1,0:T(8,128)S(1)}, u32[]{:S(2)}, u32[]{:S(2)}) %collective-permute-start.3) | collective-permute-done | bytes 53280 | tf_op jit(solution)/shard_map/ppermute | solution.py:612
  44.5 0.7 %add_y.1 = (f32[2,6,3,104,128]{4,3,2,1,0:T(8,128)S(1)}, f32[2,104,128]{2,1,0:T(8,128)S(1)}) custom-call(f32[2,6,3,104,128]{4,3,2,1,0:T(8,128)S(1)} %get-tuple-element.19.faces_ref, f32[104,128]{1,0:T(8,128)S(1)} %collective-permute-done.2.even_ref, f32[104,128]{1,0:T(8,128)S(1)} %collective-permute-done.3.odd_ref), custom_call_target="tpu_custom_call" | custom-call | tf_op jit(solution)/shard_map/add_y/pallas_call | solution.py:441
  45.1 0.1 collective-permute-start.4
  45.2 1.3 %collective-permute-done.4.got_ref = f32[2,104,128]{2,1,0:T(8,128)S(1)} collective-permute-done((f32[2,104,128]{2,1,0:T(8,128)S(1)}, f32[2,104,128]{2,1,0:T(8,128)S(1)}, u32[]{:S(2)}, u32[]{:S(2)}) %collective-permute-start.4) | collective-permute-done | bytes 106528 | tf_op jit(solution)/shard_map/ppermute | solution.py:631
  46.5 0.8 %add_z.1 = (f32[928,128]{1,0:T(8,128)S(1)}, f32[928,128]{1,0:T(8,128)S(1)}) custom-call(f32[2,6,3,104,128]{4,3,2,1,0:T(8,128)S(1)} %get-tuple-element.22.faces_ref, f32[2,104,128]{2,1,0:T(8,128)S(1)} %collective-permute-done.4.got_ref), custom_call_target="tpu_custom_call" | custom-call | tf_op jit(solution)/shard_map/add_z/pallas_call | solution.py:505
  47.3 1.6 %collective-permute-start.5 = (f32[928,128]{1,0:T(8,128)S(1)}, f32[928,128]{1,0:T(8,128)S(1)}, u32[]{:S(2)}, u32[]{:S(2)}) collective-permute-start(f32[928,128]{1,0:T(8,128)S(1)} %get-tuple-element.25), channel_id=1, source_target_pairs={{0,2},{2,0},{1,3},{3,1},{4,6},{6,4},{5,7},{7,5},{8,10},{10,8},{9,1... | collective-permute-start | bytes 1425416 | tf_op jit(solution)/shard_map/ppermute | solution.py:633
  48.9 0.2 keep.1.oi
  49.0 11.3 %collective-permute-done.5.gf = f32[928,128]{1,0:T(8,128)S(1)} collective-permute-done((f32[928,128]{1,0:T(8,128)S(1)}, f32[928,128]{1,0:T(8,128)S(1)}, u32[]{:S(2)}, u32[]{:S(2)}) %collective-permute-start.5) | collective-permute-done | bytes 475168 | tf_op jit(solution)/shard_map/ppermute | solution.py:633
  60.3 0.0 collective-permute-done.6.gi
  60.3 1.9 %final.1 = f32[1000,1,384]{2,1,0:T(1,128)} custom-call(f32[928,128]{1,0:T(8,128)S(1)} %get-tuple-element.24.of, f32[928,128]{1,0:T(8,128)S(1)} %collective-permute-done.5.gf, f32[1536,128]{1,0:T(8,128)S(1)} %keep.1.oi, f32[1536,128]{1,0:T(8,128)S(1)} %collective-permute-done.6.gi, s32[1,384]{1,0:T(1,128)S(1)} %copy-done), custom_call_target="tpu_custom_call" | custom-call | tf_op jit(solution)/shard_map/final/pallas_call | solution.py:585
  (1 shorter events, 0.0 us)
Async XLA Ops:
  0.0 9.9 %copy-start = (s32[1,384]{1,0:T(1,128)S(1)}, s32[1,384]{1,0:T(1,128)}, u32[]{:S(2)}) copy-start(s32[1,384]{1,0:T(1,128)} %place_ref.1) | copy-start | bytes 4612
  8.3 52.0 %collective-permute-start.6 = (f32[1536,128]{1,0:T(8,128)S(1)}, f32[1536,128]{1,0:T(8,128)S(1)}, u32[]{:S(2)}, u32[]{:S(2)}) collective-permute-start(f32[1536,128]{1,0:T(8,128)S(1)} %get-tuple-element.26), channel_id=1, source_target_pairs={{0,2},{2,0},{1,3},{3,1},{4,6},{6,4},{5,7},{7,5},{8,10},{10,8},{9,1... | collective-permute-start | bytes 2359304 | tf_op jit(solution)/shard_map/ppermute | solution.py:624
  9.9 17.8 %collective-permute-start = (s32[1,384]{1,0:T(1,128)S(1)}, s32[1,384]{1,0:T(1,128)S(1)}, u32[]{:S(2)}, u32[]{:S(2)}) collective-permute-start(s32[1,384]{1,0:T(1,128)S(1)} %copy-done), channel_id=1, source_target_pairs={{0,2},{2,0},{1,3},{3,1},{4,6},{6,4},{5,7},{7,5},{8,10},{10,8},{9,1... | collective-permute-start | bytes 4616 | tf_op jit(solution)/shard_map/ppermute | solution.py:620
  29.9 5.6 %collective-permute-start.1 = (f32[104,128]{1,0:T(8,128)S(1)}, f32[104,128]{1,0:T(8,128)S(1)}, u32[]{:S(2)}, u32[]{:S(2)}) collective-permute-start(f32[104,128]{1,0:T(8,128)S(1)} %get-tuple-element.18), channel_id=1, source_target_pairs={{0,16},{4,20},{8,24},{12,28},{16,0},{20,4},{24,8},{28,12},{1,17},{... | collective-permute-start | bytes 159752 | tf_op jit(solution)/shard_map/ppermute | solution.py:610
  36.0 4.2 %collective-permute-start.2 = (f32[104,128]{1,0:T(8,128)S(1)}, f32[104,128]{1,0:T(8,128)S(1)}, u32[]{:S(2)}, u32[]{:S(2)}) collective-permute-start(f32[104,128]{1,0:T(8,128)S(1)} %get-tuple-element.20), channel_id=1, source_target_pairs={{0,4},{4,0},{8,12},{12,8},{16,20},{20,16},{24,28},{28,24},{1,5},{5... | collective-permute-start | bytes 159752 | tf_op jit(solution)/shard_map/ppermute | solution.py:610
  37.5 6.9 %collective-permute-start.3 = (f32[104,128]{1,0:T(8,128)S(1)}, f32[104,128]{1,0:T(8,128)S(1)}, u32[]{:S(2)}, u32[]{:S(2)}) collective-permute-start(f32[104,128]{1,0:T(8,128)S(1)} %get-tuple-element.21), channel_id=1, source_target_pairs={{4,8},{8,4},{20,24},{24,20},{5,9},{9,5},{21,25},{25,21},{6,10},{10... | collective-permute-start | bytes 159752 | tf_op jit(solution)/shard_map/ppermute | solution.py:612
  45.1 1.4 %collective-permute-start.4 = (f32[2,104,128]{2,1,0:T(8,128)S(1)}, f32[2,104,128]{2,1,0:T(8,128)S(1)}, u32[]{:S(2)}, u32[]{:S(2)}) collective-permute-start(f32[2,104,128]{2,1,0:T(8,128)S(1)} %get-tuple-element.23), channel_id=1, source_target_pairs={{0,1},{1,0},{2,3},{3,2},{4,5},{5,4},{6,7},{7,6},{8,9},{9,8},{10,11... | collective-permute-start | bytes 319496 | tf_op jit(solution)/shard_map/ppermute | solution.py:631
  47.3 13.0 %collective-permute-start.5 = (f32[928,128]{1,0:T(8,128)S(1)}, f32[928,128]{1,0:T(8,128)S(1)}, u32[]{:S(2)}, u32[]{:S(2)}) collective-permute-start(f32[928,128]{1,0:T(8,128)S(1)} %get-tuple-element.25), channel_id=1, source_target_pairs={{0,2},{2,0},{1,3},{3,1},{4,6},{6,4},{5,7},{7,5},{8,10},{10,8},{9,1... | collective-permute-start | bytes 1425416 | tf_op jit(solution)/shard_map/ppermute | solution.py:633

commit v3 on v2

v3 whole, which is shorter than its diff:
```python
import jax
import jax.numpy as jnp
import numpy as np
from jax import lax
from jax.experimental import pallas as pl
from jax.experimental.pallas import tpu as pltpu
from jax.sharding import PartitionSpec as P


BLOCK_Y = 8
BLOCK_Z = 8
GRID_Y = 4
LANES = 128

SLAB_AXES = ((1, 2), (0, 2), (0, 1))


def legendre_columns(points, degree):
    columns = [points * 0.0 + 1.0, points]
    for order in range(2, degree + 1):
        columns.append(
            ((2 * order - 1) * points * columns[order - 1] - (order - 1) * columns[order - 2])
            / order
        )
    return columns


def derivative_table(node_count):
    degree = node_count - 1
    points = np.cos(np.pi * np.arange(node_count) / degree)
    for _ in range(100):
        columns = legendre_columns(points, degree)
        points = points - (points * columns[degree] - columns[degree - 1]) / (
            node_count * columns[degree]
        )
    points = np.sort(points)
    values = legendre_columns(points, degree)[degree]
    identity = np.eye(node_count)
    spacing = points[:, None] - points[None, :] + identity
    matrix = values[:, None] / (values[None, :] * spacing)
    matrix = np.where(identity > 0.5, 0.0, matrix)
    matrix[0, 0] = -degree * (degree + 1) / 4.0
    matrix[degree, degree] = degree * (degree + 1) / 4.0
    return matrix


def weighted(terms):
    total = None
    for value, factor in terms:
        total = value * factor if total is None else total + value * factor
    return total


def transpose_line(line, table):
    count = len(line)
    half = count // 2
    even = [line[i] + line[count - 1 - i] for i in range(half)]
    odd = [line[i] - line[count - 1 - i] for i in range(half)]
    out = [None] * count
    for m in range(half):
        w = count - 1 - m
        both = weighted([(odd[i], float(0.5 * (table[i, m] + table[i, w]))) for i in range(half)])
        diff = weighted([(even[i], float(0.5 * (table[i, m] - table[i, w]))) for i in range(half)])
        out[m] = both + diff
        out[w] = both - diff
    return out


def rows_padded(node_count):
    return (node_count * node_count + 7) // 8 * 8


def plane_at(plane, comp, n):
    return jnp.where(comp == 0, plane, (plane + n // 2) % n) * (n * n * 8)


def flux_kernel(velocity, geometry, *, node_count):
    n = node_count
    planes = velocity.shape[1]
    groups = velocity.shape[5] // LANES
    halves = velocity.shape[4]
    table = derivative_table(n)
    inner = n - 2
    blocks = [(plane, 0, n) for plane in range(planes - 1)]
    blocks += [(planes - 1, 0, n // 2), (planes - 1, n // 2, n - n // 2)]

    def body(v_hbm, g_hbm, send, part, v, g, f0, f1, st, sem):
        comp = lax.axis_index("comp")
        first = comp == 0

        def copies(index):
            plane, start, count = blocks[index]
            rows = pl.ds(start, count)
            out = []
            for k in range(groups):
                lanes = pl.ds(k * LANES, LANES)
                subs = pl.ds(k * halves, halves)
                out.append(
                    pltpu.make_async_copy(
                        v_hbm.at[:, plane, rows, :, :, lanes], v.at[plane, :, rows, :, subs, :], sem.at[2 * k, index]
                    )
                )
                out.append(
                    pltpu.make_async_copy(
                        g_hbm.at[:, :, plane, rows, :, :, lanes],
                        g.at[plane, :, :, rows, :, subs, :],
                        sem.at[2 * k + 1, index],
                    )
                )
            return out

        for index in range(len(blocks)):
            for c in copies(index):
                c.start()

        def row_of(m, b, c):
            return pl.ds(pl.multiple_of((m * n * n + b * n + c) * 8, 8), 8)

        for index, (plane, start, count) in enumerate(blocks):
            for c in copies(index):
                c.wait()

            def along_last(b, carry):
                line = []
                for c in range(n):
                    vel = [v[plane, i, b, c] for i in range(3)]
                    flux = [
                        weighted([(g[plane, i, j, b, c], vel[i]) for i in range(3)]) for j in range(3)
                    ]
                    f0[b, c] = flux[0]
                    f1[b, c] = flux[1]
                    line.append(flux[2])
                out = transpose_line(line, table)
                for c in range(n):
                    st[b, c] = out[c]
                return carry

            lax.fori_loop(start, start + count, along_last, 0)
            if start + count < n:
                continue
            coef = [
                jnp.where(first, float(table[plane, m]), float(table[planes + plane, (m + planes) % n]))
                for m in range(n)
            ]

            def along_others(c, carry):
                out = transpose_line([f1[b, c] for b in range(n)], table)
                for b in range(n):
                    flux = f0[b, c]
                    for m in range(n):
                        value = flux * coef[m]
                        if m == plane:
                            value = value + (st[b, c] + out[b])
                        row = row_of(m, b, c)
                        part[row, :] = value if plane == 0 else part[row, :] + value
                return carry

            lax.fori_loop(0, n, along_others, 0)
        for a in range(inner):
            for b in range(inner):
                for k in range(groups):
                    base = plane_at(a + 1, comp, n) + ((b + 1) * n + 1) * 8 + k * halves
                    send[pl.ds(((a * inner + b) * groups + k) * inner, inner), :] = part[
                        pl.ds(base + 1 - comp, inner, stride=8), :
                    ]

    tile = (8, LANES)
    return pl.pallas_call(
        body,
        in_specs=[pl.BlockSpec(memory_space=pltpu.HBM), pl.BlockSpec(memory_space=pltpu.HBM)],
        out_shape=whole((inner * inner * inner * groups, LANES), (n * n * n * 8, LANES)),
        scratch_shapes=[
            pltpu.VMEM((planes, 3, n, n) + tile, jnp.float32),
            pltpu.VMEM((planes, 3, 3, n, n) + tile, jnp.float32),
            pltpu.VMEM((n, n) + tile, jnp.float32),
            pltpu.VMEM((n, n) + tile, jnp.float32),
            pltpu.VMEM((n, n) + tile, jnp.float32),
            pltpu.SemaphoreType.DMA((2 * groups, planes + 1)),
        ],
        compiler_params=pltpu.CompilerParams(vmem_limit_bytes=42 * 2**20),
        name="flux",
    )(velocity, geometry)


def lane_iota(rows):
    return lax.broadcasted_iota(jnp.int32, (rows, LANES), 1)


def lane_part(rows, direction):
    lane = lane_iota(rows)
    if direction == 0:
        return lane // (BLOCK_Y * BLOCK_Z)
    if direction == 1:
        return lane // BLOCK_Z % BLOCK_Y
    return lane % BLOCK_Z


STRIDE = (BLOCK_Y * BLOCK_Z, BLOCK_Z, 1)


def turn(x, by):
    by = by % LANES
    return x if by == 0 else pltpu.roll(x, by, 1)


def split_dot(x, matrix, dims):
    both = jnp.concatenate(bf16_pair(x), axis=1)
    return lax.dot_general(both, matrix, (dims, ((), ())), preferred_element_type=jnp.float32)


def one_hot(place):
    size = place.shape[1]
    target = lax.broadcasted_iota(jnp.int32, (size, size), 0)
    return jnp.where(target == place, 1.0, 0.0).astype(jnp.bfloat16)


def gather_slots(pad, direction, pieces):
    part = lane_part(pad, direction)
    out = jnp.zeros((pad, LANES), jnp.float32)
    for slot, source, value in pieces:
        out = jnp.where(part == slot, turn(value, (slot - source) * STRIDE[direction]), out)
    return out


def payload_y(faces, groups, pad, halves):
    high_out = gather_slots(
        pad, 1, [(h * groups + k, BLOCK_Y - 1, faces[h, 3, k]) for h in range(halves) for k in range(groups)]
    )
    low_out = gather_slots(
        pad, 1, [(h * groups + k, 0, faces[h, 2, k]) for h in range(halves) for k in range(groups)]
    )
    return high_out, low_out


def row_pick(slab_axes, axis, at, n):
    if slab_axes[0] == axis:
        return pl.ds(at * n, n)
    return pl.ds(at, n, stride=n)


def add_rows(faces, h, direction, up, down, n, picks):
    mine = SLAB_AXES[direction]
    for other in range(3):
        if other == direction:
            continue
        for side in range(2):
            source = row_pick(mine, other, side * (n - 1), n)
            for k, high in picks:
                view = faces.at[h, 2 * other + side, k]
                target = row_pick(SLAB_AXES[other], direction, (n - 1) if high else 0, n)
                delta = up if high else down
                view[target, :] = view[target, :] + delta.at[k][source, :]


def both_picks(groups):
    return [(k, high) for k in range(groups) for high in (False, True)]


def add_direction(faces, h, direction, remote, up, down, n, groups, pad):
    part = lane_part(pad, direction)
    low = [faces[h, 2 * direction, k] for k in range(groups)]
    high = [faces[h, 2 * direction + 1, k] for k in range(groups)]
    zero = jnp.zeros((pad, LANES), jnp.float32)
    for k in range(groups):
        if direction == 0:
            first = lane_iota(pad) < STRIDE[0]
            here = turn(low[k], STRIDE[0])
            after = turn(low[k + 1], STRIDE[0]) if k + 1 < groups else zero
            to_high = jnp.where(first, here, after)
            before = turn(high[k - 1], STRIDE[0]) if k > 0 else zero
            to_low = jnp.where(first, before, turn(high[k], STRIDE[0]))
        else:
            last = (BLOCK_Y, BLOCK_Z)[direction - 1] - 1
            to_high = jnp.where(part == last, remote(k, True), turn(low[k], -STRIDE[direction]))
            to_low = jnp.where(part == 0, remote(k, False), turn(high[k], STRIDE[direction]))
        faces[h, 2 * direction, k] = low[k] + to_low
        faces[h, 2 * direction + 1, k] = high[k] + to_high
        up[k] = to_high
        down[k] = to_low
    add_rows(faces, h, direction, up, down, n, both_picks(groups))


def add_outer_x(faces, h, for_high, for_low, up, down, n, groups, pad):
    first = lane_iota(pad) < STRIDE[0]
    last = groups - 1
    to_high = jnp.where(first, 0.0, turn(for_high, STRIDE[0]) if h == 0 else for_high)
    to_low = jnp.where(first, for_low if h == 0 else turn(for_low, STRIDE[0]), 0.0)
    faces[h, 1, last] = faces[h, 1, last] + to_high
    faces[h, 0, 0] = faces[h, 0, 0] + to_low
    up[last] = to_high
    down[0] = to_low
    add_rows(faces, h, 0, up, down, n, [(last, True), (0, False)])


def parity_split(even, high_out, low_out):
    return jnp.where(even, high_out, low_out), jnp.where(even, low_out, high_out)


def whole(*shapes):
    return [jax.ShapeDtypeStruct(s, jnp.float32) for s in shapes]


def vmem_params():
    return pltpu.CompilerParams(vmem_limit_bytes=40 * 2**20)


def face_rows(part, s, k, h, n, halves, store):
    comp = lax.axis_index("comp")
    at = s % 2 * (n - 1)
    sub = k * halves + h
    if s // 2 == 0:
        store(0, n * n, part[pl.ds(plane_at(at, comp, n) + sub, n * n, stride=8), :])
    elif s // 2 == 2:
        count = n * n // 2
        for p in range(2):
            start = plane_at(p * (n // 2), comp, n) + at * 8 + sub
            store(p * count, count, part[pl.ds(start, count, stride=8 * n), :])
    else:
        for a in range(n):
            store(a * n, n, part[pl.ds(plane_at(a, comp, n) + at * n * 8 + sub, n, stride=8), :])


def bf16_pair(x):
    high = x.astype(jnp.bfloat16)
    return [high, (x - high.astype(jnp.float32)).astype(jnp.bfloat16)]


def edge_kernel(part, own, other, *, n, halves):
    size = own.shape[1]
    groups = size // LANES
    pad = rows_padded(n)
    step = STRIDE[0]

    def body(part_ref, own_ref, other_ref, x_even, x_odd, rows):
        comp = lax.axis_index("comp")
        elem = lax.axis_index("elem")
        payload = []
        for side in range(2):
            pieces = []
            match = []
            for h in range(halves):
                place = jnp.where(comp == h, own_ref[...], other_ref[...])
                lane = lax.broadcasted_iota(jnp.int32, (LANES, size), 0)
                goal = jnp.where(lane // step == h, lane - h * step + (size - step if side else 0), -1)
                one = jnp.where(goal == place, 1.0, 0.0).astype(jnp.bfloat16)
                match += [one, one]
                for k in range(groups):

                    def store(at, count, value):
                        rows[side, h, k, at : at + count, :] = value

                    face_rows(part_ref, side, k, h, n, halves, store)
                pieces += bf16_pair(jnp.concatenate([rows[side, h, k] for k in range(groups)], axis=1))
            payload.append(
                lax.dot_general(
                    jnp.concatenate(pieces, axis=1),
                    jnp.concatenate(match, axis=1),
                    (((1,), (1,)), ((), ())),
                    preferred_element_type=jnp.float32,
                )
            )
        x_even[...], x_odd[...] = parity_split(elem // GRID_Y % 2 == 0, payload[1], payload[0])

    return pl.pallas_call(
        body,
        out_shape=whole((pad, LANES), (pad, LANES)),
        scratch_shapes=[pltpu.VMEM((2, halves, groups, pad, LANES), jnp.float32)],
        compiler_params=vmem_params(),
        name="edge",
    )(part, own, other)


def place_kernel(part, own, other, *, n, halves):
    groups = own.shape[1] // LANES
    pad = rows_padded(n)
    inner = n - 2
    shape = (halves, 6, groups, pad, LANES)

    def body(part_ref, own_ref, other_ref, faces, keep, line_rows, up, down):
        comp = lax.axis_index("comp")
        for h in range(halves):
            place = jnp.where(comp == h, own_ref[...], other_ref[...])
            matrix = one_hot(place)
            matrix = jnp.concatenate([matrix, matrix], axis=1)
            for s in range(6):
                for k in range(groups):

                    def store(at, count, value):
                        line_rows[s, k, at : at + count, :] = value

                    face_rows(part_ref, s, k, h, n, halves, store)
                x = jnp.concatenate([line_rows[s, k] for k in range(groups)], axis=1)
                y = split_dot(x, matrix, ((1,), (1,)))
                for k in range(groups):
                    faces[h, s, k] = y[:, k * LANES : (k + 1) * LANES]
        for h in range(halves):
            add_direction(faces, h, 0, None, up, down, n, groups, pad)
        for a in range(inner):
            for b in range(inner):
                for k in range(groups):
                    base = plane_at(a + 1, comp, n) + ((b + 1) * n + 1) * 8 + k * halves
                    keep[pl.ds(((a * inner + b) * groups + k) * inner, inner), :] = part_ref[
                        pl.ds(base + comp, inner, stride=8), :
                    ]

    return pl.pallas_call(
        body,
        out_shape=whole(shape, (inner * inner * inner * groups, LANES)),
        scratch_shapes=[pltpu.VMEM(shape[1:], jnp.float32)] + [pltpu.VMEM((groups, pad, LANES), jnp.float32)] * 2,
        compiler_params=vmem_params(),
        name="place",
    )(part, own, other)


def parity_remote(even, got_even, got_odd):
    return jnp.where(even, got_even, got_odd), jnp.where(even, got_odd, got_even)


def x_kernel(faces_in, got_even, got_odd, *, n):
    halves, _, groups, pad, _ = faces_in.shape

    def body(faces_ref, even_ref, odd_ref, faces, out_even, out_odd, up, down):
        elem = lax.axis_index("elem")
        for_high, for_low = parity_remote(elem // GRID_Y % 2 == 0, even_ref[...], odd_ref[...])
        for h in range(halves):
            add_outer_x(faces, h, for_high, for_low, up, down, n, groups, pad)
        out_even[...], out_odd[...] = parity_split(
            elem % GRID_Y % 2 == 0, *payload_y(faces, groups, pad, halves)
        )

    return pl.pallas_call(
        body,
        out_shape=whole(faces_in.shape, (pad, LANES), (pad, LANES)),
        scratch_shapes=[pltpu.VMEM((groups, pad, LANES), jnp.float32)] * 2,
        input_output_aliases={0: 0},
        compiler_params=vmem_params(),
        name="add_x",
    )(faces_in, got_even, got_odd)


def y_kernel(faces_in, got_even, got_odd, *, n):
    halves, _, groups, pad, _ = faces_in.shape
    last = BLOCK_Z - 1

    def body(faces_ref, even_ref, odd_ref, faces, out, up, down):
        elem = lax.axis_index("elem")
        rep = lax.axis_index("rep")
        for_high, for_low = parity_remote(elem % GRID_Y % 2 == 0, even_ref[...], odd_ref[...])
        for h in range(halves):

            def remote(k, high):
                slot = h * groups + k
                if high:
                    return turn(for_high, (BLOCK_Y - 1 - slot) * STRIDE[1])
                return turn(for_low, -slot * STRIDE[1])

            add_direction(faces, h, 1, remote, up, down, n, groups, pad)
        lower = rep == 0
        choices = (((0, 1), (0, 0)), ((1, 0), (0, 1)), ((1, 1), (1, 0)))
        outs = []
        for mine, theirs in choices:
            pair = []
            for h, side in (mine, theirs):
                pair.append((h, side))
            outs.append(pair)
        part = lane_part(pad, 2)
        for page in range(2):
            value = jnp.zeros((pad, LANES), jnp.float32)
            for index, (a, b) in enumerate(outs):
                if index // 2 != page:
                    continue
                for k in range(groups):
                    slot = index % 2 * groups + k
                    one = turn(faces[a[0], 4 + a[1], k], slot - a[1] * last)
                    two = turn(faces[b[0], 4 + b[1], k], slot - b[1] * last)
                    value = jnp.where(part == slot, jnp.where(lower, one, two), value)
            out[page] = value

    return pl.pallas_call(
        body,
        out_shape=whole(faces_in.shape, (2, pad, LANES)),
        scratch_shapes=[pltpu.VMEM((groups, pad, LANES), jnp.float32)] * 2,
        input_output_aliases={0: 0},
        compiler_params=vmem_params(),
        name="add_y",
    )(faces_in, got_even, got_odd)


def pack_layout(n, groups):
    pad = rows_padded(n)
    mid = (0, (n - 2) * n, (n - 2) * (n - 2))
    tall = (pad // 2 + 7) // 8 * 8
    sizes = [pad * groups, mid[1] * groups, mid[2] * groups, tall, mid[1] // 2, mid[2] // 2]
    starts = [sum(sizes[:i]) for i in range(6)]
    return pad, mid, tall, starts, sum(sizes)


def middle_rows(view, s, n):
    if s == 1:
        return view[n : n * (n - 1), :]
    return jnp.concatenate([view[a * n + 1 : a * n + n - 1, :] for a in range(1, n - 1)], axis=0)


def z_kernel(faces_in, got, *, n):
    halves, _, groups, pad, _ = faces_in.shape
    last = BLOCK_Z - 1
    _, mid, tall, starts, total = pack_layout(n, groups)

    def body(faces_ref, got_ref, faces, keep, send, up, down):
        rep = lax.axis_index("rep")
        comp = lax.axis_index("comp")
        lower = rep == 0
        arrived = {
            (0, True): (0, 1),
            (0, False): (None, 0),
            (1, True): (2, None),
            (1, False): (1, 2),
        }
        for h in range(halves):

            def remote(k, high):
                values = []
                for index in arrived[(h, high)]:
                    if index is None:
                        values.append(jnp.zeros((pad, LANES), jnp.float32))
                    else:
                        slot = index % 2 * groups + k
                        values.append(turn(got_ref[index // 2], (last if high else 0) - slot))
                return jnp.where(lower, values[0], values[1])

            add_direction(faces, h, 2, remote, up, down, n, groups, pad)
        for dst, h in ((keep, comp), (send, 1 - comp)):
            for k in range(groups):
                dst[pl.ds(starts[0] + k * pad, pad), :] = faces[h, 0, k]
                for s in (1, 2):
                    dst[pl.ds(starts[s] + k * mid[s], mid[s]), :] = middle_rows(faces.at[h, 2 * s, k], s, n)
            x = faces.at[h, 1, groups - 1]
            dst[pl.ds(starts[3], tall), :] = jnp.where(
                lane_iota(tall) < STRIDE[0], turn(x[0:tall, :], STRIDE[0]), x[pad - tall : pad, :]
            )
            for s in (1, 2):
                pieces = []
                size = mid[s] // 2
                for k in range(groups):
                    rows = middle_rows(faces.at[h, 2 * s + 1, k], s, n)
                    for part in range(2):
                        pieces.append(
                            (part * groups + k, (BLOCK_Y, BLOCK_Z)[s - 1] - 1, rows[part * size : (part + 1) * size])
                        )
                dst[pl.ds(starts[3 + s], size), :] = gather_slots(size, s, pieces)

    return pl.pallas_call(
        body,
        out_shape=whole(faces_in.shape, (total, LANES), (total, LANES)),
        scratch_shapes=[pltpu.VMEM((groups, pad, LANES), jnp.float32)] * 2,
        input_output_aliases={0: 0},
        compiler_params=vmem_params(),
        name="add_z",
    )(faces_in, got)[1:]


def unpack(pack, s, n, groups, pad):
    _, mid, tall, starts, _ = pack_layout(n, groups)
    if s == 0:
        first = lane_iota(pad) < STRIDE[0]
        low = [pack[pl.ds(starts[0] + k * pad, pad), :] for k in range(groups)]
        edge = pack[pl.ds(starts[3], tall), :]
        edge_full = jnp.concatenate([turn(edge, STRIDE[0])[: pad - tall], edge], axis=0)
        high = []
        for k in range(groups):
            after = turn(low[k + 1], STRIDE[0]) if k + 1 < groups else edge_full
            high.append(jnp.where(first, turn(low[k], STRIDE[0]), after))
        return low, high
    low = [pack[pl.ds(starts[s] + k * mid[s], mid[s]), :] for k in range(groups)]
    edge = pack[pl.ds(starts[3 + s], mid[s] // 2), :]
    last = (BLOCK_Y, BLOCK_Z)[s - 1] - 1
    part = lane_part(mid[s], s)
    high = []
    for k in range(groups):
        far = jnp.concatenate([turn(edge, (last - (p * groups + k)) * STRIDE[s]) for p in range(2)], axis=0)
        high.append(jnp.where(part == last, far, turn(low[k], -STRIDE[s])))
    return low, high


def to_elements(pack, matrix, s, n, groups, pad, store):
    inner = n - 2
    for side, x in enumerate(unpack(pack, s, n, groups, pad)):
        y = split_dot(jnp.concatenate(x, axis=1), matrix, ((1,), (0,)))
        at = side * (n - 1)
        for k in range(groups):
            z = y[:, k * LANES : (k + 1) * LANES]

            def flat(row, count, step=1):
                return pl.ds(row * groups + k, count, stride=step * groups)

            if s == 0:
                store(flat(at * n * n, n * n), z[: n * n])
            for a in range(inner):
                base = (a + 1) * n * n
                if s == 1:
                    store(flat(base + at * n, n), z[a * n : a * n + n])
                if s == 2:
                    store(flat(base + n + at, inner, n), z[a * inner : (a + 1) * inner])


def early_kernel(own_face, own_in, got_in, place, *, n):
    size = place.shape[1]
    groups = size // LANES
    pad = rows_padded(n)
    inner = n - 2

    def body(of, oi, gi, place_ref, out_s, matrix_ref):
        matrix = one_hot(place_ref[...])
        matrix = jnp.concatenate([matrix, matrix], axis=0)
        matrix_ref[...] = matrix

        def store(rows, value):
            out_s[rows, :] = value

        for s in range(3):
            to_elements(of, matrix, s, n, groups, pad, store)
        for a in range(inner):
            for b in range(inner):
                for k in range(groups):
                    src = pl.ds(((a * inner + b) * groups + k) * inner, inner)
                    base = (a + 1) * n * n + (b + 1) * n + 1
                    out_s[pl.ds(base * groups + k, inner, stride=groups), :] = oi[src, :] + gi[src, :]

    return pl.pallas_call(
        body,
        out_shape=[
            jax.ShapeDtypeStruct((n * n * n * groups, LANES), jnp.float32),
            jax.ShapeDtypeStruct((2 * size, size), jnp.bfloat16),
        ],
        compiler_params=vmem_params(),
        name="early",
    )(own_face, own_in, got_in, place)


def final_kernel(early, matrix, got_face, *, n):
    total = early.shape[0]
    groups = total // (n * n * n)
    pad = rows_padded(n)
    edge = (n * n * groups + 7) // 8 * 8

    def body(early_ref, matrix_ref, gf, out_s, out, sem):
        def store(rows, value):
            out_s[rows, :] = out_s[rows, :] + value

        def copy(index, first, count):
            rows = pl.ds(first, count)
            return pltpu.make_async_copy(out_s.at[rows, :], out.at[rows, :], sem.at[index])

        matrix = matrix_ref[...]
        for s in (1, 2):
            to_elements(gf, matrix, s, n, groups, pad, store)
        done = [copy(0, edge, total - 2 * edge), copy(1, 0, edge), copy(2, total - edge, edge)]
        done[0].start()
        to_elements(gf, matrix, 0, n, groups, pad, store)
        done[1].start()
        done[2].start()
        for c in done:
            c.wait()

    return pl.pallas_call(
        body,
        out_shape=whole(early.shape, early.shape),
        out_specs=[pl.BlockSpec(memory_space=pltpu.VMEM), pl.BlockSpec(memory_space=pltpu.HBM)],
        scratch_shapes=[pltpu.SemaphoreType.DMA((3,))],
        input_output_aliases={0: 0},
        compiler_params=vmem_params(),
        name="final",
    )(early, matrix, got_face)[1]


def pairing(at, extent, odd):
    other = at + (1 if at % 2 == (1 if odd else 0) else -1)
    return other if 0 <= other < extent else None


def neighbour_pairs(count, x_odd, y_odd):
    extent = count // GRID_Y
    pairs = []
    for e in range(count):
        sx, sy = divmod(e, GRID_Y)
        tx = sx if x_odd is None else pairing(sx, extent, x_odd)
        ty = sy if y_odd is None else pairing(sy, GRID_Y, y_odd)
        if tx is not None and ty is not None:
            pairs.append((e, tx * GRID_Y + ty))
    return pairs


def exchange(value, x_odd, y_odd):
    pairs = neighbour_pairs(lax.axis_size("elem"), x_odd, y_odd)
    return lax.ppermute(value, "elem", pairs) if pairs else jnp.zeros_like(value)


def body(velocity, geometry, element_place):
    n = velocity.shape[1] * lax.axis_size("comp")
    swap = [(0, 1), (1, 0)]
    other_place = lax.ppermute(element_place, "comp", swap)
    velocity = pltpu.with_memory_space_constraint(velocity, pltpu.HBM)
    geometry = pltpu.with_memory_space_constraint(geometry, pltpu.HBM)
    send_in, part = flux_kernel(velocity, geometry, node_count=n)
    got_in = lax.ppermute(send_in, "comp", swap)
    halves = velocity.shape[4]
    even, odd = edge_kernel(part, element_place, other_place, n=n, halves=halves)
    even = exchange(even, False, None)
    odd = exchange(odd, True, None)
    faces, own_in = place_kernel(part, element_place, other_place, n=n, halves=halves)
    faces, even, odd = x_kernel(faces, even, odd, n=n)
    odd = exchange(odd, None, True)
    even = exchange(even, None, False)
    faces, out = y_kernel(faces, even, odd, n=n)
    got = lax.ppermute(out, "rep", swap)
    own_face, send_face = z_kernel(faces, got, n=n)
    got_face = lax.ppermute(send_face, "comp", swap)
    early, matrix = early_kernel(own_face, own_in, got_in, element_place, n=n)
    result = final_kernel(early, matrix, got_face, n=n)
    return result.reshape(n, n, n, 1, element_place.shape[1])


def solution(mesh):
    placed = (
        P(None, "comp", None, None, None, ("elem", "rep")),
        P(None, None, "comp", None, None, None, ("elem", "rep")),
        P("comp", ("elem", "rep")),
    )

    step = jax.shard_map(
        body,
        mesh=mesh,
        in_specs=placed,
        out_specs=P(None, None, None, "comp", ("elem", "rep")),
        check_vma=False,
    )

    def run(velocity, geometry, element_place):
        with jax.sharding.use_abstract_mesh(mesh.abstract_mesh):
            return step(velocity, geometry, element_place)

    return run
```

time: 62.4 us -> 59.8 us (0.958)
  the two profiles are of different devices: /device:TPU:24 before, /device:TPU:26 now
where the time goes in v3:
time: 59.8 us; the launch traced here: 59.6 us
  waiting for transfers between devices  37.4 us (63%)
  Pallas kernels  15.6 us (26%)
  starting transfers between devices  6.59 us (11%)
    ppermute x1, waiting for transfers between devices, body(): other_place = lax.ppermute(element_place, 'comp', swap)  17.3 us
    ppermute x1, waiting for transfers between devices, body(): got_face = lax.ppermute(send_face, 'comp', swap)  11 us
    pallas_call x1, Pallas kernels, flux_kernel(): pl.pallas_call(body, in_specs=[pl.BlockSpec(memory_space=pltpu.HBM), pl.B...  7.97 us
    ppermute x3, waiting for transfers between devices, exchange(): lax.ppermute(value, 'elem', pairs)  7.77 us
    ppermute x3, starting transfers between devices, exchange(): lax.ppermute(value, 'elem', pairs)  3.83 us
    pallas_call x1, Pallas kernels, place_kernel(): pl.pallas_call(body, out_shape=whole(shape, (inner * inner * inner * grou...  2.38 us
    pallas_call x1, Pallas kernels, final_kernel(): pl.pallas_call(body, out_shape=whole(early.shape, early.shape), out_specs...  1.7 us
    ppermute x1, starting transfers between devices, body(): other_place = lax.ppermute(element_place, 'comp', swap)  1.49 us
  transfers between devices with their start and end apart: 7, of which 6 were waited for; matrix products, arithmetic and copies ran while one was open for 0% of the time, Pallas kernels for 10%

profile of v3, /device:TPU:26, one launch (start us, length us, event | category | flops | bytes accessed | tf_op | source)
XLA Modules:
  0.0 59.6 jit_solution(9600727917772151921)
XLA Ops:
  0.0 0.0 copy-start
  0.0 8.0 %flux.1 = (f32[1536,128]{1,0:T(8,128)S(1)}, f32[8000,128]{1,0:T(8,128)S(1)}) custom-call(f32[3,5,10,10,2,384]{5,4,3,2,1,0:T(2,128)} %v_hbm.1, f32[3,3,5,10,10,2,384]{6,5,4,3,2,1,0:T(2,128)} %g_hbm.1), custom_call_target="tpu_custom_call" | custom-call | tf_op jit(solution)/shard_map/flux/pallas_call | solution.py:168
  8.0 0.6 %collective-permute-start.5 = (f32[1536,128]{1,0:T(8,128)S(1)}, f32[1536,128]{1,0:T(8,128)S(1)}, u32[]{:S(2)}, u32[]{:S(2)}) collective-permute-start(f32[1536,128]{1,0:T(8,128)S(1)} %get-tuple-element.30), channel_id=1, source_target_pairs={{0,2},{2,0},{1,3},{3,1},{4,6},{6,4},{5,7},{7,5},{8,10},{10,8},{9,1... | collective-permute-start | bytes 2359304 | tf_op jit(solution)/shard_map/ppermute | solution.py:705
  8.6 0.0 copy-done
  8.6 1.5 %collective-permute-start = (s32[1,384]{1,0:T(1,128)S(1)}, s32[1,384]{1,0:T(1,128)S(1)}, u32[]{:S(2)}, u32[]{:S(2)}) collective-permute-start(s32[1,384]{1,0:T(1,128)S(1)} %copy-done), channel_id=1, source_target_pairs={{0,2},{2,0},{1,3},{3,1},{4,6},{6,4},{5,7},{7,5},{8,10},{10,8},{9,1... | collective-permute-start | bytes 4616 | tf_op jit(solution)/shard_map/ppermute | solution.py:701
  10.1 17.3 %collective-permute-done.other_ref = s32[1,384]{1,0:T(1,128)S(1)} collective-permute-done((s32[1,384]{1,0:T(1,128)S(1)}, s32[1,384]{1,0:T(1,128)S(1)}, u32[]{:S(2)}, u32[]{:S(2)}) %collective-permute-start) | collective-permute-done | bytes 1568 | tf_op jit(solution)/shard_map/ppermute | solution.py:701
  27.4 1.0 %edge.1 = (f32[104,128]{1,0:T(8,128)S(1)}, f32[104,128]{1,0:T(8,128)}) custom-call(f32[8000,128]{1,0:T(8,128)S(1)} %get-tuple-element.20.part_ref, s32[1,384]{1,0:T(1,128)S(1)} %copy-done, s32[1,384]{1,0:T(1,128)S(1)} %collective-permute-done.other_ref), custom_call_target="tpu_custom_call" | custom-call | tf_op jit(solution)/shard_map/edge/pallas_call | solution.py:364
  28.4 0.3 collective-permute-start.1
  28.8 2.4 %place.1 = (f32[2,6,3,104,128]{4,3,2,1,0:T(8,128)S(1)}, f32[1536,128]{1,0:T(8,128)S(1)}) custom-call(f32[8000,128]{1,0:T(8,128)S(1)} %get-tuple-element.20.part_ref, s32[1,384]{1,0:T(1,128)S(1)} %copy-done, s32[1,384]{1,0:T(1,128)S(1)} %collective-permute-done.other_ref), custom_call_target="tpu_custom_call" | custom-call | tf_op jit(solution)/shard_map/place/pallas_call | solution.py:406
  31.1 2.8 %collective-permute-done.1.even_ref = f32[104,128]{1,0:T(8,128)S(1)} collective-permute-done((f32[104,128]{1,0:T(8,128)S(1)}, f32[104,128]{1,0:T(8,128)S(1)}, u32[]{:S(2)}, u32[]{:S(2)}) %collective-permute-start.1) | collective-permute-done | bytes 53280 | tf_op jit(solution)/shard_map/ppermute | solution.py:695
  33.9 0.3 add_x.1
  34.2 1.6 %collective-permute-start.2 = (f32[104,128]{1,0:T(8,128)S(1)}, f32[104,128]{1,0:T(8,128)S(1)}, u32[]{:S(2)}, u32[]{:S(2)}) collective-permute-start(f32[104,128]{1,0:T(8,128)S(1)} %get-tuple-element.24), channel_id=1, source_target_pairs={{0,4},{4,0},{8,12},{12,8},{16,20},{20,16},{24,28},{28,24},{1,5},{5... | collective-permute-start | bytes 159752 | tf_op jit(solution)/shard_map/ppermute | solution.py:695
  35.8 1.9 %collective-permute-start.3 = (f32[104,128]{1,0:T(8,128)S(1)}, f32[104,128]{1,0:T(8,128)S(1)}, u32[]{:S(2)}, u32[]{:S(2)}) collective-permute-start(f32[104,128]{1,0:T(8,128)S(1)} %get-tuple-element.25), channel_id=1, source_target_pairs={{4,8},{8,4},{20,24},{24,20},{5,9},{9,5},{21,25},{25,21},{6,10},{10... | collective-permute-start | bytes 159752 | tf_op jit(solution)/shard_map/ppermute | solution.py:695
  37.7 0.7 %collective-permute-done.2.even_ref = f32[104,128]{1,0:T(8,128)S(1)} collective-permute-done((f32[104,128]{1,0:T(8,128)S(1)}, f32[104,128]{1,0:T(8,128)S(1)}, u32[]{:S(2)}, u32[]{:S(2)}) %collective-permute-start.2) | collective-permute-done | bytes 53280 | tf_op jit(solution)/shard_map/ppermute | solution.py:695
  38.4 4.3 %collective-permute-done.3.odd_ref = f32[104,128]{1,0:T(8,128)S(1)} collective-permute-done((f32[104,128]{1,0:T(8,128)S(1)}, f32[104,128]{1,0:T(8,128)S(1)}, u32[]{:S(2)}, u32[]{:S(2)}) %collective-permute-start.3) | collective-permute-done | bytes 53280 | tf_op jit(solution)/shard_map/ppermute | solution.py:695
  42.7 0.7 %add_y.1 = (f32[2,6,3,104,128]{4,3,2,1,0:T(8,128)S(1)}, f32[2,104,128]{2,1,0:T(8,128)S(1)}) custom-call(f32[2,6,3,104,128]{4,3,2,1,0:T(8,128)S(1)} %get-tuple-element.23.faces_ref, f32[104,128]{1,0:T(8,128)S(1)} %collective-permute-done.2.even_ref, f32[104,128]{1,0:T(8,128)S(1)} %collective-permute-done.3.odd_ref), custom_call_target="tpu_custom_call", output_to_operand_aliasing={{0}: (0, {})} | custom-call | tf_op jit(solution)/shard_map/add_y/pallas_call | solution.py:479
  43.4 0.1 collective-permute-start.4
  43.5 1.3 %collective-permute-done.4.got_ref = f32[2,104,128]{2,1,0:T(8,128)S(1)} collective-permute-done((f32[2,104,128]{2,1,0:T(8,128)S(1)}, f32[2,104,128]{2,1,0:T(8,128)S(1)}, u32[]{:S(2)}, u32[]{:S(2)}) %collective-permute-start.4) | collective-permute-done | bytes 106528 | tf_op jit(solution)/shard_map/ppermute | solution.py:715
  44.8 0.8 %add_z.1 = (f32[2,6,3,104,128]{4,3,2,1,0:T(8,128)S(1)}, f32[872,128]{1,0:T(8,128)S(1)}, f32[872,128]{1,0:T(8,128)S(1)}) custom-call(f32[2,6,3,104,128]{4,3,2,1,0:T(8,128)S(1)} %get-tuple-element.26.faces_ref, f32[2,104,128]{2,1,0:T(8,128)S(1)} %collective-permute-done.4.got_ref), custom_call_target="tpu_custom_call", output_to_operand_aliasing={{0}: (0, {})} | custom-call | tf_op jit(solution)/shard_map/add_z/pallas_call | solution.py:552
  45.6 0.6 %collective-permute-start.6 = (f32[872,128]{1,0:T(8,128)S(1)}, f32[872,128]{1,0:T(8,128)S(1)}, u32[]{:S(2)}, u32[]{:S(2)}) collective-permute-start(f32[872,128]{1,0:T(8,128)S(1)} %get-tuple-element.33), channel_id=1, source_target_pairs={{0,2},{2,0},{1,3},{3,1},{4,6},{6,4},{5,7},{7,5},{8,10},{10,8},{9,1... | collective-permute-start | bytes 1339400 | tf_op jit(solution)/shard_map/ppermute | solution.py:717
  46.2 0.0 collective-permute-done.5.gi
  46.2 0.8 %early.1 = (f32[3000,128]{1,0:T(8,128)S(1)}, bf16[768,384]{1,0:T(8,128)(2,1)S(1)}) custom-call(f32[872,128]{1,0:T(8,128)S(1)} %get-tuple-element.28.of, f32[1536,128]{1,0:T(8,128)S(1)} %get-tuple-element.29.oi, f32[1536,128]{1,0:T(8,128)S(1)} %collective-permute-done.5.gi, s32[1,384]{1,0:T(1,128)S(1)} %copy-done), custom_call_target="tpu_custom_call" | custom-call | tf_op jit(solution)/shard_map/early/pallas_call | solution.py:629
  46.9 11.0 %collective-permute-done.6.gf = f32[872,128]{1,0:T(8,128)S(1)} collective-permute-done((f32[872,128]{1,0:T(8,128)S(1)}, f32[872,128]{1,0:T(8,128)S(1)}, u32[]{:S(2)}, u32[]{:S(2)}) %collective-permute-start.6) | collective-permute-done | bytes 446496 | tf_op jit(solution)/shard_map/ppermute | solution.py:717
  57.9 1.7 %final.1 = (f32[3000,128]{1,0:T(8,128)S(1)}, f32[3000,128]{1,0:T(8,128)}) custom-call(f32[3000,128]{1,0:T(8,128)S(1)} %get-tuple-element.31.early_ref, bf16[768,384]{1,0:T(8,128)(2,1)S(1)} %get-tuple-element.32.matrix_ref, f32[872,128]{1,0:T(8,128)S(1)} %collective-permute-done.6.gf), custom_call_target="tpu_custom_call", output_to_operand_aliasing={{0}: (0, {})} | custom-call | tf_op jit(solution)/shard_map/final/pallas_call | solution.py:665
  (1 shorter events, 0.0 us)
Async XLA Ops:
  0.0 8.6 %copy-start = (s32[1,384]{1,0:T(1,128)S(1)}, s32[1,384]{1,0:T(1,128)}, u32[]{:S(2)}) copy-start(s32[1,384]{1,0:T(1,128)} %place_ref.1) | copy-start | bytes 4612
  8.0 38.2 %collective-permute-start.5 = (f32[1536,128]{1,0:T(8,128)S(1)}, f32[1536,128]{1,0:T(8,128)S(1)}, u32[]{:S(2)}, u32[]{:S(2)}) collective-permute-start(f32[1536,128]{1,0:T(8,128)S(1)} %get-tuple-element.30), channel_id=1, source_target_pairs={{0,2},{2,0},{1,3},{3,1},{4,6},{6,4},{5,7},{7,5},{8,10},{10,8},{9,1... | collective-permute-start | bytes 2359304 | tf_op jit(solution)/shard_map/ppermute | solution.py:705
  8.6 18.8 %collective-permute-start = (s32[1,384]{1,0:T(1,128)S(1)}, s32[1,384]{1,0:T(1,128)S(1)}, u32[]{:S(2)}, u32[]{:S(2)}) collective-permute-start(s32[1,384]{1,0:T(1,128)S(1)} %copy-done), channel_id=1, source_target_pairs={{0,2},{2,0},{1,3},{3,1},{4,6},{6,4},{5,7},{7,5},{8,10},{10,8},{9,1... | collective-permute-start | bytes 4616 | tf_op jit(solution)/shard_map/ppermute | solution.py:701
  28.4 5.5 %collective-permute-start.1 = (f32[104,128]{1,0:T(8,128)S(1)}, f32[104,128]{1,0:T(8,128)S(1)}, u32[]{:S(2)}, u32[]{:S(2)}) collective-permute-start(f32[104,128]{1,0:T(8,128)S(1)} %get-tuple-element.22), channel_id=1, source_target_pairs={{0,16},{4,20},{8,24},{12,28},{16,0},{20,4},{24,8},{28,12},{1,17},{... | collective-permute-start | bytes 159752 | tf_op jit(solution)/shard_map/ppermute | solution.py:695
  34.2 4.2 %collective-permute-start.2 = (f32[104,128]{1,0:T(8,128)S(1)}, f32[104,128]{1,0:T(8,128)S(1)}, u32[]{:S(2)}, u32[]{:S(2)}) collective-permute-start(f32[104,128]{1,0:T(8,128)S(1)} %get-tuple-element.24), channel_id=1, source_target_pairs={{0,4},{4,0},{8,12},{12,8},{16,20},{20,16},{24,28},{28,24},{1,5},{5... | collective-permute-start | bytes 159752 | tf_op jit(solution)/shard_map/ppermute | solution.py:695
  35.8 6.9 %collective-permute-start.3 = (f32[104,128]{1,0:T(8,128)S(1)}, f32[104,128]{1,0:T(8,128)S(1)}, u32[]{:S(2)}, u32[]{:S(2)}) collective-permute-start(f32[104,128]{1,0:T(8,128)S(1)} %get-tuple-element.25), channel_id=1, source_target_pairs={{4,8},{8,4},{20,24},{24,20},{5,9},{9,5},{21,25},{25,21},{6,10},{10... | collective-permute-start | bytes 159752 | tf_op jit(solution)/shard_map/ppermute | solution.py:695
  43.4 1.4 %collective-permute-start.4 = (f32[2,104,128]{2,1,0:T(8,128)S(1)}, f32[2,104,128]{2,1,0:T(8,128)S(1)}, u32[]{:S(2)}, u32[]{:S(2)}) collective-permute-start(f32[2,104,128]{2,1,0:T(8,128)S(1)} %get-tuple-element.27), channel_id=1, source_target_pairs={{0,1},{1,0},{2,3},{3,2},{4,5},{5,4},{6,7},{7,6},{8,9},{9,8},{10,11... | collective-permute-start | bytes 319496 | tf_op jit(solution)/shard_map/ppermute | solution.py:715
  45.6 12.4 %collective-permute-start.6 = (f32[872,128]{1,0:T(8,128)S(1)}, f32[872,128]{1,0:T(8,128)S(1)}, u32[]{:S(2)}, u32[]{:S(2)}) collective-permute-start(f32[872,128]{1,0:T(8,128)S(1)} %get-tuple-element.33), channel_id=1, source_target_pairs={{0,2},{2,0},{1,3},{3,1},{4,6},{6,4},{5,7},{7,5},{8,10},{10,8},{9,1... | collective-permute-start | bytes 1339400 | tf_op jit(solution)/shard_map/ppermute | solution.py:717

commit v4 on v3

--- a/solution.py
+++ b/solution.py
@@ -412,8 +412,11 @@
     )(part, own, other)
 
 
-def parity_remote(even, got_even, got_odd):
-    return jnp.where(even, got_even, got_odd), jnp.where(even, got_odd, got_even)
+def parity_remote(at, extent, got_even, got_odd):
+    even = at % 2 == 0
+    high = jnp.where(even, got_even, got_odd)
+    low = jnp.where(even, got_odd, got_even)
+    return jnp.where(at + 1 < extent, high, 0.0), jnp.where(at > 0, low, 0.0)
 
 
 def x_kernel(faces_in, got_even, got_odd, *, n):
@@ -421,7 +424,8 @@
 
     def body(faces_ref, even_ref, odd_ref, faces, out_even, out_odd, up, down):
         elem = lax.axis_index("elem")
-        for_high, for_low = parity_remote(elem // GRID_Y % 2 == 0, even_ref[...], odd_ref[...])
+        extent = lax.axis_size("elem") // GRID_Y
+        for_high, for_low = parity_remote(elem // GRID_Y, extent, even_ref[...], odd_ref[...])
         for h in range(halves):
             add_outer_x(faces, h, for_high, for_low, up, down, n, groups, pad)
         out_even[...], out_odd[...] = parity_split(
@@ -445,7 +449,7 @@
     def body(faces_ref, even_ref, odd_ref, faces, out, up, down):
         elem = lax.axis_index("elem")
         rep = lax.axis_index("rep")
-        for_high, for_low = parity_remote(elem % GRID_Y % 2 == 0, even_ref[...], odd_ref[...])
+        for_high, for_low = parity_remote(elem % GRID_Y, GRID_Y, even_ref[...], odd_ref[...])
         for h in range(halves):
 
             def remote(k, high):
@@ -490,9 +494,10 @@
     pad = rows_padded(n)
     mid = (0, (n - 2) * n, (n - 2) * (n - 2))
     tall = (pad // 2 + 7) // 8 * 8
-    sizes = [pad * groups, mid[1] * groups, mid[2] * groups, tall, mid[1] // 2, mid[2] // 2]
-    starts = [sum(sizes[:i]) for i in range(6)]
-    return pad, mid, tall, starts, sum(sizes)
+    x_sizes = [pad * groups, tall]
+    sizes = [mid[1] * groups, mid[2] * groups, mid[1] // 2, mid[2] // 2]
+    starts = [0] + [sum(sizes[:i]) for i in range(4)]
+    return pad, mid, tall, starts, (sum(x_sizes), sum(sizes))
 
 
 def middle_rows(view, s, n):
@@ -504,9 +509,9 @@
 def z_kernel(faces_in, got, *, n):
     halves, _, groups, pad, _ = faces_in.shape
     last = BLOCK_Z - 1
-    _, mid, tall, starts, total = pack_layout(n, groups)
-
-    def body(faces_ref, got_ref, faces, keep, send, up, down):
+    _, mid, tall, starts, totals = pack_layout(n, groups)
+
+    def body(faces_ref, got_ref, faces, keep_x, keep, send_x, send, up, down):
         rep = lax.axis_index("rep")
         comp = lax.axis_index("comp")
         lower = rep == 0
@@ -529,13 +534,13 @@
                 return jnp.where(lower, values[0], values[1])
 
             add_direction(faces, h, 2, remote, up, down, n, groups, pad)
-        for dst, h in ((keep, comp), (send, 1 - comp)):
+        for dst_x, dst, h in ((keep_x, keep, comp), (send_x, send, 1 - comp)):
             for k in range(groups):
-                dst[pl.ds(starts[0] + k * pad, pad), :] = faces[h, 0, k]
+                dst_x[pl.ds(k * pad, pad), :] = faces[h, 0, k]
                 for s in (1, 2):
                     dst[pl.ds(starts[s] + k * mid[s], mid[s]), :] = middle_rows(faces.at[h, 2 * s, k], s, n)
             x = faces.at[h, 1, groups - 1]
-            dst[pl.ds(starts[3], tall), :] = jnp.where(
+            dst_x[pl.ds(groups * pad, tall), :] = jnp.where(
                 lane_iota(tall) < STRIDE[0], turn(x[0:tall, :], STRIDE[0]), x[pad - tall : pad, :]
             )
             for s in (1, 2):
@@ -547,11 +552,11 @@
                         pieces.append(
                             (part * groups + k, (BLOCK_Y, BLOCK_Z)[s - 1] - 1, rows[part * size : (part + 1) * size])
                         )
-                dst[pl.ds(starts[3 + s], size), :] = gather_slots(size, s, pieces)
-
-    return pl.pallas_call(
-        body,
-        out_shape=whole(faces_in.shape, (total, LANES), (total, LANES)),
+                dst[pl.ds(starts[2 + s], size), :] = gather_slots(size, s, pieces)
+
+    return pl.pallas_call(
+        body,
+        out_shape=whole(faces_in.shape, *[(total, LANES) for total in totals * 2]),
         scratch_shapes=[pltpu.VMEM((groups, pad, LANES), jnp.float32)] * 2,
         input_output_aliases={0: 0},
         compiler_params=vmem_params(),
@@ -563,8 +568,8 @@
     _, mid, tall, starts, _ = pack_layout(n, groups)
     if s == 0:
         first = lane_iota(pad) < STRIDE[0]
-        low = [pack[pl.ds(starts[0] + k * pad, pad), :] for k in range(groups)]
-        edge = pack[pl.ds(starts[3], tall), :]
+        low = [pack[pl.ds(k * pad, pad), :] for k in range(groups)]
+        edge = pack[pl.ds(groups * pad, tall), :]
         edge_full = jnp.concatenate([turn(edge, STRIDE[0])[: pad - tall], edge], axis=0)
         high = []
         for k in range(groups):
@@ -572,7 +577,7 @@
             high.append(jnp.where(first, turn(low[k], STRIDE[0]), after))
         return low, high
     low = [pack[pl.ds(starts[s] + k * mid[s], mid[s]), :] for k in range(groups)]
-    edge = pack[pl.ds(starts[3 + s], mid[s] // 2), :]
+    edge = pack[pl.ds(starts[2 + s], mid[s] // 2), :]
     last = (BLOCK_Y, BLOCK_Z)[s - 1] - 1
     part = lane_part(mid[s], s)
     high = []
@@ -603,13 +608,13 @@
                     store(flat(base + n + at, inner, n), z[a * inner : (a + 1) * inner])
 
 
-def early_kernel(own_face, own_in, got_in, place, *, n):
+def early_kernel(own_x, own_face, own_in, got_in, place, *, n):
     size = place.shape[1]
     groups = size // LANES
     pad = rows_padded(n)
     inner = n - 2
 
-    def body(of, oi, gi, place_ref, out_s, matrix_ref):
+    def body(ox, of, oi, gi, place_ref, out_s, matrix_ref):
         matrix = one_hot(place_ref[...])
         matrix = jnp.concatenate([matrix, matrix], axis=0)
         matrix_ref[...] = matrix
@@ -618,7 +623,7 @@
             out_s[rows, :] = value
 
         for s in range(3):
-            to_elements(of, matrix, s, n, groups, pad, store)
+            to_elements(of if s else ox, matrix, s, n, groups, pad, store)
         for a in range(inner):
             for b in range(inner):
                 for k in range(groups):
@@ -634,64 +639,103 @@
         ],
         compiler_params=vmem_params(),
         name="early",
-    )(own_face, own_in, got_in, place)
-
-
-def final_kernel(early, matrix, got_face, *, n):
+    )(own_x, own_face, own_in, got_in, place)
+
+
+def outer_rows(n, groups):
+    return (n * n * groups + 7) // 8 * 8
+
+
+def middle_kernel(early, matrix, got_face, *, n):
     total = early.shape[0]
     groups = total // (n * n * n)
     pad = rows_padded(n)
-    edge = (n * n * groups + 7) // 8 * 8
+    edge = outer_rows(n, groups)
 
     def body(early_ref, matrix_ref, gf, out_s, out, sem):
         def store(rows, value):
             out_s[rows, :] = out_s[rows, :] + value
 
-        def copy(index, first, count):
-            rows = pl.ds(first, count)
-            return pltpu.make_async_copy(out_s.at[rows, :], out.at[rows, :], sem.at[index])
-
         matrix = matrix_ref[...]
         for s in (1, 2):
             to_elements(gf, matrix, s, n, groups, pad, store)
-        done = [copy(0, edge, total - 2 * edge), copy(1, 0, edge), copy(2, total - edge, edge)]
-        done[0].start()
-        to_elements(gf, matrix, 0, n, groups, pad, store)
-        done[1].start()
-        done[2].start()
+        rows = pl.ds(edge, total - 2 * edge)
+        done = pltpu.make_async_copy(out_s.at[rows, :], out.at[rows, :], sem)
+        done.start()
+        done.wait()
+
+    return pl.pallas_call(
+        body,
+        out_shape=whole(early.shape, early.shape),
+        out_specs=[pl.BlockSpec(memory_space=pltpu.VMEM), pl.BlockSpec(memory_space=pltpu.HBM)],
+        scratch_shapes=[pltpu.SemaphoreType.DMA],
+        input_output_aliases={0: 0},
+        compiler_params=vmem_params(),
+        name="middle",
+    )(early, matrix, got_face)
+
+
+def final_kernel(early, result, matrix, got_x, *, n):
+    total = early.shape[0]
+    groups = total // (n * n * n)
+    pad = rows_padded(n)
+    edge = outer_rows(n, groups)
+
+    def body(early_ref, result_ref, matrix_ref, gx, out, ends, sem):
+        far = total - edge
+        ends[0:edge, :] = early_ref[0:edge, :]
+        ends[edge : 2 * edge, :] = early_ref[far:total, :]
+
+        def store(rows, value):
+            start = rows.start if rows.start < edge else rows.start - far + edge
+            here = pl.ds(start, rows.size, stride=rows.stride)
+            ends[here, :] = ends[here, :] + value
+
+        to_elements(gx, matrix_ref[...], 0, n, groups, pad, store)
+        done = [
+            pltpu.make_async_copy(ends.at[pl.ds(i * edge, edge), :], out.at[pl.ds(i * far, edge), :], sem.at[i])
+            for i in range(2)
+        ]
+        for c in done:
+            c.start()
         for c in done:
             c.wait()
 
     return pl.pallas_call(
         body,
-        out_shape=whole(early.shape, early.shape),
-        out_specs=[pl.BlockSpec(memory_space=pltpu.VMEM), pl.BlockSpec(memory_space=pltpu.HBM)],
-        scratch_shapes=[pltpu.SemaphoreType.DMA((3,))],
-        input_output_aliases={0: 0},
+        out_shape=whole(early.shape)[0],
+        in_specs=[
+            pl.BlockSpec(memory_space=pltpu.VMEM),
+            pl.BlockSpec(memory_space=pltpu.HBM),
+            pl.BlockSpec(memory_space=pltpu.VMEM),
+            pl.BlockSpec(memory_space=pltpu.VMEM),
+        ],
+        out_specs=pl.BlockSpec(memory_space=pltpu.HBM),
+        scratch_shapes=[pltpu.VMEM((2 * edge, LANES), jnp.float32), pltpu.SemaphoreType.DMA((2,))],
+        input_output_aliases={1: 0},
         compiler_params=vmem_params(),
         name="final",
-    )(early, matrix, got_face)[1]
+    )(early, result, matrix, got_x)
 
 
 def pairing(at, extent, odd):
-    other = at + (1 if at % 2 == (1 if odd else 0) else -1)
-    return other if 0 <= other < extent else None
-
-
-def neighbour_pairs(count, x_odd, y_odd):
-    extent = count // GRID_Y
+    return (at + (1 if at % 2 == (1 if odd else 0) else -1)) % extent
+
+
+def neighbour_pairs(count, along_x, odd):
+    extent = count // GRID_Y if along_x else GRID_Y
+    if extent == 1 or (odd and extent == 2):
+        return []
     pairs = []
     for e in range(count):
         sx, sy = divmod(e, GRID_Y)
-        tx = sx if x_odd is None else pairing(sx, extent, x_odd)
-        ty = sy if y_odd is None else pairing(sy, GRID_Y, y_odd)
-        if tx is not None and ty is not None:
-            pairs.append((e, tx * GRID_Y + ty))
+        to = pairing(sx, extent, odd) * GRID_Y + sy if along_x else sx * GRID_Y + pairing(sy, extent, odd)
+        pairs.append((e, to))
     return pairs
 
 
-def exchange(value, x_odd, y_odd):
-    pairs = neighbour_pairs(lax.axis_size("elem"), x_odd, y_odd)
+def exchange(value, along_x, odd):
+    pairs = neighbour_pairs(lax.axis_size("elem"), along_x, odd)
     return lax.ppermute(value, "elem", pairs) if pairs else jnp.zeros_like(value)
 
 
@@ -705,18 +749,20 @@
     got_in = lax.ppermute(send_in, "comp", swap)
     halves = velocity.shape[4]
     even, odd = edge_kernel(part, element_place, other_place, n=n, halves=halves)
-    even = exchange(even, False, None)
-    odd = exchange(odd, True, None)
+    even = exchange(even, True, False)
+    odd = exchange(odd, True, True)
     faces, own_in = place_kernel(part, element_place, other_place, n=n, halves=halves)
     faces, even, odd = x_kernel(faces, even, odd, n=n)
-    odd = exchange(odd, None, True)
-    even = exchange(even, None, False)
+    odd = exchange(odd, False, True)
+    even = exchange(even, False, False)
     faces, out = y_kernel(faces, even, odd, n=n)
     got = lax.ppermute(out, "rep", swap)
-    own_face, send_face = z_kernel(faces, got, n=n)
+    own_x, own_face, send_x, send_face = z_kernel(faces, got, n=n)
     got_face = lax.ppermute(send_face, "comp", swap)
-    early, matrix = early_kernel(own_face, own_in, got_in, element_place, n=n)
-    result = final_kernel(early, matrix, got_face, n=n)
+    got_x = lax.ppermute(send_x, "comp", swap)
+    early, matrix = early_kernel(own_x, own_face, own_in, got_in, element_place, n=n)
+    early, result = middle_kernel(early, matrix, got_face, n=n)
+    result = final_kernel(early, result, matrix, got_x, n=n)
     return result.reshape(n, n, n, 1, element_place.shape[1])
 
 

time: 59.8 us -> 58.3 us (0.975)
  the two profiles are of different devices: /device:TPU:26 before, /device:TPU:0 now
where the time goes in v4:
time: 58.3 us; the launch traced here: 58.2 us
  waiting for transfers between devices  30.3 us (52%)
  Pallas kernels  16.5 us (28%)
  starting transfers between devices  11.3 us (19%)
    ppermute x1, waiting for transfers between devices, body(): other_place = lax.ppermute(element_place, 'comp', swap)  17.5 us
    pallas_call x1, Pallas kernels, flux_kernel(): pl.pallas_call(body, in_specs=[pl.BlockSpec(memory_space=pltpu.HBM), pl.B...  7.96 us
    ppermute x1, waiting for transfers between devices, body(): got_face = lax.ppermute(send_face, 'comp', swap)  6.3 us
    ppermute x3, starting transfers between devices, exchange(): lax.ppermute(value, 'elem', pairs)  5.98 us
    ppermute x3, waiting for transfers between devices, exchange(): lax.ppermute(value, 'elem', pairs)  3.51 us
    ppermute x1, starting transfers between devices, body(): got_in = lax.ppermute(send_in, 'comp', swap)  3.04 us
    pallas_call x1, Pallas kernels, place_kernel(): pl.pallas_call(body, out_shape=whole(shape, (inner * inner * inner * grou...  2.38 us
    ppermute x1, waiting for transfers between devices, body(): got_x = lax.ppermute(send_x, 'comp', swap)  1.66 us
  transfers between devices with their start and end apart: 8, of which 6 were waited for; matrix products, arithmetic and copies ran while one was open for 0% of the time, Pallas kernels for 13%

profile of v4, /device:TPU:0, one launch (start us, length us, event | category | flops | bytes accessed | tf_op | source)
XLA Modules:
  0.0 58.2 jit_solution(15958930509128036177)
XLA Ops:
  0.0 8.0 %flux.1 = (f32[1536,128]{1,0:T(8,128)S(1)}, f32[8000,128]{1,0:T(8,128)S(1)}) custom-call(f32[3,5,10,10,2,384]{5,4,3,2,1,0:T(2,128)} %v_hbm.1, f32[3,3,5,10,10,2,384]{6,5,4,3,2,1,0:T(2,128)} %g_hbm.1), custom_call_target="tpu_custom_call" | custom-call | tf_op jit(solution)/shard_map/flux/pallas_call | solution.py:168
  8.0 3.0 %collective-permute-start.5 = (f32[1536,128]{1,0:T(8,128)S(1)}, f32[1536,128]{1,0:T(8,128)S(1)}, u32[]{:S(2)}, u32[]{:S(2)}) collective-permute-start(f32[1536,128]{1,0:T(8,128)S(1)} %get-tuple-element.34), channel_id=1, source_target_pairs={{0,2},{2,0},{1,3},{3,1},{4,6},{6,4},{5,7},{7,5},{8,10},{10,8},{9,1... | collective-permute-start | bytes 2359304 | tf_op jit(solution)/shard_map/ppermute | solution.py:749
  11.0 0.1 collective-permute-start
  11.1 17.5 %collective-permute-done.other_ref = s32[1,384]{1,0:T(1,128)S(1)} collective-permute-done((s32[1,384]{1,0:T(1,128)S(1)}, s32[1,384]{1,0:T(1,128)S(1)}, u32[]{:S(2)}, u32[]{:S(2)}) %collective-permute-start) | collective-permute-done | bytes 1568 | tf_op jit(solution)/shard_map/ppermute | solution.py:745
  28.6 1.0 %edge.1 = (f32[104,128]{1,0:T(8,128)S(1)}, f32[104,128]{1,0:T(8,128)}) custom-call(f32[8000,128]{1,0:T(8,128)S(1)} %get-tuple-element.23.part_ref, s32[1,384]{1,0:T(1,128)S(1)} %copy-done, s32[1,384]{1,0:T(1,128)S(1)} %collective-permute-done.other_ref), custom_call_target="tpu_custom_call" | custom-call | tf_op jit(solution)/shard_map/edge/pallas_call | solution.py:364
  29.7 2.8 %collective-permute-start.1 = (f32[104,128]{1,0:T(8,128)S(1)}, f32[104,128]{1,0:T(8,128)S(1)}, u32[]{:S(2)}, u32[]{:S(2)}) collective-permute-start(f32[104,128]{1,0:T(8,128)S(1)} %get-tuple-element.25), channel_id=1, source_target_pairs={{0,16},{4,20},{8,24},{12,28},{16,0},{20,4},{24,8},{28,12},{1,17},{... | collective-permute-start | bytes 159752 | tf_op jit(solution)/shard_map/ppermute | solution.py:739
  32.5 2.4 %place.1 = (f32[2,6,3,104,128]{4,3,2,1,0:T(8,128)S(1)}, f32[1536,128]{1,0:T(8,128)S(1)}) custom-call(f32[8000,128]{1,0:T(8,128)S(1)} %get-tuple-element.23.part_ref, s32[1,384]{1,0:T(1,128)S(1)} %copy-done, s32[1,384]{1,0:T(1,128)S(1)} %collective-permute-done.other_ref), custom_call_target="tpu_custom_call" | custom-call | tf_op jit(solution)/shard_map/place/pallas_call | solution.py:406
  34.9 0.3 add_x.1
  35.2 1.6 %collective-permute-start.2 = (f32[104,128]{1,0:T(8,128)S(1)}, f32[104,128]{1,0:T(8,128)S(1)}, u32[]{:S(2)}, u32[]{:S(2)}) collective-permute-start(f32[104,128]{1,0:T(8,128)S(1)} %get-tuple-element.27), channel_id=1, source_target_pairs={{0,4},{4,0},{8,12},{12,8},{16,20},{20,16},{24,28},{28,24},{1,5},{5... | collective-permute-start | bytes 159752 | tf_op jit(solution)/shard_map/ppermute | solution.py:739
  36.8 1.5 %collective-permute-start.3 = (f32[104,128]{1,0:T(8,128)S(1)}, f32[104,128]{1,0:T(8,128)S(1)}, u32[]{:S(2)}, u32[]{:S(2)}) collective-permute-start(f32[104,128]{1,0:T(8,128)S(1)} %get-tuple-element.28), channel_id=1, source_target_pairs={{0,12},{4,8},{8,4},{12,0},{16,28},{20,24},{24,20},{28,16},{1,13},{... | collective-permute-start | bytes 159752 | tf_op jit(solution)/shard_map/ppermute | solution.py:739
  38.3 1.5 %collective-permute-done.2.even_ref = f32[104,128]{1,0:T(8,128)S(1)} collective-permute-done((f32[104,128]{1,0:T(8,128)S(1)}, f32[104,128]{1,0:T(8,128)S(1)}, u32[]{:S(2)}, u32[]{:S(2)}) %collective-permute-start.2) | collective-permute-done | bytes 53280 | tf_op jit(solution)/shard_map/ppermute | solution.py:739
  39.8 2.0 %collective-permute-done.3.odd_ref = f32[104,128]{1,0:T(8,128)S(1)} collective-permute-done((f32[104,128]{1,0:T(8,128)S(1)}, f32[104,128]{1,0:T(8,128)S(1)}, u32[]{:S(2)}, u32[]{:S(2)}) %collective-permute-start.3) | collective-permute-done | bytes 53280 | tf_op jit(solution)/shard_map/ppermute | solution.py:739
  41.8 0.7 %add_y.1 = (f32[2,6,3,104,128]{4,3,2,1,0:T(8,128)S(1)}, f32[2,104,128]{2,1,0:T(8,128)S(1)}) custom-call(f32[2,6,3,104,128]{4,3,2,1,0:T(8,128)S(1)} %get-tuple-element.26.faces_ref, f32[104,128]{1,0:T(8,128)S(1)} %collective-permute-done.2.even_ref, f32[104,128]{1,0:T(8,128)S(1)} %collective-permute-done.3.odd_ref), custom_call_target="tpu_custom_call", output_to_operand_aliasing={{0}: (0, {})} | custom-call | tf_op jit(solution)/shard_map/add_y/pallas_call | solution.py:483
  42.5 0.1 collective-permute-start.4
  42.6 1.3 %collective-permute-done.4.got_ref = f32[2,104,128]{2,1,0:T(8,128)S(1)} collective-permute-done((f32[2,104,128]{2,1,0:T(8,128)S(1)}, f32[2,104,128]{2,1,0:T(8,128)S(1)}, u32[]{:S(2)}, u32[]{:S(2)}) %collective-permute-start.4) | collective-permute-done | bytes 106528 | tf_op jit(solution)/shard_map/ppermute | solution.py:759
  43.9 0.8 %add_z.1 = (f32[2,6,3,104,128]{4,3,2,1,0:T(8,128)S(1)}, f32[368,128]{1,0:T(8,128)S(1)}, f32[504,128]{1,0:T(8,128)S(1)}, f32[368,128]{1,0:T(8,128)S(1)}, f32[504,128]{1,0:T(8,128)S(1)}) custom-call(f32[2,6,3,104,128]{4,3,2,1,0:T(8,128)S(1)} %get-tuple-element.29.faces_ref, ...), custom_call_target="tpu_custom_call", output_to_operand_aliasing={{0}: (0, {})} | custom-call | tf_op jit(solution)/shard_map/add_z/pallas_call | solution.py:557
  44.7 1.6 %collective-permute-start.6 = (f32[504,128]{1,0:T(8,128)S(1)}, f32[504,128]{1,0:T(8,128)S(1)}, u32[]{:S(2)}, u32[]{:S(2)}) collective-permute-start(f32[504,128]{1,0:T(8,128)S(1)} %get-tuple-element.37), channel_id=1, source_target_pairs={{0,2},{2,0},{1,3},{3,1},{4,6},{6,4},{5,7},{7,5},{8,10},{10,8},{9,1... | collective-permute-start | bytes 774152 | tf_op jit(solution)/shard_map/ppermute | solution.py:761
  46.3 0.5 collective-permute-start.7
  46.8 0.0 collective-permute-done.5.gi
  46.8 0.8 %early.1 = (f32[3000,128]{1,0:T(8,128)S(1)}, bf16[768,384]{1,0:T(8,128)(2,1)S(1)}) custom-call(f32[368,128]{1,0:T(8,128)S(1)} %get-tuple-element.31.ox, f32[504,128]{1,0:T(8,128)S(1)} %get-tuple-element.32.of, f32[1536,128]{1,0:T(8,128)S(1)} %get-tuple-element.33.oi, f32[1536,128]{1,0:T(8,128)S(1)} %collective-permute-done.5.gi, s32[1,384]{1,0:T(1,128)S(1)} %copy-done), custom_call_target="tpu_custom_call" | custom-call | tf_op jit(solution)/shard_map/early/pallas_call | solution.py:634
  47.6 6.3 %collective-permute-done.6.gf = f32[504,128]{1,0:T(8,128)S(1)} collective-permute-done((f32[504,128]{1,0:T(8,128)S(1)}, f32[504,128]{1,0:T(8,128)S(1)}, u32[]{:S(2)}, u32[]{:S(2)}) %collective-permute-start.6) | collective-permute-done | bytes 258080 | tf_op jit(solution)/shard_map/ppermute | solution.py:761
  53.8 1.5 %middle.1 = (f32[3000,128]{1,0:T(8,128)S(1)}, f32[3000,128]{1,0:T(8,128)}) custom-call(f32[3000,128]{1,0:T(8,128)S(1)} %get-tuple-element.35.early_ref, bf16[768,384]{1,0:T(8,128)(2,1)S(1)} %get-tuple-element.36.matrix_ref, f32[504,128]{1,0:T(8,128)S(1)} %collective-permute-done.6.gf), custom_call_target="tpu_custom_call", output_to_operand_aliasing={{0}: (0, {})} | custom-call | tf_op jit(solution)/shard_map/middle/pallas_call | solution.py:667
  55.4 1.7 %collective-permute-done.7.gx = f32[368,128]{1,0:T(8,128)S(1)} collective-permute-done((f32[368,128]{1,0:T(8,128)S(1)}, f32[368,128]{1,0:T(8,128)S(1)}, u32[]{:S(2)}, u32[]{:S(2)}) %collective-permute-start.7) | collective-permute-done | bytes 188448 | tf_op jit(solution)/shard_map/ppermute | solution.py:762
  57.1 1.1 %final.1 = f32[3000,128]{1,0:T(8,128)} custom-call(f32[3000,128]{1,0:T(8,128)S(1)} %get-tuple-element.38.early_ref, f32[3000,128]{1,0:T(8,128)} %get-tuple-element.39.result_ref, bf16[768,384]{1,0:T(8,128)(2,1)S(1)} %get-tuple-element.36.matrix_ref, f32[368,128]{1,0:T(8,128)S(1)} %collective-permute-done.7.gx), custom_call_target="tpu_custom_call", output_to_operand_aliasing={{}: (1, {})} | custom-call | tf_op jit(solution)/shard_map/final/pallas_call | solution.py:704
  (4 shorter events, 0.0 us)
Async XLA Ops:
  0.0 11.0 %copy-start = (s32[1,384]{1,0:T(1,128)S(1)}, s32[1,384]{1,0:T(1,128)}, u32[]{:S(2)}) copy-start(s32[1,384]{1,0:T(1,128)} %place_ref.1) | copy-start | bytes 4612
  8.0 38.8 %collective-permute-start.5 = (f32[1536,128]{1,0:T(8,128)S(1)}, f32[1536,128]{1,0:T(8,128)S(1)}, u32[]{:S(2)}, u32[]{:S(2)}) collective-permute-start(f32[1536,128]{1,0:T(8,128)S(1)} %get-tuple-element.34), channel_id=1, source_target_pairs={{0,2},{2,0},{1,3},{3,1},{4,6},{6,4},{5,7},{7,5},{8,10},{10,8},{9,1... | collective-permute-start | bytes 2359304 | tf_op jit(solution)/shard_map/ppermute | solution.py:749
  11.0 17.6 %collective-permute-start = (s32[1,384]{1,0:T(1,128)S(1)}, s32[1,384]{1,0:T(1,128)S(1)}, u32[]{:S(2)}, u32[]{:S(2)}) collective-permute-start(s32[1,384]{1,0:T(1,128)S(1)} %copy-done), channel_id=1, source_target_pairs={{0,2},{2,0},{1,3},{3,1},{4,6},{6,4},{5,7},{7,5},{8,10},{10,8},{9,1... | collective-permute-start | bytes 4616 | tf_op jit(solution)/shard_map/ppermute | solution.py:745
  29.7 5.2 %collective-permute-start.1 = (f32[104,128]{1,0:T(8,128)S(1)}, f32[104,128]{1,0:T(8,128)S(1)}, u32[]{:S(2)}, u32[]{:S(2)}) collective-permute-start(f32[104,128]{1,0:T(8,128)S(1)} %get-tuple-element.25), channel_id=1, source_target_pairs={{0,16},{4,20},{8,24},{12,28},{16,0},{20,4},{24,8},{28,12},{1,17},{... | collective-permute-start | bytes 159752 | tf_op jit(solution)/shard_map/ppermute | solution.py:739
  35.2 4.6 %collective-permute-start.2 = (f32[104,128]{1,0:T(8,128)S(1)}, f32[104,128]{1,0:T(8,128)S(1)}, u32[]{:S(2)}, u32[]{:S(2)}) collective-permute-start(f32[104,128]{1,0:T(8,128)S(1)} %get-tuple-element.27), channel_id=1, source_target_pairs={{0,4},{4,0},{8,12},{12,8},{16,20},{20,16},{24,28},{28,24},{1,5},{5... | collective-permute-start | bytes 159752 | tf_op jit(solution)/shard_map/ppermute | solution.py:739
  36.8 5.0 %collective-permute-start.3 = (f32[104,128]{1,0:T(8,128)S(1)}, f32[104,128]{1,0:T(8,128)S(1)}, u32[]{:S(2)}, u32[]{:S(2)}) collective-permute-start(f32[104,128]{1,0:T(8,128)S(1)} %get-tuple-element.28), channel_id=1, source_target_pairs={{0,12},{4,8},{8,4},{12,0},{16,28},{20,24},{24,20},{28,16},{1,13},{... | collective-permute-start | bytes 159752 | tf_op jit(solution)/shard_map/ppermute | solution.py:739
  42.5 1.4 %collective-permute-start.4 = (f32[2,104,128]{2,1,0:T(8,128)S(1)}, f32[2,104,128]{2,1,0:T(8,128)S(1)}, u32[]{:S(2)}, u32[]{:S(2)}) collective-permute-start(f32[2,104,128]{2,1,0:T(8,128)S(1)} %get-tuple-element.30), channel_id=1, source_target_pairs={{0,1},{1,0},{2,3},{3,2},{4,5},{5,4},{6,7},{7,6},{8,9},{9,8},{10,11... | collective-permute-start | bytes 319496 | tf_op jit(solution)/shard_map/ppermute | solution.py:759
  44.7 9.2 %collective-permute-start.6 = (f32[504,128]{1,0:T(8,128)S(1)}, f32[504,128]{1,0:T(8,128)S(1)}, u32[]{:S(2)}, u32[]{:S(2)}) collective-permute-start(f32[504,128]{1,0:T(8,128)S(1)} %get-tuple-element.37), channel_id=1, source_target_pairs={{0,2},{2,0},{1,3},{3,1},{4,6},{6,4},{5,7},{7,5},{8,10},{10,8},{9,1... | collective-permute-start | bytes 774152 | tf_op jit(solution)/shard_map/ppermute | solution.py:761
  46.3 10.8 %collective-permute-start.7 = (f32[368,128]{1,0:T(8,128)S(1)}, f32[368,128]{1,0:T(8,128)S(1)}, u32[]{:S(2)}, u32[]{:S(2)}) collective-permute-start(f32[368,128]{1,0:T(8,128)S(1)} %get-tuple-element.40), channel_id=1, source_target_pairs={{0,2},{2,0},{1,3},{3,1},{4,6},{6,4},{5,7},{7,5},{8,10},{10,8},{9,1... | collective-permute-start | bytes 565256 | tf_op jit(solution)/shard_map/ppermute | solution.py:762

commit v5 on v4

--- a/solution.py
+++ b/solution.py
@@ -70,6 +70,15 @@
     return (node_count * node_count + 7) // 8 * 8
 
 
+def in_pairs(start, count, step):
+    def pair(i, carry):
+        step(start + 2 * i)
+        step(start + 2 * i + 1)
+        return carry
+
+    lax.fori_loop(0, count // 2, pair, 0)
+
+
 def plane_at(plane, comp, n):
     return jnp.where(comp == 0, plane, (plane + n // 2) % n) * (n * n * 8)
 
@@ -81,10 +90,12 @@
     halves = velocity.shape[4]
     table = derivative_table(n)
     inner = n - 2
-    blocks = [(plane, 0, n) for plane in range(planes - 1)]
-    blocks += [(planes - 1, 0, n // 2), (planes - 1, n // 2, n - n // 2)]
-
-    def body(v_hbm, g_hbm, send, part, v, g, f0, f1, st, sem):
+    cut = n // 4 * 2
+    blocks = [(0, 0, cut), (0, cut, n - cut)]
+    blocks += [(plane, 0, n) for plane in range(1, planes - 1)]
+    blocks += [(planes - 1, 0, n - 2), (planes - 1, n - 2, 2)]
+
+    def body(v_hbm, g_hbm, send, part, v, g, f1, sem):
         comp = lax.axis_index("comp")
         first = comp == 0
 
@@ -117,51 +128,48 @@
             return pl.ds(pl.multiple_of((m * n * n + b * n + c) * 8, 8), 8)
 
         for index, (plane, start, count) in enumerate(blocks):
+            coef = [
+                jnp.where(first, float(table[plane, m]), float(table[planes + plane, (m + planes) % n]))
+                for m in range(n)
+            ]
             for c in copies(index):
                 c.wait()
 
-            def along_last(b, carry):
+            def along_ends(b):
                 line = []
+                rows = []
                 for c in range(n):
                     vel = [v[plane, i, b, c] for i in range(3)]
                     flux = [
                         weighted([(g[plane, i, j, b, c], vel[i]) for i in range(3)]) for j in range(3)
                     ]
-                    f0[b, c] = flux[0]
                     f1[b, c] = flux[1]
                     line.append(flux[2])
+                    rows.append([flux[0] * coef[m] for m in range(n)])
                 out = transpose_line(line, table)
                 for c in range(n):
-                    st[b, c] = out[c]
-                return carry
-
-            lax.fori_loop(start, start + count, along_last, 0)
+                    for m in range(n):
+                        value = rows[c][m] + out[c] if m == plane else rows[c][m]
+                        row = row_of(m, b, c)
+                        part[row, :] = value if plane == 0 else part[row, :] + value
+
+            in_pairs(start, count, along_ends)
             if start + count < n:
                 continue
-            coef = [
-                jnp.where(first, float(table[plane, m]), float(table[planes + plane, (m + planes) % n]))
-                for m in range(n)
-            ]
-
-            def along_others(c, carry):
+
+            def along_middle(c):
                 out = transpose_line([f1[b, c] for b in range(n)], table)
                 for b in range(n):
-                    flux = f0[b, c]
-                    for m in range(n):
-                        value = flux * coef[m]
-                        if m == plane:
-                            value = value + (st[b, c] + out[b])
-                        row = row_of(m, b, c)
-                        part[row, :] = value if plane == 0 else part[row, :] + value
-                return carry
-
-            lax.fori_loop(0, n, along_others, 0)
+                    row = row_of(plane, b, c)
+                    part[row, :] = part[row, :] + out[b]
+
+            in_pairs(0, n, along_middle)
         for a in range(inner):
+            base = plane_at(a + 1, comp, n) + 1 - comp
             for b in range(inner):
                 for k in range(groups):
-                    base = plane_at(a + 1, comp, n) + ((b + 1) * n + 1) * 8 + k * halves
                     send[pl.ds(((a * inner + b) * groups + k) * inner, inner), :] = part[
-                        pl.ds(base + 1 - comp, inner, stride=8), :
+                        pl.ds(base + (((b + 1) * n + 1) * 8 + k * halves), inner, stride=8), :
                     ]
 
     tile = (8, LANES)
@@ -173,9 +181,7 @@
             pltpu.VMEM((planes, 3, n, n) + tile, jnp.float32),
             pltpu.VMEM((planes, 3, 3, n, n) + tile, jnp.float32),
             pltpu.VMEM((n, n) + tile, jnp.float32),
-            pltpu.VMEM((n, n) + tile, jnp.float32),
-            pltpu.VMEM((n, n) + tile, jnp.float32),
-            pltpu.SemaphoreType.DMA((2 * groups, planes + 1)),
+            pltpu.SemaphoreType.DMA((2 * groups, planes + 2)),
         ],
         compiler_params=pltpu.CompilerParams(vmem_limit_bytes=42 * 2**20),
         name="flux",

time: 58.3 us -> 58 us (level)
  no operation moved by 1% of the time
where the time goes in v5:
time: 58 us; the launch traced here: 57.9 us
  waiting for transfers between devices  30.3 us (52%)
  Pallas kernels  16.2 us (28%)
  starting transfers between devices  11.3 us (19%)
    ppermute x1, waiting for transfers between devices, body(): other_place = lax.ppermute(element_place, 'comp', swap)  17.5 us
    pallas_call x1, Pallas kernels, flux_kernel(): pl.pallas_call(body, in_specs=[pl.BlockSpec(memory_space=pltpu.HBM), pl.B...  7.67 us
    ppermute x1, waiting for transfers between devices, body(): got_face = lax.ppermute(send_face, 'comp', swap)  6.3 us
    ppermute x3, starting transfers between devices, exchange(): lax.ppermute(value, 'elem', pairs)  5.97 us
    ppermute x3, waiting for transfers between devices, exchange(): lax.ppermute(value, 'elem', pairs)  3.52 us
    ppermute x1, starting transfers between devices, body(): got_in = lax.ppermute(send_in, 'comp', swap)  3.04 us
    pallas_call x1, Pallas kernels, place_kernel(): pl.pallas_call(body, out_shape=whole(shape, (inner * inner * inner * grou...  2.38 us
    ppermute x1, waiting for transfers between devices, body(): got_x = lax.ppermute(send_x, 'comp', swap)  1.66 us
  transfers between devices with their start and end apart: 8, of which 6 were waited for; matrix products, arithmetic and copies ran while one was open for 0% of the time, Pallas kernels for 13%

profile of v5, /device:TPU:0, one launch (start us, length us, event | category | flops | bytes accessed | tf_op | source)
XLA Modules:
  0.0 57.9 jit_solution(15270475800292736629)
XLA Ops:
  0.0 7.7 %flux.1 = (f32[1536,128]{1,0:T(8,128)S(1)}, f32[8000,128]{1,0:T(8,128)S(1)}) custom-call(f32[3,5,10,10,2,384]{5,4,3,2,1,0:T(2,128)} %v_hbm.1, f32[3,3,5,10,10,2,384]{6,5,4,3,2,1,0:T(2,128)} %g_hbm.1), custom_call_target="tpu_custom_call" | custom-call | tf_op jit(solution)/shard_map/flux/pallas_call | solution.py:176
  7.7 3.0 %collective-permute-start.5 = (f32[1536,128]{1,0:T(8,128)S(1)}, f32[1536,128]{1,0:T(8,128)S(1)}, u32[]{:S(2)}, u32[]{:S(2)}) collective-permute-start(f32[1536,128]{1,0:T(8,128)S(1)} %get-tuple-element.34), channel_id=1, source_target_pairs={{0,2},{2,0},{1,3},{3,1},{4,6},{6,4},{5,7},{7,5},{8,10},{10,8},{9,1... | collective-permute-start | bytes 2359304 | tf_op jit(solution)/shard_map/ppermute | solution.py:755
  10.7 0.1 collective-permute-start
  10.8 17.5 %collective-permute-done.other_ref = s32[1,384]{1,0:T(1,128)S(1)} collective-permute-done((s32[1,384]{1,0:T(1,128)S(1)}, s32[1,384]{1,0:T(1,128)S(1)}, u32[]{:S(2)}, u32[]{:S(2)}) %collective-permute-start) | collective-permute-done | bytes 1568 | tf_op jit(solution)/shard_map/ppermute | solution.py:751
  28.3 1.0 %edge.1 = (f32[104,128]{1,0:T(8,128)S(1)}, f32[104,128]{1,0:T(8,128)}) custom-call(f32[8000,128]{1,0:T(8,128)S(1)} %get-tuple-element.23.part_ref, s32[1,384]{1,0:T(1,128)S(1)} %copy-done, s32[1,384]{1,0:T(1,128)S(1)} %collective-permute-done.other_ref), custom_call_target="tpu_custom_call" | custom-call | tf_op jit(solution)/shard_map/edge/pallas_call | solution.py:370
  29.4 2.8 %collective-permute-start.1 = (f32[104,128]{1,0:T(8,128)S(1)}, f32[104,128]{1,0:T(8,128)S(1)}, u32[]{:S(2)}, u32[]{:S(2)}) collective-permute-start(f32[104,128]{1,0:T(8,128)S(1)} %get-tuple-element.25), channel_id=1, source_target_pairs={{0,16},{4,20},{8,24},{12,28},{16,0},{20,4},{24,8},{28,12},{1,17},{... | collective-permute-start | bytes 159752 | tf_op jit(solution)/shard_map/ppermute | solution.py:745
  32.2 2.4 %place.1 = (f32[2,6,3,104,128]{4,3,2,1,0:T(8,128)S(1)}, f32[1536,128]{1,0:T(8,128)S(1)}) custom-call(f32[8000,128]{1,0:T(8,128)S(1)} %get-tuple-element.23.part_ref, s32[1,384]{1,0:T(1,128)S(1)} %copy-done, s32[1,384]{1,0:T(1,128)S(1)} %collective-permute-done.other_ref), custom_call_target="tpu_custom_call" | custom-call | tf_op jit(solution)/shard_map/place/pallas_call | solution.py:412
  34.6 0.3 add_x.1
  34.9 1.6 %collective-permute-start.2 = (f32[104,128]{1,0:T(8,128)S(1)}, f32[104,128]{1,0:T(8,128)S(1)}, u32[]{:S(2)}, u32[]{:S(2)}) collective-permute-start(f32[104,128]{1,0:T(8,128)S(1)} %get-tuple-element.27), channel_id=1, source_target_pairs={{0,4},{4,0},{8,12},{12,8},{16,20},{20,16},{24,28},{28,24},{1,5},{5... | collective-permute-start | bytes 159752 | tf_op jit(solution)/shard_map/ppermute | solution.py:745
  36.5 1.5 %collective-permute-start.3 = (f32[104,128]{1,0:T(8,128)S(1)}, f32[104,128]{1,0:T(8,128)S(1)}, u32[]{:S(2)}, u32[]{:S(2)}) collective-permute-start(f32[104,128]{1,0:T(8,128)S(1)} %get-tuple-element.28), channel_id=1, source_target_pairs={{0,12},{4,8},{8,4},{12,0},{16,28},{20,24},{24,20},{28,16},{1,13},{... | collective-permute-start | bytes 159752 | tf_op jit(solution)/shard_map/ppermute | solution.py:745
  38.0 1.5 %collective-permute-done.2.even_ref = f32[104,128]{1,0:T(8,128)S(1)} collective-permute-done((f32[104,128]{1,0:T(8,128)S(1)}, f32[104,128]{1,0:T(8,128)S(1)}, u32[]{:S(2)}, u32[]{:S(2)}) %collective-permute-start.2) | collective-permute-done | bytes 53280 | tf_op jit(solution)/shard_map/ppermute | solution.py:745
  39.5 2.0 %collective-permute-done.3.odd_ref = f32[104,128]{1,0:T(8,128)S(1)} collective-permute-done((f32[104,128]{1,0:T(8,128)S(1)}, f32[104,128]{1,0:T(8,128)S(1)}, u32[]{:S(2)}, u32[]{:S(2)}) %collective-permute-start.3) | collective-permute-done | bytes 53280 | tf_op jit(solution)/shard_map/ppermute | solution.py:745
  41.6 0.7 %add_y.1 = (f32[2,6,3,104,128]{4,3,2,1,0:T(8,128)S(1)}, f32[2,104,128]{2,1,0:T(8,128)S(1)}) custom-call(f32[2,6,3,104,128]{4,3,2,1,0:T(8,128)S(1)} %get-tuple-element.26.faces_ref, f32[104,128]{1,0:T(8,128)S(1)} %collective-permute-done.2.even_ref, f32[104,128]{1,0:T(8,128)S(1)} %collective-permute-done.3.odd_ref), custom_call_target="tpu_custom_call", output_to_operand_aliasing={{0}: (0, {})} | custom-call | tf_op jit(solution)/shard_map/add_y/pallas_call | solution.py:489
  42.2 0.1 collective-permute-start.4
  42.3 1.3 %collective-permute-done.4.got_ref = f32[2,104,128]{2,1,0:T(8,128)S(1)} collective-permute-done((f32[2,104,128]{2,1,0:T(8,128)S(1)}, f32[2,104,128]{2,1,0:T(8,128)S(1)}, u32[]{:S(2)}, u32[]{:S(2)}) %collective-permute-start.4) | collective-permute-done | bytes 106528 | tf_op jit(solution)/shard_map/ppermute | solution.py:765
  43.6 0.8 %add_z.1 = (f32[2,6,3,104,128]{4,3,2,1,0:T(8,128)S(1)}, f32[368,128]{1,0:T(8,128)S(1)}, f32[504,128]{1,0:T(8,128)S(1)}, f32[368,128]{1,0:T(8,128)S(1)}, f32[504,128]{1,0:T(8,128)S(1)}) custom-call(f32[2,6,3,104,128]{4,3,2,1,0:T(8,128)S(1)} %get-tuple-element.29.faces_ref, ...), custom_call_target="tpu_custom_call", output_to_operand_aliasing={{0}: (0, {})} | custom-call | tf_op jit(solution)/shard_map/add_z/pallas_call | solution.py:563
  44.4 1.6 %collective-permute-start.6 = (f32[504,128]{1,0:T(8,128)S(1)}, f32[504,128]{1,0:T(8,128)S(1)}, u32[]{:S(2)}, u32[]{:S(2)}) collective-permute-start(f32[504,128]{1,0:T(8,128)S(1)} %get-tuple-element.37), channel_id=1, source_target_pairs={{0,2},{2,0},{1,3},{3,1},{4,6},{6,4},{5,7},{7,5},{8,10},{10,8},{9,1... | collective-permute-start | bytes 774152 | tf_op jit(solution)/shard_map/ppermute | solution.py:767
  46.0 0.5 collective-permute-start.7
  46.5 0.0 collective-permute-done.5.gi
  46.5 0.8 %early.1 = (f32[3000,128]{1,0:T(8,128)S(1)}, bf16[768,384]{1,0:T(8,128)(2,1)S(1)}) custom-call(f32[368,128]{1,0:T(8,128)S(1)} %get-tuple-element.31.ox, f32[504,128]{1,0:T(8,128)S(1)} %get-tuple-element.32.of, f32[1536,128]{1,0:T(8,128)S(1)} %get-tuple-element.33.oi, f32[1536,128]{1,0:T(8,128)S(1)} %collective-permute-done.5.gi, s32[1,384]{1,0:T(1,128)S(1)} %copy-done), custom_call_target="tpu_custom_call" | custom-call | tf_op jit(solution)/shard_map/early/pallas_call | solution.py:640
  47.3 6.3 %collective-permute-done.6.gf = f32[504,128]{1,0:T(8,128)S(1)} collective-permute-done((f32[504,128]{1,0:T(8,128)S(1)}, f32[504,128]{1,0:T(8,128)S(1)}, u32[]{:S(2)}, u32[]{:S(2)}) %collective-permute-start.6) | collective-permute-done | bytes 258080 | tf_op jit(solution)/shard_map/ppermute | solution.py:767
  53.6 1.6 %middle.1 = (f32[3000,128]{1,0:T(8,128)S(1)}, f32[3000,128]{1,0:T(8,128)}) custom-call(f32[3000,128]{1,0:T(8,128)S(1)} %get-tuple-element.35.early_ref, bf16[768,384]{1,0:T(8,128)(2,1)S(1)} %get-tuple-element.36.matrix_ref, f32[504,128]{1,0:T(8,128)S(1)} %collective-permute-done.6.gf), custom_call_target="tpu_custom_call", output_to_operand_aliasing={{0}: (0, {})} | custom-call | tf_op jit(solution)/shard_map/middle/pallas_call | solution.py:673
  55.1 1.7 %collective-permute-done.7.gx = f32[368,128]{1,0:T(8,128)S(1)} collective-permute-done((f32[368,128]{1,0:T(8,128)S(1)}, f32[368,128]{1,0:T(8,128)S(1)}, u32[]{:S(2)}, u32[]{:S(2)}) %collective-permute-start.7) | collective-permute-done | bytes 188448 | tf_op jit(solution)/shard_map/ppermute | solution.py:768
  56.8 1.1 %final.1 = f32[3000,128]{1,0:T(8,128)} custom-call(f32[3000,128]{1,0:T(8,128)S(1)} %get-tuple-element.38.early_ref, f32[3000,128]{1,0:T(8,128)} %get-tuple-element.39.result_ref, bf16[768,384]{1,0:T(8,128)(2,1)S(1)} %get-tuple-element.36.matrix_ref, f32[368,128]{1,0:T(8,128)S(1)} %collective-permute-done.7.gx), custom_call_target="tpu_custom_call", output_to_operand_aliasing={{}: (1, {})} | custom-call | tf_op jit(solution)/shard_map/final/pallas_call | solution.py:710
  (4 shorter events, 0.0 us)
Async XLA Ops:
  0.0 10.7 %copy-start = (s32[1,384]{1,0:T(1,128)S(1)}, s32[1,384]{1,0:T(1,128)}, u32[]{:S(2)}) copy-start(s32[1,384]{1,0:T(1,128)} %place_ref.1) | copy-start | bytes 4612
  7.7 38.8 %collective-permute-start.5 = (f32[1536,128]{1,0:T(8,128)S(1)}, f32[1536,128]{1,0:T(8,128)S(1)}, u32[]{:S(2)}, u32[]{:S(2)}) collective-permute-start(f32[1536,128]{1,0:T(8,128)S(1)} %get-tuple-element.34), channel_id=1, source_target_pairs={{0,2},{2,0},{1,3},{3,1},{4,6},{6,4},{5,7},{7,5},{8,10},{10,8},{9,1... | collective-permute-start | bytes 2359304 | tf_op jit(solution)/shard_map/ppermute | solution.py:755
  10.7 17.6 %collective-permute-start = (s32[1,384]{1,0:T(1,128)S(1)}, s32[1,384]{1,0:T(1,128)S(1)}, u32[]{:S(2)}, u32[]{:S(2)}) collective-permute-start(s32[1,384]{1,0:T(1,128)S(1)} %copy-done), channel_id=1, source_target_pairs={{0,2},{2,0},{1,3},{3,1},{4,6},{6,4},{5,7},{7,5},{8,10},{10,8},{9,1... | collective-permute-start | bytes 4616 | tf_op jit(solution)/shard_map/ppermute | solution.py:751
  29.4 5.2 %collective-permute-start.1 = (f32[104,128]{1,0:T(8,128)S(1)}, f32[104,128]{1,0:T(8,128)S(1)}, u32[]{:S(2)}, u32[]{:S(2)}) collective-permute-start(f32[104,128]{1,0:T(8,128)S(1)} %get-tuple-element.25), channel_id=1, source_target_pairs={{0,16},{4,20},{8,24},{12,28},{16,0},{20,4},{24,8},{28,12},{1,17},{... | collective-permute-start | bytes 159752 | tf_op jit(solution)/shard_map/ppermute | solution.py:745
  34.9 4.6 %collective-permute-start.2 = (f32[104,128]{1,0:T(8,128)S(1)}, f32[104,128]{1,0:T(8,128)S(1)}, u32[]{:S(2)}, u32[]{:S(2)}) collective-permute-start(f32[104,128]{1,0:T(8,128)S(1)} %get-tuple-element.27), channel_id=1, source_target_pairs={{0,4},{4,0},{8,12},{12,8},{16,20},{20,16},{24,28},{28,24},{1,5},{5... | collective-permute-start | bytes 159752 | tf_op jit(solution)/shard_map/ppermute | solution.py:745
  36.5 5.0 %collective-permute-start.3 = (f32[104,128]{1,0:T(8,128)S(1)}, f32[104,128]{1,0:T(8,128)S(1)}, u32[]{:S(2)}, u32[]{:S(2)}) collective-permute-start(f32[104,128]{1,0:T(8,128)S(1)} %get-tuple-element.28), channel_id=1, source_target_pairs={{0,12},{4,8},{8,4},{12,0},{16,28},{20,24},{24,20},{28,16},{1,13},{... | collective-permute-start | bytes 159752 | tf_op jit(solution)/shard_map/ppermute | solution.py:745
  42.2 1.4 %collective-permute-start.4 = (f32[2,104,128]{2,1,0:T(8,128)S(1)}, f32[2,104,128]{2,1,0:T(8,128)S(1)}, u32[]{:S(2)}, u32[]{:S(2)}) collective-permute-start(f32[2,104,128]{2,1,0:T(8,128)S(1)} %get-tuple-element.30), channel_id=1, source_target_pairs={{0,1},{1,0},{2,3},{3,2},{4,5},{5,4},{6,7},{7,6},{8,9},{9,8},{10,11... | collective-permute-start | bytes 319496 | tf_op jit(solution)/shard_map/ppermute | solution.py:765
  44.4 9.2 %collective-permute-start.6 = (f32[504,128]{1,0:T(8,128)S(1)}, f32[504,128]{1,0:T(8,128)S(1)}, u32[]{:S(2)}, u32[]{:S(2)}) collective-permute-start(f32[504,128]{1,0:T(8,128)S(1)} %get-tuple-element.37), channel_id=1, source_target_pairs={{0,2},{2,0},{1,3},{3,1},{4,6},{6,4},{5,7},{7,5},{8,10},{10,8},{9,1... | collective-permute-start | bytes 774152 | tf_op jit(solution)/shard_map/ppermute | solution.py:767
  46.0 10.8 %collective-permute-start.7 = (f32[368,128]{1,0:T(8,128)S(1)}, f32[368,128]{1,0:T(8,128)S(1)}, u32[]{:S(2)}, u32[]{:S(2)}) collective-permute-start(f32[368,128]{1,0:T(8,128)S(1)} %get-tuple-element.40), channel_id=1, source_target_pairs={{0,2},{2,0},{1,3},{3,1},{4,6},{6,4},{5,7},{7,5},{8,10},{10,8},{9,1... | collective-permute-start | bytes 565256 | tf_op jit(solution)/shard_map/ppermute | solution.py:768

commit v6 on v5

--- a/solution.py
+++ b/solution.py
@@ -379,10 +379,9 @@
 def place_kernel(part, own, other, *, n, halves):
     groups = own.shape[1] // LANES
     pad = rows_padded(n)
-    inner = n - 2
     shape = (halves, 6, groups, pad, LANES)
 
-    def body(part_ref, own_ref, other_ref, faces, keep, line_rows, up, down):
+    def body(part_ref, own_ref, other_ref, faces, line_rows, up, down):
         comp = lax.axis_index("comp")
         for h in range(halves):
             place = jnp.where(comp == h, own_ref[...], other_ref[...])
@@ -401,17 +400,10 @@
                     faces[h, s, k] = y[:, k * LANES : (k + 1) * LANES]
         for h in range(halves):
             add_direction(faces, h, 0, None, up, down, n, groups, pad)
-        for a in range(inner):
-            for b in range(inner):
-                for k in range(groups):
-                    base = plane_at(a + 1, comp, n) + ((b + 1) * n + 1) * 8 + k * halves
-                    keep[pl.ds(((a * inner + b) * groups + k) * inner, inner), :] = part_ref[
-                        pl.ds(base + comp, inner, stride=8), :
-                    ]
-
-    return pl.pallas_call(
-        body,
-        out_shape=whole(shape, (inner * inner * inner * groups, LANES)),
+
+    return pl.pallas_call(
+        body,
+        out_shape=whole(shape)[0],
         scratch_shapes=[pltpu.VMEM(shape[1:], jnp.float32)] + [pltpu.VMEM((groups, pad, LANES), jnp.float32)] * 2,
         compiler_params=vmem_params(),
         name="place",
@@ -499,8 +491,8 @@
 def pack_layout(n, groups):
     pad = rows_padded(n)
     mid = (0, (n - 2) * n, (n - 2) * (n - 2))
-    tall = (pad // 2 + 7) // 8 * 8
-    x_sizes = [pad * groups, tall]
+    tall = n * n // 2
+    x_sizes = [n * n * groups, tall]
     sizes = [mid[1] * groups, mid[2] * groups, mid[1] // 2, mid[2] // 2]
     starts = [0] + [sum(sizes[:i]) for i in range(4)]
     return pad, mid, tall, starts, (sum(x_sizes), sum(sizes))
@@ -542,12 +534,12 @@
             add_direction(faces, h, 2, remote, up, down, n, groups, pad)
         for dst_x, dst, h in ((keep_x, keep, comp), (send_x, send, 1 - comp)):
             for k in range(groups):
-                dst_x[pl.ds(k * pad, pad), :] = faces[h, 0, k]
+                dst_x[k * n * n : (k + 1) * n * n, :] = faces[h, 0, k, 0 : n * n, :]
                 for s in (1, 2):
                     dst[pl.ds(starts[s] + k * mid[s], mid[s]), :] = middle_rows(faces.at[h, 2 * s, k], s, n)
             x = faces.at[h, 1, groups - 1]
-            dst_x[pl.ds(groups * pad, tall), :] = jnp.where(
-                lane_iota(tall) < STRIDE[0], turn(x[0:tall, :], STRIDE[0]), x[pad - tall : pad, :]
+            dst_x[groups * n * n : groups * n * n + tall, :] = jnp.where(
+                lane_iota(tall) < STRIDE[0], turn(x[0:tall, :], STRIDE[0]), x[tall : n * n, :]
             )
             for s in (1, 2):
                 pieces = []
@@ -570,13 +562,13 @@
     )(faces_in, got)[1:]
 
 
-def unpack(pack, s, n, groups, pad):
+def unpack(pack, s, n, groups):
     _, mid, tall, starts, _ = pack_layout(n, groups)
     if s == 0:
-        first = lane_iota(pad) < STRIDE[0]
-        low = [pack[pl.ds(k * pad, pad), :] for k in range(groups)]
-        edge = pack[pl.ds(groups * pad, tall), :]
-        edge_full = jnp.concatenate([turn(edge, STRIDE[0])[: pad - tall], edge], axis=0)
+        first = lane_iota(n * n) < STRIDE[0]
+        low = [pack[k * n * n : (k + 1) * n * n, :] for k in range(groups)]
+        edge = pack[groups * n * n : groups * n * n + tall, :]
+        edge_full = jnp.concatenate([turn(edge, STRIDE[0]), edge], axis=0)
         high = []
         for k in range(groups):
             after = turn(low[k + 1], STRIDE[0]) if k + 1 < groups else edge_full
@@ -593,9 +585,9 @@
     return low, high
 
 
-def to_elements(pack, matrix, s, n, groups, pad, store):
+def to_elements(pack, matrix, s, n, groups, store, after=None):
     inner = n - 2
-    for side, x in enumerate(unpack(pack, s, n, groups, pad)):
+    for side, x in enumerate(unpack(pack, s, n, groups)):
         y = split_dot(jnp.concatenate(x, axis=1), matrix, ((1,), (0,)))
         at = side * (n - 1)
         for k in range(groups):
@@ -612,15 +604,17 @@
                     store(flat(base + at * n, n), z[a * n : a * n + n])
                 if s == 2:
                     store(flat(base + n + at, inner, n), z[a * inner : (a + 1) * inner])
-
-
-def early_kernel(own_x, own_face, own_in, got_in, place, *, n):
+        if after is not None:
+            after(side)
+
+
+def early_kernel(own_x, own_face, part, got_in, place, *, n, halves):
     size = place.shape[1]
     groups = size // LANES
-    pad = rows_padded(n)
     inner = n - 2
 
-    def body(ox, of, oi, gi, place_ref, out_s, matrix_ref):
+    def body(ox, of, part_ref, gi, place_ref, out_s, matrix_ref):
+        comp = lax.axis_index("comp")
         matrix = one_hot(place_ref[...])
         matrix = jnp.concatenate([matrix, matrix], axis=0)
         matrix_ref[...] = matrix
@@ -629,13 +623,15 @@
             out_s[rows, :] = value
 
         for s in range(3):
-            to_elements(of if s else ox, matrix, s, n, groups, pad, store)
+            to_elements(of if s else ox, matrix, s, n, groups, store)
         for a in range(inner):
+            start = plane_at(a + 1, comp, n) + comp
             for b in range(inner):
                 for k in range(groups):
                     src = pl.ds(((a * inner + b) * groups + k) * inner, inner)
                     base = (a + 1) * n * n + (b + 1) * n + 1
-                    out_s[pl.ds(base * groups + k, inner, stride=groups), :] = oi[src, :] + gi[src, :]
+                    own = part_ref[pl.ds(start + (((b + 1) * n + 1) * 8 + k * halves), inner, stride=8), :]
+                    out_s[pl.ds(base * groups + k, inner, stride=groups), :] = own + gi[src, :]
 
     return pl.pallas_call(
         body,
@@ -645,7 +641,7 @@
         ],
         compiler_params=vmem_params(),
         name="early",
-    )(own_x, own_face, own_in, got_in, place)
+    )(own_x, own_face, part, got_in, place)
 
 
 def outer_rows(n, groups):
@@ -655,7 +651,6 @@
 def middle_kernel(early, matrix, got_face, *, n):
     total = early.shape[0]
     groups = total // (n * n * n)
-    pad = rows_padded(n)
     edge = outer_rows(n, groups)
 
     def body(early_ref, matrix_ref, gf, out_s, out, sem):
@@ -664,7 +659,7 @@
 
         matrix = matrix_ref[...]
         for s in (1, 2):
-            to_elements(gf, matrix, s, n, groups, pad, store)
+            to_elements(gf, matrix, s, n, groups, store)
         rows = pl.ds(edge, total - 2 * edge)
         done = pltpu.make_async_copy(out_s.at[rows, :], out.at[rows, :], sem)
         done.start()
@@ -684,7 +679,6 @@
 def final_kernel(early, result, matrix, got_x, *, n):
     total = early.shape[0]
     groups = total // (n * n * n)
-    pad = rows_padded(n)
     edge = outer_rows(n, groups)
 
     def body(early_ref, result_ref, matrix_ref, gx, out, ends, sem):
@@ -697,13 +691,11 @@
             here = pl.ds(start, rows.size, stride=rows.stride)
             ends[here, :] = ends[here, :] + value
 
-        to_elements(gx, matrix_ref[...], 0, n, groups, pad, store)
         done = [
             pltpu.make_async_copy(ends.at[pl.ds(i * edge, edge), :], out.at[pl.ds(i * far, edge), :], sem.at[i])
             for i in range(2)
         ]
-        for c in done:
-            c.start()
+        to_elements(gx, matrix_ref[...], 0, n, groups, store, lambda side: done[side].start())
         for c in done:
             c.wait()
 
@@ -757,7 +749,7 @@
     even, odd = edge_kernel(part, element_place, other_place, n=n, halves=halves)
     even = exchange(even, True, False)
     odd = exchange(odd, True, True)
-    faces, own_in = place_kernel(part, element_place, other_place, n=n, halves=halves)
+    faces = place_kernel(part, element_place, other_place, n=n, halves=halves)
     faces, even, odd = x_kernel(faces, even, odd, n=n)
     odd = exchange(odd, False, True)
     even = exchange(even, False, False)
@@ -766,7 +758,7 @@
     own_x, own_face, send_x, send_face = z_kernel(faces, got, n=n)
     got_face = lax.ppermute(send_face, "comp", swap)
     got_x = lax.ppermute(send_x, "comp", swap)
-    early, matrix = early_kernel(own_x, own_face, own_in, got_in, element_place, n=n)
+    early, matrix = early_kernel(own_x, own_face, part, got_in, element_place, n=n, halves=halves)
     early, result = middle_kernel(early, matrix, got_face, n=n)
     result = final_kernel(early, result, matrix, got_x, n=n)
     return result.reshape(n, n, n, 1, element_place.shape[1])

time: 58 us -> 57.8 us (level)
  no operation moved by 1% of the time
where the time goes in v6:
time: 57.8 us; the launch traced here: 57.6 us
  waiting for transfers between devices  30 us (52%)
  Pallas kernels  16.2 us (28%)
  starting transfers between devices  11.4 us (20%)
    ppermute x1, waiting for transfers between devices, body(): other_place = lax.ppermute(element_place, 'comp', swap)  17.5 us
    pallas_call x1, Pallas kernels, flux_kernel(): pl.pallas_call(body, in_specs=[pl.BlockSpec(memory_space=pltpu.HBM), pl.B...  7.67 us
    ppermute x1, waiting for transfers between devices, body(): got_face = lax.ppermute(send_face, 'comp', swap)  6.23 us
    ppermute x3, starting transfers between devices, exchange(): lax.ppermute(value, 'elem', pairs)  6.09 us
    ppermute x3, waiting for transfers between devices, exchange(): lax.ppermute(value, 'elem', pairs)  3.52 us
    ppermute x1, starting transfers between devices, body(): got_in = lax.ppermute(send_in, 'comp', swap)  3.04 us
    pallas_call x1, Pallas kernels, place_kernel(): pl.pallas_call(body, out_shape=whole(shape)[0], scratch_shapes=[pltpu.VME...  2.27 us
    pallas_call x1, Pallas kernels, middle_kernel(): pl.pallas_call(body, out_shape=whole(early.shape, early.shape), out_specs...  1.56 us
  transfers between devices with their start and end apart: 8, of which 6 were waited for; matrix products, arithmetic and copies ran while one was open for 0% of the time, Pallas kernels for 13%

profile of v6, /device:TPU:0, one launch (start us, length us, event | category | flops | bytes accessed | tf_op | source)
XLA Modules:
  0.0 57.6 jit_solution(17088512180216342513)
XLA Ops:
  0.0 7.7 %flux.1 = (f32[1536,128]{1,0:T(8,128)S(1)}, f32[8000,128]{1,0:T(8,128)S(1)}) custom-call(f32[3,5,10,10,2,384]{5,4,3,2,1,0:T(2,128)} %v_hbm.1, f32[3,3,5,10,10,2,384]{6,5,4,3,2,1,0:T(2,128)} %g_hbm.1), custom_call_target="tpu_custom_call" | custom-call | tf_op jit(solution)/shard_map/flux/pallas_call | solution.py:176
  7.7 3.0 %collective-permute-start.5 = (f32[1536,128]{1,0:T(8,128)S(1)}, f32[1536,128]{1,0:T(8,128)S(1)}, u32[]{:S(2)}, u32[]{:S(2)}) collective-permute-start(f32[1536,128]{1,0:T(8,128)S(1)} %get-tuple-element.30), channel_id=1, source_target_pairs={{0,2},{2,0},{1,3},{3,1},{4,6},{6,4},{5,7},{7,5},{8,10},{10,8},{9,1... | collective-permute-start | bytes 2359304 | tf_op jit(solution)/shard_map/ppermute | solution.py:747
  10.7 0.1 collective-permute-start
  10.8 17.5 %collective-permute-done.other_ref = s32[1,384]{1,0:T(1,128)S(1)} collective-permute-done((s32[1,384]{1,0:T(1,128)S(1)}, s32[1,384]{1,0:T(1,128)S(1)}, u32[]{:S(2)}, u32[]{:S(2)}) %collective-permute-start) | collective-permute-done | bytes 1568 | tf_op jit(solution)/shard_map/ppermute | solution.py:743
  28.3 1.0 %edge.1 = (f32[104,128]{1,0:T(8,128)S(1)}, f32[104,128]{1,0:T(8,128)}) custom-call(f32[8000,128]{1,0:T(8,128)S(1)} %get-tuple-element.21.part_ref, s32[1,384]{1,0:T(1,128)S(1)} %copy-done, s32[1,384]{1,0:T(1,128)S(1)} %collective-permute-done.other_ref), custom_call_target="tpu_custom_call" | custom-call | tf_op jit(solution)/shard_map/edge/pallas_call | solution.py:370
  29.4 2.8 %collective-permute-start.1 = (f32[104,128]{1,0:T(8,128)S(1)}, f32[104,128]{1,0:T(8,128)S(1)}, u32[]{:S(2)}, u32[]{:S(2)}) collective-permute-start(f32[104,128]{1,0:T(8,128)S(1)} %get-tuple-element.22), channel_id=1, source_target_pairs={{0,16},{4,20},{8,24},{12,28},{16,0},{20,4},{24,8},{28,12},{1,17},{... | collective-permute-start | bytes 159752 | tf_op jit(solution)/shard_map/ppermute | solution.py:737
  32.2 2.3 %place.1.faces_ref = f32[2,6,3,104,128]{4,3,2,1,0:T(8,128)S(1)} custom-call(f32[8000,128]{1,0:T(8,128)S(1)} %get-tuple-element.21.part_ref, s32[1,384]{1,0:T(1,128)S(1)} %copy-done, s32[1,384]{1,0:T(1,128)S(1)} %collective-permute-done.other_ref), custom_call_target="tpu_custom_call" | custom-call | tf_op jit(solution)/shard_map/place/pallas_call | solution.py:404
  34.5 0.3 add_x.1
  34.8 1.7 %collective-permute-start.2 = (f32[104,128]{1,0:T(8,128)S(1)}, f32[104,128]{1,0:T(8,128)S(1)}, u32[]{:S(2)}, u32[]{:S(2)}) collective-permute-start(f32[104,128]{1,0:T(8,128)S(1)} %get-tuple-element.24), channel_id=1, source_target_pairs={{0,4},{4,0},{8,12},{12,8},{16,20},{20,16},{24,28},{28,24},{1,5},{5... | collective-permute-start | bytes 159752 | tf_op jit(solution)/shard_map/ppermute | solution.py:737
  36.5 1.5 %collective-permute-start.3 = (f32[104,128]{1,0:T(8,128)S(1)}, f32[104,128]{1,0:T(8,128)S(1)}, u32[]{:S(2)}, u32[]{:S(2)}) collective-permute-start(f32[104,128]{1,0:T(8,128)S(1)} %get-tuple-element.25), channel_id=1, source_target_pairs={{0,12},{4,8},{8,4},{12,0},{16,28},{20,24},{24,20},{28,16},{1,13},{... | collective-permute-start | bytes 159752 | tf_op jit(solution)/shard_map/ppermute | solution.py:737
  38.0 1.4 %collective-permute-done.2.even_ref = f32[104,128]{1,0:T(8,128)S(1)} collective-permute-done((f32[104,128]{1,0:T(8,128)S(1)}, f32[104,128]{1,0:T(8,128)S(1)}, u32[]{:S(2)}, u32[]{:S(2)}) %collective-permute-start.2) | collective-permute-done | bytes 53280 | tf_op jit(solution)/shard_map/ppermute | solution.py:737
  39.4 2.2 %collective-permute-done.3.odd_ref = f32[104,128]{1,0:T(8,128)S(1)} collective-permute-done((f32[104,128]{1,0:T(8,128)S(1)}, f32[104,128]{1,0:T(8,128)S(1)}, u32[]{:S(2)}, u32[]{:S(2)}) %collective-permute-start.3) | collective-permute-done | bytes 53280 | tf_op jit(solution)/shard_map/ppermute | solution.py:737
  41.6 0.7 %add_y.1 = (f32[2,6,3,104,128]{4,3,2,1,0:T(8,128)S(1)}, f32[2,104,128]{2,1,0:T(8,128)S(1)}) custom-call(f32[2,6,3,104,128]{4,3,2,1,0:T(8,128)S(1)} %get-tuple-element.23.faces_ref, f32[104,128]{1,0:T(8,128)S(1)} %collective-permute-done.2.even_ref, f32[104,128]{1,0:T(8,128)S(1)} %collective-permute-done.3.odd_ref), custom_call_target="tpu_custom_call", output_to_operand_aliasing={{0}: (0, {})} | custom-call | tf_op jit(solution)/shard_map/add_y/pallas_call | solution.py:481
  42.2 0.1 collective-permute-start.4
  42.3 1.3 %collective-permute-done.4.got_ref = f32[2,104,128]{2,1,0:T(8,128)S(1)} collective-permute-done((f32[2,104,128]{2,1,0:T(8,128)S(1)}, f32[2,104,128]{2,1,0:T(8,128)S(1)}, u32[]{:S(2)}, u32[]{:S(2)}) %collective-permute-start.4) | collective-permute-done | bytes 106528 | tf_op jit(solution)/shard_map/ppermute | solution.py:757
  43.6 0.8 %add_z.1 = (f32[2,6,3,104,128]{4,3,2,1,0:T(8,128)S(1)}, f32[350,128]{1,0:T(8,128)S(1)}, f32[504,128]{1,0:T(8,128)S(1)}, f32[350,128]{1,0:T(8,128)S(1)}, f32[504,128]{1,0:T(8,128)S(1)}) custom-call(f32[2,6,3,104,128]{4,3,2,1,0:T(8,128)S(1)} %get-tuple-element.26.faces_ref, ...), custom_call_target="tpu_custom_call", output_to_operand_aliasing={{0}: (0, {})} | custom-call | tf_op jit(solution)/shard_map/add_z/pallas_call | solution.py:555
  44.4 1.6 %collective-permute-start.6 = (f32[504,128]{1,0:T(8,128)S(1)}, f32[504,128]{1,0:T(8,128)S(1)}, u32[]{:S(2)}, u32[]{:S(2)}) collective-permute-start(f32[504,128]{1,0:T(8,128)S(1)} %get-tuple-element.33), channel_id=1, source_target_pairs={{0,2},{2,0},{1,3},{3,1},{4,6},{6,4},{5,7},{7,5},{8,10},{10,8},{9,1... | collective-permute-start | bytes 774152 | tf_op jit(solution)/shard_map/ppermute | solution.py:759
  46.0 0.5 collective-permute-start.7
  46.5 0.0 collective-permute-done.5.gi
  46.5 0.8 %early.1 = (f32[3000,128]{1,0:T(8,128)S(1)}, bf16[768,384]{1,0:T(8,128)(2,1)S(1)}) custom-call(f32[350,128]{1,0:T(8,128)S(1)} %get-tuple-element.28.ox, f32[504,128]{1,0:T(8,128)S(1)} %get-tuple-element.29.of, f32[8000,128]{1,0:T(8,128)S(1)} %get-tuple-element.21.part_ref, f32[1536,128]{1,0:T(8,128)S(1)} %collective-permute-done.5.gi, s32[1,384]{1,0:T(1,128)S(1)} %copy-done), custom_call_target="tpu_custom_call" | custom-call | tf_op jit(solution)/shard_map/early/pallas_call | solution.py:636
  47.3 6.2 %collective-permute-done.6.gf = f32[504,128]{1,0:T(8,128)S(1)} collective-permute-done((f32[504,128]{1,0:T(8,128)S(1)}, f32[504,128]{1,0:T(8,128)S(1)}, u32[]{:S(2)}, u32[]{:S(2)}) %collective-permute-start.6) | collective-permute-done | bytes 258080 | tf_op jit(solution)/shard_map/ppermute | solution.py:759
  53.6 1.6 %middle.1 = (f32[3000,128]{1,0:T(8,128)S(1)}, f32[3000,128]{1,0:T(8,128)}) custom-call(f32[3000,128]{1,0:T(8,128)S(1)} %get-tuple-element.31.early_ref, bf16[768,384]{1,0:T(8,128)(2,1)S(1)} %get-tuple-element.32.matrix_ref, f32[504,128]{1,0:T(8,128)S(1)} %collective-permute-done.6.gf), custom_call_target="tpu_custom_call", output_to_operand_aliasing={{0}: (0, {})} | custom-call | tf_op jit(solution)/shard_map/middle/pallas_call | solution.py:668
  55.1 1.5 %collective-permute-done.7.gx = f32[350,128]{1,0:T(8,128)S(1)} collective-permute-done((f32[350,128]{1,0:T(8,128)S(1)}, f32[350,128]{1,0:T(8,128)S(1)}, u32[]{:S(2)}, u32[]{:S(2)}) %collective-permute-start.7) | collective-permute-done | bytes 179232 | tf_op jit(solution)/shard_map/ppermute | solution.py:760
  56.6 1.0 %final.1 = f32[3000,128]{1,0:T(8,128)} custom-call(f32[3000,128]{1,0:T(8,128)S(1)} %get-tuple-element.34.early_ref, f32[3000,128]{1,0:T(8,128)} %get-tuple-element.35.result_ref, bf16[768,384]{1,0:T(8,128)(2,1)S(1)} %get-tuple-element.32.matrix_ref, f32[350,128]{1,0:T(8,128)S(1)} %collective-permute-done.7.gx), custom_call_target="tpu_custom_call", output_to_operand_aliasing={{}: (1, {})} | custom-call | tf_op jit(solution)/shard_map/final/pallas_call | solution.py:702
  (4 shorter events, 0.0 us)
Async XLA Ops:
  0.0 10.7 %copy-start = (s32[1,384]{1,0:T(1,128)S(1)}, s32[1,384]{1,0:T(1,128)}, u32[]{:S(2)}) copy-start(s32[1,384]{1,0:T(1,128)} %place_ref.1) | copy-start | bytes 4612
  7.7 38.8 %collective-permute-start.5 = (f32[1536,128]{1,0:T(8,128)S(1)}, f32[1536,128]{1,0:T(8,128)S(1)}, u32[]{:S(2)}, u32[]{:S(2)}) collective-permute-start(f32[1536,128]{1,0:T(8,128)S(1)} %get-tuple-element.30), channel_id=1, source_target_pairs={{0,2},{2,0},{1,3},{3,1},{4,6},{6,4},{5,7},{7,5},{8,10},{10,8},{9,1... | collective-permute-start | bytes 2359304 | tf_op jit(solution)/shard_map/ppermute | solution.py:747
  10.7 17.6 %collective-permute-start = (s32[1,384]{1,0:T(1,128)S(1)}, s32[1,384]{1,0:T(1,128)S(1)}, u32[]{:S(2)}, u32[]{:S(2)}) collective-permute-start(s32[1,384]{1,0:T(1,128)S(1)} %copy-done), channel_id=1, source_target_pairs={{0,2},{2,0},{1,3},{3,1},{4,6},{6,4},{5,7},{7,5},{8,10},{10,8},{9,1... | collective-permute-start | bytes 4616 | tf_op jit(solution)/shard_map/ppermute | solution.py:743
  29.4 5.1 %collective-permute-start.1 = (f32[104,128]{1,0:T(8,128)S(1)}, f32[104,128]{1,0:T(8,128)S(1)}, u32[]{:S(2)}, u32[]{:S(2)}) collective-permute-start(f32[104,128]{1,0:T(8,128)S(1)} %get-tuple-element.22), channel_id=1, source_target_pairs={{0,16},{4,20},{8,24},{12,28},{16,0},{20,4},{24,8},{28,12},{1,17},{... | collective-permute-start | bytes 159752 | tf_op jit(solution)/shard_map/ppermute | solution.py:737
  34.8 4.6 %collective-permute-start.2 = (f32[104,128]{1,0:T(8,128)S(1)}, f32[104,128]{1,0:T(8,128)S(1)}, u32[]{:S(2)}, u32[]{:S(2)}) collective-permute-start(f32[104,128]{1,0:T(8,128)S(1)} %get-tuple-element.24), channel_id=1, source_target_pairs={{0,4},{4,0},{8,12},{12,8},{16,20},{20,16},{24,28},{28,24},{1,5},{5... | collective-permute-start | bytes 159752 | tf_op jit(solution)/shard_map/ppermute | solution.py:737
  36.5 5.0 %collective-permute-start.3 = (f32[104,128]{1,0:T(8,128)S(1)}, f32[104,128]{1,0:T(8,128)S(1)}, u32[]{:S(2)}, u32[]{:S(2)}) collective-permute-start(f32[104,128]{1,0:T(8,128)S(1)} %get-tuple-element.25), channel_id=1, source_target_pairs={{0,12},{4,8},{8,4},{12,0},{16,28},{20,24},{24,20},{28,16},{1,13},{... | collective-permute-start | bytes 159752 | tf_op jit(solution)/shard_map/ppermute | solution.py:737
  42.2 1.4 %collective-permute-start.4 = (f32[2,104,128]{2,1,0:T(8,128)S(1)}, f32[2,104,128]{2,1,0:T(8,128)S(1)}, u32[]{:S(2)}, u32[]{:S(2)}) collective-permute-start(f32[2,104,128]{2,1,0:T(8,128)S(1)} %get-tuple-element.27), channel_id=1, source_target_pairs={{0,1},{1,0},{2,3},{3,2},{4,5},{5,4},{6,7},{7,6},{8,9},{9,8},{10,11... | collective-permute-start | bytes 319496 | tf_op jit(solution)/shard_map/ppermute | solution.py:757
  44.4 9.2 %collective-permute-start.6 = (f32[504,128]{1,0:T(8,128)S(1)}, f32[504,128]{1,0:T(8,128)S(1)}, u32[]{:S(2)}, u32[]{:S(2)}) collective-permute-start(f32[504,128]{1,0:T(8,128)S(1)} %get-tuple-element.33), channel_id=1, source_target_pairs={{0,2},{2,0},{1,3},{3,1},{4,6},{6,4},{5,7},{7,5},{8,10},{10,8},{9,1... | collective-permute-start | bytes 774152 | tf_op jit(solution)/shard_map/ppermute | solution.py:759
  46.0 10.6 %collective-permute-start.7 = (f32[350,128]{1,0:T(8,128)S(1)}, f32[350,128]{1,0:T(8,128)S(1)}, u32[]{:S(2)}, u32[]{:S(2)}) collective-permute-start(f32[350,128]{1,0:T(8,128)S(1)} %get-tuple-element.36), channel_id=1, source_target_pairs={{0,2},{2,0},{1,3},{3,1},{4,6},{6,4},{5,7},{7,5},{8,10},{10,8},{9,1... | collective-permute-start | bytes 537608 | tf_op jit(solution)/shard_map/ppermute | solution.py:760

commit v7 on v6

--- a/solution.py
+++ b/solution.py
@@ -310,13 +310,14 @@
     return pltpu.CompilerParams(vmem_limit_bytes=40 * 2**20)
 
 
-def face_rows(part, s, k, h, n, halves, store):
+def face_rows(part, s, k, h, n, halves, store, direction=None):
     comp = lax.axis_index("comp")
+    direction = s // 2 if direction is None else direction
     at = s % 2 * (n - 1)
     sub = k * halves + h
-    if s // 2 == 0:
+    if direction == 0:
         store(0, n * n, part[pl.ds(plane_at(at, comp, n) + sub, n * n, stride=8), :])
-    elif s // 2 == 2:
+    elif direction == 2:
         count = n * n // 2
         for p in range(2):
             start = plane_at(p * (n // 2), comp, n) + at * 8 + sub
@@ -337,26 +338,31 @@
     pad = rows_padded(n)
     step = STRIDE[0]
 
-    def body(part_ref, own_ref, other_ref, x_even, x_odd, rows):
+    single = lax.axis_size("elem") // GRID_Y <= 2
+
+    def body(part_ref, own_ref, other_ref, x_even, *refs):
+        x_odd, rows = refs[:-1], refs[-1]
         comp = lax.axis_index("comp")
         elem = lax.axis_index("elem")
+        up = elem // GRID_Y % 2 == 0
+        sides = [jnp.where(up, 1, 0)] if single else [0, 1]
         payload = []
-        for side in range(2):
+        for index, side in enumerate(sides):
             pieces = []
             match = []
             for h in range(halves):
                 place = jnp.where(comp == h, own_ref[...], other_ref[...])
                 lane = lax.broadcasted_iota(jnp.int32, (LANES, size), 0)
-                goal = jnp.where(lane // step == h, lane - h * step + (size - step if side else 0), -1)
+                goal = jnp.where(lane // step == h, lane - h * step + side * (size - step), -1)
                 one = jnp.where(goal == place, 1.0, 0.0).astype(jnp.bfloat16)
                 match += [one, one]
                 for k in range(groups):
 
                     def store(at, count, value):
-                        rows[side, h, k, at : at + count, :] = value
-
-                    face_rows(part_ref, side, k, h, n, halves, store)
-                pieces += bf16_pair(jnp.concatenate([rows[side, h, k] for k in range(groups)], axis=1))
+                        rows[index, h, k, at : at + count, :] = value
+
+                    face_rows(part_ref, side, k, h, n, halves, store, 0)
+                pieces += bf16_pair(jnp.concatenate([rows[index, h, k] for k in range(groups)], axis=1))
             payload.append(
                 lax.dot_general(
                     jnp.concatenate(pieces, axis=1),
@@ -365,15 +371,19 @@
                     preferred_element_type=jnp.float32,
                 )
             )
-        x_even[...], x_odd[...] = parity_split(elem // GRID_Y % 2 == 0, payload[1], payload[0])
-
-    return pl.pallas_call(
-        body,
-        out_shape=whole((pad, LANES), (pad, LANES)),
+        if single:
+            x_even[...] = payload[0]
+        else:
+            x_even[...], x_odd[0][...] = parity_split(up, payload[1], payload[0])
+
+    outs = pl.pallas_call(
+        body,
+        out_shape=whole(*[(pad, LANES)] * (1 if single else 2)),
         scratch_shapes=[pltpu.VMEM((2, halves, groups, pad, LANES), jnp.float32)],
         compiler_params=vmem_params(),
         name="edge",
     )(part, own, other)
+    return outs[0], outs[-1]
 
 
 def place_kernel(part, own, other, *, n, halves):
@@ -492,7 +502,7 @@
     pad = rows_padded(n)
     mid = (0, (n - 2) * n, (n - 2) * (n - 2))
     tall = n * n // 2
-    x_sizes = [n * n * groups, tall]
+    x_sizes = [n * (n - 1) * groups, tall, n]
     sizes = [mid[1] * groups, mid[2] * groups, mid[1] // 2, mid[2] // 2]
     starts = [0] + [sum(sizes[:i]) for i in range(4)]
     return pad, mid, tall, starts, (sum(x_sizes), sum(sizes))
@@ -508,6 +518,7 @@
     halves, _, groups, pad, _ = faces_in.shape
     last = BLOCK_Z - 1
     _, mid, tall, starts, totals = pack_layout(n, groups)
+    short = n * (n - 1)
 
     def body(faces_ref, got_ref, faces, keep_x, keep, send_x, send, up, down):
         rep = lax.axis_index("rep")
@@ -534,11 +545,14 @@
             add_direction(faces, h, 2, remote, up, down, n, groups, pad)
         for dst_x, dst, h in ((keep_x, keep, comp), (send_x, send, 1 - comp)):
             for k in range(groups):
-                dst_x[k * n * n : (k + 1) * n * n, :] = faces[h, 0, k, 0 : n * n, :]
+                dst_x[k * short : (k + 1) * short, :] = faces[h, 0, k, 0:short, :]
                 for s in (1, 2):
                     dst[pl.ds(starts[s] + k * mid[s], mid[s]), :] = middle_rows(faces.at[h, 2 * s, k], s, n)
             x = faces.at[h, 1, groups - 1]
-            dst_x[groups * n * n : groups * n * n + tall, :] = jnp.where(
+            dst_x[groups * short + tall : groups * short + tall + n, :] = gather_slots(
+                n, 1, [(k, BLOCK_Y - 1, faces[h, 0, k, short : n * n, :]) for k in range(groups)]
+            )
+            dst_x[groups * short : groups * short + tall, :] = jnp.where(
                 lane_iota(tall) < STRIDE[0], turn(x[0:tall, :], STRIDE[0]), x[tall : n * n, :]
             )
             for s in (1, 2):
@@ -566,8 +580,15 @@
     _, mid, tall, starts, _ = pack_layout(n, groups)
     if s == 0:
         first = lane_iota(n * n) < STRIDE[0]
-        low = [pack[k * n * n : (k + 1) * n * n, :] for k in range(groups)]
-        edge = pack[groups * n * n : groups * n * n + tall, :]
+        short = n * (n - 1)
+        low = []
+        outer = pack[groups * short + tall : groups * short + tall + n, :]
+        for k in range(groups):
+            rows = pack[k * short : (k + 1) * short, :]
+            far = turn(outer, (BLOCK_Y - 1 - k) * STRIDE[1])
+            near = turn(rows[:n], -STRIDE[1])
+            low.append(jnp.concatenate([rows, jnp.where(lane_part(n, 1) == BLOCK_Y - 1, far, near)], axis=0))
+        edge = pack[groups * short : groups * short + tall, :]
         edge_full = jnp.concatenate([turn(edge, STRIDE[0]), edge], axis=0)
         high = []
         for k in range(groups):

time: 57.8 us -> 57.1 us (0.988)
  Pallas kernels: 16.2 us -> 15.6 us
    pallas_call x1, Pallas kernels: 1.04 us -> 0.28 us  [edge_kernel(): pl.pallas_call(body, out_shape=whole(*[(pad, LANES)] * (1 if single else...]
  transfers between devices with their start and end apart: 8 -> 8, of which waited for: 6 -> 6; matrix products, arithmetic and copies ran while one was open for 0% -> 0% of each run, Pallas kernels for 13% -> 12%
where the time goes in v7:
time: 57.1 us; the launch traced here: 56.9 us
  waiting for transfers between devices  29.8 us (52%)
  Pallas kernels  15.6 us (27%)
  starting transfers between devices  11.4 us (20%)
    ppermute x1, waiting for transfers between devices, body(): other_place = lax.ppermute(element_place, 'comp', swap)  17.5 us
    pallas_call x1, Pallas kernels, flux_kernel(): pl.pallas_call(body, in_specs=[pl.BlockSpec(memory_space=pltpu.HBM), pl.B...  7.74 us
    ppermute x1, waiting for transfers between devices, body(): got_face = lax.ppermute(send_face, 'comp', swap)  6.17 us
    ppermute x3, starting transfers between devices, exchange(): lax.ppermute(value, 'elem', pairs)  6.16 us
    ppermute x3, waiting for transfers between devices, exchange(): lax.ppermute(value, 'elem', pairs)  3.52 us
    ppermute x1, starting transfers between devices, body(): got_in = lax.ppermute(send_in, 'comp', swap)  3.04 us
    pallas_call x1, Pallas kernels, place_kernel(): pl.pallas_call(body, out_shape=whole(shape)[0], scratch_shapes=[pltpu.VME...  2.27 us
    pallas_call x1, Pallas kernels, middle_kernel(): pl.pallas_call(body, out_shape=whole(early.shape, early.shape), out_specs...  1.56 us
  transfers between devices with their start and end apart: 8, of which 6 were waited for; matrix products, arithmetic and copies ran while one was open for 0% of the time, Pallas kernels for 12%

profile of v7, /device:TPU:0, one launch (start us, length us, event | category | flops | bytes accessed | tf_op | source)
XLA Modules:
  0.0 56.9 jit_solution(4640638987685862873)
XLA Ops:
  0.0 7.7 %flux.1 = (f32[1536,128]{1,0:T(8,128)S(1)}, f32[8000,128]{1,0:T(8,128)S(1)}) custom-call(f32[3,5,10,10,2,384]{5,4,3,2,1,0:T(2,128)} %v_hbm.1, f32[3,3,5,10,10,2,384]{6,5,4,3,2,1,0:T(2,128)} %g_hbm.1), custom_call_target="tpu_custom_call" | custom-call | tf_op jit(solution)/shard_map/flux/pallas_call | solution.py:176
  7.8 3.0 %collective-permute-start.5 = (f32[1536,128]{1,0:T(8,128)S(1)}, f32[1536,128]{1,0:T(8,128)S(1)}, u32[]{:S(2)}, u32[]{:S(2)}) collective-permute-start(f32[1536,128]{1,0:T(8,128)S(1)} %get-tuple-element.28), channel_id=1, source_target_pairs={{0,2},{2,0},{1,3},{3,1},{4,6},{6,4},{5,7},{7,5},{8,10},{10,8},{9,1... | collective-permute-start | bytes 2359304 | tf_op jit(solution)/shard_map/ppermute | solution.py:768
  10.8 0.1 collective-permute-start
  10.9 17.5 %collective-permute-done.other_ref = s32[1,384]{1,0:T(1,128)S(1)} collective-permute-done((s32[1,384]{1,0:T(1,128)S(1)}, s32[1,384]{1,0:T(1,128)S(1)}, u32[]{:S(2)}, u32[]{:S(2)}) %collective-permute-start) | collective-permute-done | bytes 1568 | tf_op jit(solution)/shard_map/ppermute | solution.py:764
  28.4 0.3 edge.1
  28.7 2.9 %collective-permute-start.1 = (f32[104,128]{1,0:T(8,128)S(1)}, f32[104,128]{1,0:T(8,128)S(1)}, u32[]{:S(2)}, u32[]{:S(2)}) collective-permute-start(f32[104,128]{1,0:T(8,128)S(1)} %edge.1), channel_id=1, source_target_pairs={{0,16},{4,20},{8,24},{12,28},{16,0},{20,4},{24,8},{28,12},{1,17},{... | collective-permute-start | bytes 159752 | tf_op jit(solution)/shard_map/ppermute | solution.py:758
  31.6 2.3 %place.1.faces_ref = f32[2,6,3,104,128]{4,3,2,1,0:T(8,128)S(1)} custom-call(f32[8000,128]{1,0:T(8,128)S(1)} %get-tuple-element.20.part_ref, s32[1,384]{1,0:T(1,128)S(1)} %copy-done, s32[1,384]{1,0:T(1,128)S(1)} %collective-permute-done.other_ref), custom_call_target="tpu_custom_call" | custom-call | tf_op jit(solution)/shard_map/place/pallas_call | solution.py:414
  33.8 0.0 collective-permute-done.1.even_ref
  33.9 0.3 add_x.1
  34.2 1.7 %collective-permute-start.2 = (f32[104,128]{1,0:T(8,128)S(1)}, f32[104,128]{1,0:T(8,128)S(1)}, u32[]{:S(2)}, u32[]{:S(2)}) collective-permute-start(f32[104,128]{1,0:T(8,128)S(1)} %get-tuple-element.22), channel_id=1, source_target_pairs={{0,4},{4,0},{8,12},{12,8},{16,20},{20,16},{24,28},{28,24},{1,5},{5... | collective-permute-start | bytes 159752 | tf_op jit(solution)/shard_map/ppermute | solution.py:758
  35.9 1.5 %collective-permute-start.3 = (f32[104,128]{1,0:T(8,128)S(1)}, f32[104,128]{1,0:T(8,128)S(1)}, u32[]{:S(2)}, u32[]{:S(2)}) collective-permute-start(f32[104,128]{1,0:T(8,128)S(1)} %get-tuple-element.23), channel_id=1, source_target_pairs={{0,12},{4,8},{8,4},{12,0},{16,28},{20,24},{24,20},{28,16},{1,13},{... | collective-permute-start | bytes 159752 | tf_op jit(solution)/shard_map/ppermute | solution.py:758
  37.4 1.4 %collective-permute-done.2.even_ref = f32[104,128]{1,0:T(8,128)S(1)} collective-permute-done((f32[104,128]{1,0:T(8,128)S(1)}, f32[104,128]{1,0:T(8,128)S(1)}, u32[]{:S(2)}, u32[]{:S(2)}) %collective-permute-start.2) | collective-permute-done | bytes 53280 | tf_op jit(solution)/shard_map/ppermute | solution.py:758
  38.8 2.2 %collective-permute-done.3.odd_ref = f32[104,128]{1,0:T(8,128)S(1)} collective-permute-done((f32[104,128]{1,0:T(8,128)S(1)}, f32[104,128]{1,0:T(8,128)S(1)}, u32[]{:S(2)}, u32[]{:S(2)}) %collective-permute-start.3) | collective-permute-done | bytes 53280 | tf_op jit(solution)/shard_map/ppermute | solution.py:758
  40.9 0.7 %add_y.1 = (f32[2,6,3,104,128]{4,3,2,1,0:T(8,128)S(1)}, f32[2,104,128]{2,1,0:T(8,128)S(1)}) custom-call(f32[2,6,3,104,128]{4,3,2,1,0:T(8,128)S(1)} %get-tuple-element.21.faces_ref, f32[104,128]{1,0:T(8,128)S(1)} %collective-permute-done.2.even_ref, f32[104,128]{1,0:T(8,128)S(1)} %collective-permute-done.3.odd_ref), custom_call_target="tpu_custom_call", output_to_operand_aliasing={{0}: (0, {})} | custom-call | tf_op jit(solution)/shard_map/add_y/pallas_call | solution.py:491
  41.6 0.1 collective-permute-start.4
  41.7 1.3 %collective-permute-done.4.got_ref = f32[2,104,128]{2,1,0:T(8,128)S(1)} collective-permute-done((f32[2,104,128]{2,1,0:T(8,128)S(1)}, f32[2,104,128]{2,1,0:T(8,128)S(1)}, u32[]{:S(2)}, u32[]{:S(2)}) %collective-permute-start.4) | collective-permute-done | bytes 106528 | tf_op jit(solution)/shard_map/ppermute | solution.py:778
  43.0 0.8 %add_z.1 = (f32[2,6,3,104,128]{4,3,2,1,0:T(8,128)S(1)}, f32[330,128]{1,0:T(8,128)S(1)}, f32[504,128]{1,0:T(8,128)S(1)}, f32[330,128]{1,0:T(8,128)S(1)}, f32[504,128]{1,0:T(8,128)S(1)}) custom-call(f32[2,6,3,104,128]{4,3,2,1,0:T(8,128)S(1)} %get-tuple-element.24.faces_ref, ...), custom_call_target="tpu_custom_call", output_to_operand_aliasing={{0}: (0, {})} | custom-call | tf_op jit(solution)/shard_map/add_z/pallas_call | solution.py:569
  43.8 1.6 %collective-permute-start.6 = (f32[504,128]{1,0:T(8,128)S(1)}, f32[504,128]{1,0:T(8,128)S(1)}, u32[]{:S(2)}, u32[]{:S(2)}) collective-permute-start(f32[504,128]{1,0:T(8,128)S(1)} %get-tuple-element.31), channel_id=1, source_target_pairs={{0,2},{2,0},{1,3},{3,1},{4,6},{6,4},{5,7},{7,5},{8,10},{10,8},{9,1... | collective-permute-start | bytes 774152 | tf_op jit(solution)/shard_map/ppermute | solution.py:780
  45.4 0.5 collective-permute-start.7
  45.9 0.9 %early.1 = (f32[3000,128]{1,0:T(8,128)S(1)}, bf16[768,384]{1,0:T(8,128)(2,1)S(1)}) custom-call(f32[330,128]{1,0:T(8,128)S(1)} %get-tuple-element.26.ox, f32[504,128]{1,0:T(8,128)S(1)} %get-tuple-element.27.of, f32[8000,128]{1,0:T(8,128)S(1)} %get-tuple-element.20.part_ref, f32[1536,128]{1,0:T(8,128)S(1)} %collective-permute-done.5.gi, s32[1,384]{1,0:T(1,128)S(1)} %copy-done), custom_call_target="tpu_custom_call" | custom-call | tf_op jit(solution)/shard_map/early/pallas_call | solution.py:657
  46.8 6.2 %collective-permute-done.6.gf = f32[504,128]{1,0:T(8,128)S(1)} collective-permute-done((f32[504,128]{1,0:T(8,128)S(1)}, f32[504,128]{1,0:T(8,128)S(1)}, u32[]{:S(2)}, u32[]{:S(2)}) %collective-permute-start.6) | collective-permute-done | bytes 258080 | tf_op jit(solution)/shard_map/ppermute | solution.py:780
  53.0 1.6 %middle.1 = (f32[3000,128]{1,0:T(8,128)S(1)}, f32[3000,128]{1,0:T(8,128)}) custom-call(f32[3000,128]{1,0:T(8,128)S(1)} %get-tuple-element.29.early_ref, bf16[768,384]{1,0:T(8,128)(2,1)S(1)} %get-tuple-element.30.matrix_ref, f32[504,128]{1,0:T(8,128)S(1)} %collective-permute-done.6.gf), custom_call_target="tpu_custom_call", output_to_operand_aliasing={{0}: (0, {})} | custom-call | tf_op jit(solution)/shard_map/middle/pallas_call | solution.py:689
  54.5 1.3 %collective-permute-done.7.gx = f32[330,128]{1,0:T(8,128)S(1)} collective-permute-done((f32[330,128]{1,0:T(8,128)S(1)}, f32[330,128]{1,0:T(8,128)S(1)}, u32[]{:S(2)}, u32[]{:S(2)}) %collective-permute-start.7) | collective-permute-done | bytes 168992 | tf_op jit(solution)/shard_map/ppermute | solution.py:781
  55.8 1.1 %final.1 = f32[3000,128]{1,0:T(8,128)} custom-call(f32[3000,128]{1,0:T(8,128)S(1)} %get-tuple-element.32.early_ref, f32[3000,128]{1,0:T(8,128)} %get-tuple-element.33.result_ref, bf16[768,384]{1,0:T(8,128)(2,1)S(1)} %get-tuple-element.30.matrix_ref, f32[330,128]{1,0:T(8,128)S(1)} %collective-permute-done.7.gx), custom_call_target="tpu_custom_call", output_to_operand_aliasing={{}: (1, {})} | custom-call | tf_op jit(solution)/shard_map/final/pallas_call | solution.py:723
  (4 shorter events, 0.0 us)
Async XLA Ops:
  0.0 10.8 %copy-start = (s32[1,384]{1,0:T(1,128)S(1)}, s32[1,384]{1,0:T(1,128)}, u32[]{:S(2)}) copy-start(s32[1,384]{1,0:T(1,128)} %place_ref.1) | copy-start | bytes 4612
  7.8 38.1 %collective-permute-start.5 = (f32[1536,128]{1,0:T(8,128)S(1)}, f32[1536,128]{1,0:T(8,128)S(1)}, u32[]{:S(2)}, u32[]{:S(2)}) collective-permute-start(f32[1536,128]{1,0:T(8,128)S(1)} %get-tuple-element.28), channel_id=1, source_target_pairs={{0,2},{2,0},{1,3},{3,1},{4,6},{6,4},{5,7},{7,5},{8,10},{10,8},{9,1... | collective-permute-start | bytes 2359304 | tf_op jit(solution)/shard_map/ppermute | solution.py:768
  10.8 17.6 %collective-permute-start = (s32[1,384]{1,0:T(1,128)S(1)}, s32[1,384]{1,0:T(1,128)S(1)}, u32[]{:S(2)}, u32[]{:S(2)}) collective-permute-start(s32[1,384]{1,0:T(1,128)S(1)} %copy-done), channel_id=1, source_target_pairs={{0,2},{2,0},{1,3},{3,1},{4,6},{6,4},{5,7},{7,5},{8,10},{10,8},{9,1... | collective-permute-start | bytes 4616 | tf_op jit(solution)/shard_map/ppermute | solution.py:764
  28.7 5.2 %collective-permute-start.1 = (f32[104,128]{1,0:T(8,128)S(1)}, f32[104,128]{1,0:T(8,128)S(1)}, u32[]{:S(2)}, u32[]{:S(2)}) collective-permute-start(f32[104,128]{1,0:T(8,128)S(1)} %edge.1), channel_id=1, source_target_pairs={{0,16},{4,20},{8,24},{12,28},{16,0},{20,4},{24,8},{28,12},{1,17},{... | collective-permute-start | bytes 159752 | tf_op jit(solution)/shard_map/ppermute | solution.py:758
  34.2 4.6 %collective-permute-start.2 = (f32[104,128]{1,0:T(8,128)S(1)}, f32[104,128]{1,0:T(8,128)S(1)}, u32[]{:S(2)}, u32[]{:S(2)}) collective-permute-start(f32[104,128]{1,0:T(8,128)S(1)} %get-tuple-element.22), channel_id=1, source_target_pairs={{0,4},{4,0},{8,12},{12,8},{16,20},{20,16},{24,28},{28,24},{1,5},{5... | collective-permute-start | bytes 159752 | tf_op jit(solution)/shard_map/ppermute | solution.py:758
  35.9 5.0 %collective-permute-start.3 = (f32[104,128]{1,0:T(8,128)S(1)}, f32[104,128]{1,0:T(8,128)S(1)}, u32[]{:S(2)}, u32[]{:S(2)}) collective-permute-start(f32[104,128]{1,0:T(8,128)S(1)} %get-tuple-element.23), channel_id=1, source_target_pairs={{0,12},{4,8},{8,4},{12,0},{16,28},{20,24},{24,20},{28,16},{1,13},{... | collective-permute-start | bytes 159752 | tf_op jit(solution)/shard_map/ppermute | solution.py:758
  41.6 1.4 %collective-permute-start.4 = (f32[2,104,128]{2,1,0:T(8,128)S(1)}, f32[2,104,128]{2,1,0:T(8,128)S(1)}, u32[]{:S(2)}, u32[]{:S(2)}) collective-permute-start(f32[2,104,128]{2,1,0:T(8,128)S(1)} %get-tuple-element.25), channel_id=1, source_target_pairs={{0,1},{1,0},{2,3},{3,2},{4,5},{5,4},{6,7},{7,6},{8,9},{9,8},{10,11... | collective-permute-start | bytes 319496 | tf_op jit(solution)/shard_map/ppermute | solution.py:778
  43.8 9.2 %collective-permute-start.6 = (f32[504,128]{1,0:T(8,128)S(1)}, f32[504,128]{1,0:T(8,128)S(1)}, u32[]{:S(2)}, u32[]{:S(2)}) collective-permute-start(f32[504,128]{1,0:T(8,128)S(1)} %get-tuple-element.31), channel_id=1, source_target_pairs={{0,2},{2,0},{1,3},{3,1},{4,6},{6,4},{5,7},{7,5},{8,10},{10,8},{9,1... | collective-permute-start | bytes 774152 | tf_op jit(solution)/shard_map/ppermute | solution.py:780
  45.4 10.5 %collective-permute-start.7 = (f32[330,128]{1,0:T(8,128)S(1)}, f32[330,128]{1,0:T(8,128)S(1)}, u32[]{:S(2)}, u32[]{:S(2)}) collective-permute-start(f32[330,128]{1,0:T(8,128)S(1)} %get-tuple-element.34), channel_id=1, source_target_pairs={{0,2},{2,0},{1,3},{3,1},{4,6},{6,4},{5,7},{7,5},{8,10},{10,8},{9,1... | collective-permute-start | bytes 506888 | tf_op jit(solution)/shard_map/ppermute | solution.py:781
